TPU v7x, 128 devices: a whole 4x4x4 slice. The times are simulated.
128 devices in a mesh: samp: 2 (over core), grid: 64 (over z, y, x).
Axes of the slice: x: 4, y: 4, z: 4, core: 2. Of those that a mesh axis runs over, the one named last changes fastest.
Arguments:
- log_coef: float32 [2, 4096, 2048], P('samp', 'grid'), may hold values from -4 to 4
- source: float32 [2, 4096, 2048], P('samp', 'grid'), may hold values from -0.6 to 0.6
Outputs:
- correction: float32 [2, 4096, 2048], P('samp', 'grid')
- level_mean: float32 [4096, 2048], P('grid', 'samp')
- level_var: float32 [4096, 2048], P('grid', 'samp')
All inputs are finite; a program needn't handle non-finite values.
Results may differ from a plain program's by a relative error of at most 0.0003.
Values sent between devices are 32-bit elements; how exact they have to be, the bound alone decides.
No kernel may reach another device: no remote copies, remote signals or barrier semaphores. Data moves between devices by JAX's collectives and lax.ppermute only.
A program may use at most 192 MiB of HBM per device.

v0:
```python
import jax
import jax.numpy as jnp
from jax import lax
from jax.sharding import PartitionSpec as P

LEVELS = 5
VCYCLES = 2
COARSE_SWEEPS = 4


damping = 0.8


def extended_2(value, sides, width):
    for axis, dim in sides:
        peers, length = (lax.axis_size(axis), value.shape[dim])
        up = [(i, (i + 1) % peers) for i in range(peers - 1)]
        down = [(j, i) for i, j in up]
        last = lax.slice_in_dim(value, length - width, length, axis=dim)
        initial = lax.slice_in_dim(value, 0, width, axis=dim)
        before = lax.ppermute(last, axis, up)
        after = lax.ppermute(initial, axis, down)
        value = jnp.concatenate([before, value, after], axis=dim)
    return value


def cut_along(value, dim, peers):
    lengths = value.shape
    blocks = value.reshape(*lengths[:dim], peers, lengths[dim] // peers, *lengths[dim + 1 :])
    return jnp.moveaxis(blocks, dim, 0)


def sum_at_owner(value, axis, dim):
    blocks = cut_along(value, dim, lax.axis_size(axis))
    arrived = lax.all_to_all(blocks, axis, split_axis=0, concat_axis=0, tiled=True)
    return arrived.sum(axis=0)


def in_one_piece(arrays, axis, dim, along):
    ends, at = ([], 0)
    for a in arrays[:-1]:
        at += a.shape[along]
        ends.append(at)
    both = jnp.concatenate(arrays, axis=along)
    return tuple(jnp.split(sum_at_owner(both, axis, dim), ends, axis=along))


def harmonic(former, latter):
    return 2.0 * former * latter / (former + latter)


def halve(coeffs):
    row_count, col_count = coeffs.shape
    return jnp.mean(coeffs.reshape(row_count // 2, 2, col_count // 2, 2), axis=(1, 3))


def quad_sum(values):
    row_count, col_count = values.shape
    return jnp.sum(values.reshape(row_count // 2, 2, col_count // 2, 2), axis=(1, 3))


def expand(values):
    return jnp.repeat(jnp.repeat(values, 2, axis=0), 2, axis=1)


def side_weights(coeffs):
    shifted = jnp.concatenate([coeffs[:, 1:], coeffs[:, -1:]], axis=1)
    east_face = harmonic(coeffs, shifted)
    west_face = jnp.concatenate([harmonic(coeffs[:, :1], coeffs[:, :1]), east_face[:, :-1]], axis=1)
    return (west_face, east_face)


def slab_weights(padded, coeffs, margin, is_top, is_bottom):
    col_count = coeffs.shape[1]
    upper = jnp.where(is_top, jnp.broadcast_to(coeffs[:1], (margin, col_count)), padded[:margin])
    lower = jnp.where(
        is_bottom, jnp.broadcast_to(coeffs[-1:], (margin, col_count)), padded[-margin:]
    )
    extended = jnp.concatenate([upper, coeffs, lower], axis=0)
    west_face, east_face = side_weights(extended)
    return (west_face, east_face, harmonic(extended[:-1], extended[1:]))


def band(weights, start, count):
    west_face, east_face, vertical = weights
    return (
        west_face[start : start + count],
        east_face[start : start + count],
        vertical[start - 1 : start + count],
    )


def pad_rows(values):
    return jnp.pad(values, ((1, 1), (0, 0)))


def apply_rows(wide, west_face, east_face, vertical):
    middle = wide[1:-1]
    zero_column = jnp.zeros_like(middle[:, :1])
    west_values = jnp.concatenate([zero_column, middle[:, :-1]], axis=1)
    east_values = jnp.concatenate([middle[:, 1:], zero_column], axis=1)
    north_face = vertical[:-1]
    south_face = vertical[1:]
    diagonal = west_face + east_face + north_face + south_face
    applied = diagonal * middle - (
        west_face * west_values
        + east_face * east_values
        + north_face * wide[:-2]
        + south_face * wide[2:]
    )
    return (middle, applied, diagonal)


def relax_rows(wide, right_side, west_face, east_face, vertical):
    middle, applied, diagonal = apply_rows(wide, west_face, east_face, vertical)
    return middle + damping * (right_side - applied) / diagonal


def pair_sweep(wide, side_wide, weights, row_count, is_top, is_bottom):
    first_pass = relax_rows(wide, side_wide[1:-1], *band(weights, 1, row_count + 2))
    position = lax.broadcasted_iota(jnp.int32, (row_count + 2, 1), 0)
    outside = jnp.logical_or(
        jnp.logical_and(position == 0, is_top),
        jnp.logical_and(position == row_count + 1, is_bottom),
    )
    first_pass = jnp.where(outside, jnp.float32(0.0), first_pass)
    return relax_rows(first_pass, side_wide[2:-2], *band(weights, 2, row_count))


def local(log_coef, source):
    depth = 2
    grid_count = lax.axis_size("grid")
    grid_index = lax.axis_index("grid")
    is_top = grid_index == 0
    is_bottom = grid_index == grid_count - 1
    coeffs = jnp.exp(log_coef[0])
    ladder = []
    margins = []
    for height in range(LEVELS):
        if height:
            coeffs = halve(coeffs)
        if height < LEVELS - 1:
            padded = extended_2(coeffs, (("grid", 0),), depth)
            ladder.append(slab_weights(padded, coeffs, depth, is_top, is_bottom))
            margins.append(depth)
        else:
            padded = extended_2(coeffs, (("grid", 0),), 1)
            ladder.append(slab_weights(padded, coeffs, 1, is_top, is_bottom))
            margins.append(1)

    def residual_of(height, iterate, right_side):
        wide = extended_2(iterate, (("grid", 0),), 1)
        middle, applied, diagonal = apply_rows(
            wide, *band(ladder[height], margins[height], iterate.shape[0])
        )
        return right_side - applied

    def bottom_solve(right_side):
        row_count = right_side.shape[0]
        weights = band(ladder[-1], 1, row_count)
        iterate = relax_rows(pad_rows(jnp.zeros_like(right_side)), right_side, *weights)
        for repeat in range(COARSE_SWEEPS - 1):
            wide = extended_2(iterate, (("grid", 0),), 1)
            iterate = relax_rows(wide, right_side, *weights)
        return iterate

    def vcycle_slab(height, iterate, right_side):
        if height == LEVELS - 1:
            return bottom_solve(right_side)
        row_count = iterate.shape[0]
        stacked = extended_2(jnp.stack((iterate, right_side)), (("grid", 1),), 2)
        side_wide = stacked[1]
        iterate = pair_sweep(stacked[0], side_wide, ladder[height], row_count, is_top, is_bottom)
        residual = residual_of(height, iterate, right_side)
        coarse_side = quad_sum(residual)
        errors = vcycle_slab(height + 1, jnp.zeros_like(coarse_side), coarse_side)
        iterate = iterate + expand(errors)
        wide = extended_2(iterate, (("grid", 0),), 2)
        iterate = pair_sweep(wide, side_wide, ladder[height], row_count, is_top, is_bottom)
        return iterate

    source_field = source[0]
    fine_field = jnp.zeros_like(source_field)
    for repeat in range(VCYCLES):
        fine_field = vcycle_slab(0, fine_field, source_field)
    coarse_side = quad_sum(source_field)
    coarse = jnp.zeros_like(coarse_side)
    for repeat in range(VCYCLES):
        coarse = vcycle_slab(1, coarse, coarse_side)
    correction = fine_field - expand(coarse)
    sample_total = lax.axis_size("samp")
    summed, squares = in_one_piece((correction, correction * correction), "samp", 1, 0)
    level_mean = summed / sample_total
    level_var = (squares - sample_total * level_mean * level_mean) / (sample_total - 1)
    return (correction[None], level_mean, level_var)


def solution(mesh):
    in_specs = (P("samp", "grid", None), P("samp", "grid", None))
    out_specs = (P("samp", "grid", None), P("grid", "samp"), P("grid", "samp"))
    return jax.shard_map(local, mesh=mesh, in_specs=in_specs, out_specs=out_specs, check_vma=False)
```

profile of v0, /device:TPU:97, one launch (start us, length us, event | category | flops | bytes accessed | tf_op | source)
XLA Modules:
  0.0 1362.9 jit_solution(4398269514917495496)
XLA Ops:
  6.6 6.7 collective-permute-start.1
  22.4 7.6 collective-permute-start.3
  31.1 36.9 %exp.16 = f32[32,2,1024,2]{3,2,1,0:T(8,128)} reshape(f32[1,64,2048]{2,1,0:T(8,128)} %copy.381) | data formatting | bytes 1048576 | tf_op jit(solution)/shard_map/exp | solution.py:136
  68.0 13.2 reduce_sum.181
  81.3 9.8 div.308
  113.7 36.9 %reshape_squeeze.3 = f32[32,2,1024,2]{3,2,1,0:T(8,128)} reshape(f32[1,64,2048]{2,1,0:T(8,128)} %param.3) | data formatting | bytes 1048576 | tf_op jit(solution)/shard_map/reshape;squeeze | solution.py:59
  152.1 13.9 %reduce_sum.192 = f32[32,1024]{1,0:T(8,128)} reduce(f32[32,2,1024,2]{3,2,1,0:T(8,128)} %reshape_squeeze.3, f32[]{:T(128)} %constant.16.clone.1), dimensions={1,3}, to_apply=%region_12.13 | reduce | flops 98304 | bytes 655364 | tf_op jit(solution)/shard_map/reduce_sum | solution.py:59
  169.4 7.6 collective-permute-start.21
  180.5 6.6 collective-permute-done.20
  268.8 36.9 %reshape.306 = f32[32,2,1024,2]{3,2,1,0:T(8,128)} reshape(f32[64,2048]{1,0:T(8,128)} %copy.380) | data formatting | bytes 1048576 | tf_op jit(solution)/shard_map/reshape | solution.py:59
  305.8 13.2 reduce_sum.180
  343.3 6.5 collective-permute-done.10
  350.6 10.5 reshape.307
  430.5 7.6 collective-permute-start.27
  441.6 7.8 collective-permute-start.29
  452.9 7.8 collective-permute-start.31
  468.1 7.8 collective-permute-start.33
  479.3 7.6 collective-permute-start.71
  499.8 7.6 collective-permute-start.35
  641.5 36.9 %reshape.318 = f32[32,2,1024,2]{3,2,1,0:T(8,128)} reshape(f32[64,2048]{1,0:T(8,128)} %copy.408) | data formatting | bytes 1048576 | tf_op jit(solution)/shard_map/reshape | solution.py:59
  678.4 13.9 %reduce_sum.188 = f32[32,1024]{1,0:T(8,128)} reduce(f32[32,2,1024,2]{3,2,1,0:T(8,128)} %reshape.318, f32[]{:T(128)} %constant.16.clone.1), dimensions={1,3}, to_apply=%region_8.9 | reduce | flops 98304 | bytes 655364 | tf_op jit(solution)/shard_map/reduce_sum | solution.py:59
  715.5 7.2 collective-permute-start.73
  725.4 10.5 reshape.319
  742.4 7.6 collective-permute-start.49
  754.2 10.5 reshape.330
  772.2 7.6 collective-permute-start.75
  796.3 7.0 collective-permute-start.77
  814.1 7.6 collective-permute-start.53
  834.1 7.6 collective-permute-start.79
  859.2 7.4 collective-permute-start.81
  883.2 7.6 collective-permute-start.57
  892.7 7.6 collective-permute-start.83
  903.2 7.6 collective-permute-start.59
  913.7 7.6 collective-permute-start.85
  924.2 7.6 collective-permute-start.61
  935.8 7.6 collective-permute-start.87
  1003.5 6.9 collective-permute-start.91
  1046.3 7.7 collective-permute-start.93
  1079.8 7.6 collective-permute-start.69
  1094.4 7.6 collective-permute-start.97
  1111.4 10.5 reshape.339
  1149.7 6.5 collective-permute-done.100
  1196.7 7.8 collective-permute-start.107
  1207.7 7.8 collective-permute-start.109
  1219.1 7.8 collective-permute-start.111
  1234.3 7.8 collective-permute-start.113
  1276.2 7.5 collective-permute-start.117
  1307.8 52.8 %all_to_all.5 = f32[2,128,1024]{1,2,0:T(8,128)S(1)} all-to-all(f32[2,128,1024]{1,2,0:T(8,128)S(1)} %bitcast.620), channel_id=1, replica_groups=mesh['samp'=2,'grid'=64] {'samp'}, dimensions={0} | all-to-all | bytes 2097152 | tf_op jit(solution)/shard_map/all_to_all | solution.py:35
  (928 shorter events, 798.3 us)
Async XLA Ops:
  6.6 218.1 %collective-permute-start.1 = (f32[2,2,2048]{2,1,0:T(2,128)}, f32[2,2,2048]{2,1,0:T(2,128)}, u32[]{:S(2)}, u32[]{:S(2)}) collective-permute-start(f32[2,2,2048]{2,1,0:T(2,128)} %copy.365), channel_id=1, source_target_pairs={{1,0},{2,1},{3,2},{4,3},{5,4},{6,5},{7,6},{8,7},{9,8},{10,9},{11,1... | collective-permute-start | bytes 98312 | tf_op jit(solution)/shard_map/ppermute | solution.py:22
  14.5 213.0 %collective-permute-start = (f32[2,2,2048]{2,1,0:T(2,128)}, f32[2,2,2048]{2,1,0:T(2,128)}, u32[]{:S(2)}, u32[]{:S(2)}) collective-permute-start(f32[2,2,2048]{2,1,0:T(2,128)} %copy.364), channel_id=1, source_target_pairs={{0,1},{1,2},{2,3},{3,4},{4,5},{5,6},{6,7},{7,8},{8,9},{9,10},{10,1... | collective-permute-start | bytes 98312 | tf_op jit(solution)/shard_map/ppermute | solution.py:21
  22.4 193.5 %collective-permute-start.3 = (f32[2,2048]{1,0:T(2,128)}, f32[2,2048]{1,0:T(2,128)}, u32[]{:S(2)}, u32[]{:S(2)}) collective-permute-start(f32[2,2048]{1,0:T(2,128)} %copy.370), channel_id=1, source_target_pairs={{1,0},{2,1},{3,2},{4,3},{5,4},{6,5},{7,6},{8,7},{9,8},{10,9},{11,1... | collective-permute-start | bytes 49160 | tf_op jit(solution)/shard_map/ppermute | solution.py:22
  103.5 64.0 %collective-permute-start.25 = (f32[1,128]{1,0:T(1,128)S(1)}, f32[1,128]{1,0:T(1,128)S(1)}, u32[]{:S(2)}, u32[]{:S(2)}) collective-permute-start(f32[1,128]{1,0:T(1,128)S(1)} %get-tuple-element.378), channel_id=1, source_target_pairs={{1,0},{2,1},{3,2},{4,3},{5,4},{6,5},{7,6},{8,7},{9,8},{10,9},{11,1... | collective-permute-start | bytes 1544 | tf_op jit(solution)/shard_map/ppermute | solution.py:22
  105.5 63.9 %collective-permute-start.24 = (f32[1,128]{1,0:T(1,128)S(1)}, f32[1,128]{1,0:T(1,128)S(1)}, u32[]{:S(2)}, u32[]{:S(2)}) collective-permute-start(f32[1,128]{1,0:T(1,128)S(1)} %get-tuple-element.379), channel_id=1, source_target_pairs={{0,1},{1,2},{2,3},{3,4},{4,5},{5,6},{6,7},{7,8},{8,9},{9,10},{10,1... | collective-permute-start | bytes 1544 | tf_op jit(solution)/shard_map/ppermute | solution.py:21
  167.5 50.5 %collective-permute-start.2 = (f32[2,2048]{1,0:T(2,128)}, f32[2,2048]{1,0:T(2,128)S(1)}, u32[]{:S(2)}, u32[]{:S(2)}) collective-permute-start(f32[2,2048]{1,0:T(2,128)} %copy.369), channel_id=1, source_target_pairs={{0,1},{1,2},{2,3},{3,4},{4,5},{5,6},{6,7},{7,8},{8,9},{9,10},{10,1... | collective-permute-start | bytes 49160 | tf_op jit(solution)/shard_map/ppermute | solution.py:21
  468.1 22.3 %collective-permute-start.33 = (f32[2,256]{1,0:T(2,128)S(1)}, f32[2,256]{1,0:T(2,128)S(1)}, u32[]{:S(2)}, u32[]{:S(2)}) collective-permute-start(f32[2,256]{1,0:T(2,128)S(1)} %get-tuple-element.275), channel_id=1, source_target_pairs={{1,0},{2,1},{3,2},{4,3},{5,4},{6,5},{7,6},{8,7},{9,8},{10,9},{11,1... | collective-permute-start | bytes 6152 | tf_op jit(solution)/shard_map/ppermute | solution.py:22
  475.9 14.5 %collective-permute-start.32 = (f32[2,256]{1,0:T(2,128)S(1)}, f32[2,256]{1,0:T(2,128)S(1)}, u32[]{:S(2)}, u32[]{:S(2)}) collective-permute-start(f32[2,256]{1,0:T(2,128)S(1)} %get-tuple-element.274), channel_id=1, source_target_pairs={{0,1},{1,2},{2,3},{3,4},{4,5},{5,6},{6,7},{7,8},{8,9},{9,10},{10,1... | collective-permute-start | bytes 6152 | tf_op jit(solution)/shard_map/ppermute | solution.py:21
  479.3 30.0 %collective-permute-start.71 = (f32[2,2,1024]{2,1,0:T(2,128)}, f32[2,2,1024]{2,1,0:T(2,128)}, u32[]{:S(2)}, u32[]{:S(2)}) collective-permute-start(f32[2,2,1024]{2,1,0:T(2,128)} %get-tuple-element.155), channel_id=1, source_target_pairs={{1,0},{2,1},{3,2},{4,3},{5,4},{6,5},{7,6},{8,7},{9,8},{10,9},{11,1... | collective-permute-start | bytes 49160 | tf_op jit(solution)/shard_map/ppermute | solution.py:22
  486.8 22.5 %collective-permute-start.70 = (f32[2,2,1024]{2,1,0:T(2,128)}, f32[2,2,1024]{2,1,0:T(2,128)}, u32[]{:S(2)}, u32[]{:S(2)}) collective-permute-start(f32[2,2,1024]{2,1,0:T(2,128)} %get-tuple-element.154), channel_id=1, source_target_pairs={{0,1},{1,2},{2,3},{3,4},{4,5},{5,6},{6,7},{7,8},{8,9},{9,10},{10,1... | collective-permute-start | bytes 49160 | tf_op jit(solution)/shard_map/ppermute | solution.py:21
  708.8 15.8 %collective-permute-start.47 = (f32[1,1024]{1,0:T(1,128)S(1)}, f32[1,1024]{1,0:T(1,128)S(1)}, u32[]{:S(2)}, u32[]{:S(2)}) collective-permute-start(f32[1,1024]{1,0:T(1,128)S(1)} %get-tuple-element.127), channel_id=1, source_target_pairs={{1,0},{2,1},{3,2},{4,3},{5,4},{6,5},{7,6},{8,7},{9,8},{10,9},{11,1... | collective-permute-start | bytes 12296 | tf_op jit(solution)/shard_map/ppermute | solution.py:22
  711.8 12.8 collective-permute-start.46
  715.5 36.6 %collective-permute-start.73 = (f32[1,1024]{1,0:T(1,128)}, f32[1,1024]{1,0:T(1,128)}, u32[]{:S(2)}, u32[]{:S(2)}) collective-permute-start(f32[1,1024]{1,0:T(1,128)} %get-tuple-element.147), channel_id=1, source_target_pairs={{1,0},{2,1},{3,2},{4,3},{5,4},{6,5},{7,6},{8,7},{9,8},{10,9},{11,1... | collective-permute-start | bytes 12296 | tf_op jit(solution)/shard_map/ppermute | solution.py:22
  722.6 29.5 %collective-permute-start.72 = (f32[1,1024]{1,0:T(1,128)}, f32[1,1024]{1,0:T(1,128)}, u32[]{:S(2)}, u32[]{:S(2)}) collective-permute-start(f32[1,1024]{1,0:T(1,128)} %get-tuple-element.146), channel_id=1, source_target_pairs={{0,1},{1,2},{2,3},{3,4},{4,5},{5,6},{6,7},{7,8},{8,9},{9,10},{10,1... | collective-permute-start | bytes 12296 | tf_op jit(solution)/shard_map/ppermute | solution.py:21
  742.4 39.3 %collective-permute-start.49 = (f32[2,2,512]{2,1,0:T(2,128)}, f32[2,2,512]{2,1,0:T(2,128)}, u32[]{:S(2)}, u32[]{:S(2)}) collective-permute-start(f32[2,2,512]{2,1,0:T(2,128)} %get-tuple-element.201), channel_id=1, source_target_pairs={{1,0},{2,1},{3,2},{4,3},{5,4},{6,5},{7,6},{8,7},{9,8},{10,9},{11,1... | collective-permute-start | bytes 24584 | tf_op jit(solution)/shard_map/ppermute | solution.py:22
  750.0 31.7 %collective-permute-start.48 = (f32[2,2,512]{2,1,0:T(2,128)}, f32[2,2,512]{2,1,0:T(2,128)}, u32[]{:S(2)}, u32[]{:S(2)}) collective-permute-start(f32[2,2,512]{2,1,0:T(2,128)} %get-tuple-element.200), channel_id=1, source_target_pairs={{0,1},{1,2},{2,3},{3,4},{4,5},{5,6},{6,7},{7,8},{8,9},{9,10},{10,1... | collective-permute-start | bytes 24584 | tf_op jit(solution)/shard_map/ppermute | solution.py:21
  789.8 15.5 %collective-permute-start.51 = (f32[1,512]{1,0:T(1,128)S(1)}, f32[1,512]{1,0:T(1,128)S(1)}, u32[]{:S(2)}, u32[]{:S(2)}) collective-permute-start(f32[1,512]{1,0:T(1,128)S(1)} %get-tuple-element.199), channel_id=1, source_target_pairs={{1,0},{2,1},{3,2},{4,3},{5,4},{6,5},{7,6},{8,7},{9,8},{10,9},{11,1... | collective-permute-start | bytes 6152 | tf_op jit(solution)/shard_map/ppermute | solution.py:22
  796.3 27.3 %collective-permute-start.77 = (f32[1,512]{1,0:T(1,128)}, f32[1,512]{1,0:T(1,128)}, u32[]{:S(2)}, u32[]{:S(2)}) collective-permute-start(f32[1,512]{1,0:T(1,128)} %get-tuple-element.221), channel_id=1, source_target_pairs={{1,0},{2,1},{3,2},{4,3},{5,4},{6,5},{7,6},{8,7},{9,8},{10,9},{11,1... | collective-permute-start | bytes 6152 | tf_op jit(solution)/shard_map/ppermute | solution.py:22
  803.3 20.3 %collective-permute-start.76 = (f32[1,512]{1,0:T(1,128)}, f32[1,512]{1,0:T(1,128)}, u32[]{:S(2)}, u32[]{:S(2)}) collective-permute-start(f32[1,512]{1,0:T(1,128)} %get-tuple-element.220), channel_id=1, source_target_pairs={{0,1},{1,2},{2,3},{3,4},{4,5},{5,6},{6,7},{7,8},{8,9},{9,10},{10,1... | collective-permute-start | bytes 6152 | tf_op jit(solution)/shard_map/ppermute | solution.py:21
  814.1 29.6 %collective-permute-start.53 = (f32[2,2,256]{2,1,0:T(2,128)}, f32[2,2,256]{2,1,0:T(2,128)}, u32[]{:S(2)}, u32[]{:S(2)}) collective-permute-start(f32[2,2,256]{2,1,0:T(2,128)} %get-tuple-element.273), channel_id=1, source_target_pairs={{1,0},{2,1},{3,2},{4,3},{5,4},{6,5},{7,6},{8,7},{9,8},{10,9},{11,1... | collective-permute-start | bytes 12296 | tf_op jit(solution)/shard_map/ppermute | solution.py:22
  821.6 22.0 %collective-permute-start.52 = (f32[2,2,256]{2,1,0:T(2,128)}, f32[2,2,256]{2,1,0:T(2,128)}, u32[]{:S(2)}, u32[]{:S(2)}) collective-permute-start(f32[2,2,256]{2,1,0:T(2,128)} %get-tuple-element.272), channel_id=1, source_target_pairs={{0,1},{1,2},{2,3},{3,4},{4,5},{5,6},{6,7},{7,8},{8,9},{9,10},{10,1... | collective-permute-start | bytes 12296 | tf_op jit(solution)/shard_map/ppermute | solution.py:21
  852.7 15.9 %collective-permute-start.55 = (f32[1,256]{1,0:T(1,128)S(1)}, f32[1,256]{1,0:T(1,128)S(1)}, u32[]{:S(2)}, u32[]{:S(2)}) collective-permute-start(f32[1,256]{1,0:T(1,128)S(1)} %get-tuple-element.271), channel_id=1, source_target_pairs={{1,0},{2,1},{3,2},{4,3},{5,4},{6,5},{7,6},{8,7},{9,8},{10,9},{11,1... | collective-permute-start | bytes 3080 | tf_op jit(solution)/shard_map/ppermute | solution.py:22
  859.2 14.4 %collective-permute-start.81 = (f32[1,256]{1,0:T(1,128)}, f32[1,256]{1,0:T(1,128)}, u32[]{:S(2)}, u32[]{:S(2)}) collective-permute-start(f32[1,256]{1,0:T(1,128)} %get-tuple-element.293), channel_id=1, source_target_pairs={{1,0},{2,1},{3,2},{4,3},{5,4},{6,5},{7,6},{8,7},{9,8},{10,9},{11,1... | collective-permute-start | bytes 3080 | tf_op jit(solution)/shard_map/ppermute | solution.py:22
  881.2 19.1 %collective-permute-start.56 = (f32[1,128]{1,0:T(1,128)S(1)}, f32[1,128]{1,0:T(1,128)S(1)}, u32[]{:S(2)}, u32[]{:S(2)}) collective-permute-start(f32[1,128]{1,0:T(1,128)S(1)} %get-tuple-element.320), channel_id=1, source_target_pairs={{0,1},{1,2},{2,3},{3,4},{4,5},{5,6},{6,7},{7,8},{8,9},{9,10},{10,1... | collective-permute-start | bytes 1544 | tf_op jit(solution)/shard_map/ppermute | solution.py:21
  883.2 17.2 %collective-permute-start.57 = (f32[1,128]{1,0:T(1,128)S(1)}, f32[1,128]{1,0:T(1,128)S(1)}, u32[]{:S(2)}, u32[]{:S(2)}) collective-permute-start(f32[1,128]{1,0:T(1,128)S(1)} %get-tuple-element.321), channel_id=1, source_target_pairs={{1,0},{2,1},{3,2},{4,3},{5,4},{6,5},{7,6},{8,7},{9,8},{10,9},{11,1... | collective-permute-start | bytes 1544 | tf_op jit(solution)/shard_map/ppermute | solution.py:22
  890.8 20.0 %collective-permute-start.82 = (f32[1,128]{1,0:T(1,128)S(1)}, f32[1,128]{1,0:T(1,128)S(1)}, u32[]{:S(2)}, u32[]{:S(2)}) collective-permute-start(f32[1,128]{1,0:T(1,128)S(1)} %get-tuple-element.374), channel_id=1, source_target_pairs={{0,1},{1,2},{2,3},{3,4},{4,5},{5,6},{6,7},{7,8},{8,9},{9,10},{10,1... | collective-permute-start | bytes 1544 | tf_op jit(solution)/shard_map/ppermute | solution.py:21
  892.7 18.1 %collective-permute-start.83 = (f32[1,128]{1,0:T(1,128)S(1)}, f32[1,128]{1,0:T(1,128)S(1)}, u32[]{:S(2)}, u32[]{:S(2)}) collective-permute-start(f32[1,128]{1,0:T(1,128)S(1)} %get-tuple-element.375), channel_id=1, source_target_pairs={{1,0},{2,1},{3,2},{4,3},{5,4},{6,5},{7,6},{8,7},{9,8},{10,9},{11,1... | collective-permute-start | bytes 1544 | tf_op jit(solution)/shard_map/ppermute | solution.py:22
  901.3 20.0 %collective-permute-start.58 = (f32[1,128]{1,0:T(1,128)S(1)}, f32[1,128]{1,0:T(1,128)S(1)}, u32[]{:S(2)}, u32[]{:S(2)}) collective-permute-start(f32[1,128]{1,0:T(1,128)S(1)} %get-tuple-element.314), channel_id=1, source_target_pairs={{0,1},{1,2},{2,3},{3,4},{4,5},{5,6},{6,7},{7,8},{8,9},{9,10},{10,1... | collective-permute-start | bytes 1544 | tf_op jit(solution)/shard_map/ppermute | solution.py:21
  903.2 18.1 %collective-permute-start.59 = (f32[1,128]{1,0:T(1,128)S(1)}, f32[1,128]{1,0:T(1,128)S(1)}, u32[]{:S(2)}, u32[]{:S(2)}) collective-permute-start(f32[1,128]{1,0:T(1,128)S(1)} %get-tuple-element.315), channel_id=1, source_target_pairs={{1,0},{2,1},{3,2},{4,3},{5,4},{6,5},{7,6},{8,7},{9,8},{10,9},{11,1... | collective-permute-start | bytes 1544 | tf_op jit(solution)/shard_map/ppermute | solution.py:22
  911.8 20.0 %collective-permute-start.84 = (f32[1,128]{1,0:T(1,128)S(1)}, f32[1,128]{1,0:T(1,128)S(1)}, u32[]{:S(2)}, u32[]{:S(2)}) collective-permute-start(f32[1,128]{1,0:T(1,128)S(1)} %get-tuple-element.368), channel_id=1, source_target_pairs={{0,1},{1,2},{2,3},{3,4},{4,5},{5,6},{6,7},{7,8},{8,9},{9,10},{10,1... | collective-permute-start | bytes 1544 | tf_op jit(solution)/shard_map/ppermute | solution.py:21
  913.7 18.1 %collective-permute-start.85 = (f32[1,128]{1,0:T(1,128)S(1)}, f32[1,128]{1,0:T(1,128)S(1)}, u32[]{:S(2)}, u32[]{:S(2)}) collective-permute-start(f32[1,128]{1,0:T(1,128)S(1)} %get-tuple-element.369), channel_id=1, source_target_pairs={{1,0},{2,1},{3,2},{4,3},{5,4},{6,5},{7,6},{8,7},{9,8},{10,9},{11,1... | collective-permute-start | bytes 1544 | tf_op jit(solution)/shard_map/ppermute | solution.py:22
  922.2 21.2 %collective-permute-start.60 = (f32[1,128]{1,0:T(1,128)S(1)}, f32[1,128]{1,0:T(1,128)S(1)}, u32[]{:S(2)}, u32[]{:S(2)}) collective-permute-start(f32[1,128]{1,0:T(1,128)S(1)} %get-tuple-element.308), channel_id=1, source_target_pairs={{0,1},{1,2},{2,3},{3,4},{4,5},{5,6},{6,7},{7,8},{8,9},{9,10},{10,1... | collective-permute-start | bytes 1544 | tf_op jit(solution)/shard_map/ppermute | solution.py:21
  924.2 19.3 %collective-permute-start.61 = (f32[1,128]{1,0:T(1,128)S(1)}, f32[1,128]{1,0:T(1,128)S(1)}, u32[]{:S(2)}, u32[]{:S(2)}) collective-permute-start(f32[1,128]{1,0:T(1,128)S(1)} %get-tuple-element.309), channel_id=1, source_target_pairs={{1,0},{2,1},{3,2},{4,3},{5,4},{6,5},{7,6},{8,7},{9,8},{10,9},{11,1... | collective-permute-start | bytes 1544 | tf_op jit(solution)/shard_map/ppermute | solution.py:22
  933.9 22.7 %collective-permute-start.86 = (f32[1,128]{1,0:T(1,128)}, f32[1,128]{1,0:T(1,128)}, u32[]{:S(2)}, u32[]{:S(2)}) collective-permute-start(f32[1,128]{1,0:T(1,128)} %get-tuple-element.362), channel_id=1, source_target_pairs={{0,1},{1,2},{2,3},{3,4},{4,5},{5,6},{6,7},{7,8},{8,9},{9,10},{10,1... | collective-permute-start | bytes 1544 | tf_op jit(solution)/shard_map/ppermute | solution.py:21
  935.8 20.8 %collective-permute-start.87 = (f32[1,128]{1,0:T(1,128)}, f32[1,128]{1,0:T(1,128)}, u32[]{:S(2)}, u32[]{:S(2)}) collective-permute-start(f32[1,128]{1,0:T(1,128)} %get-tuple-element.363), channel_id=1, source_target_pairs={{1,0},{2,1},{3,2},{4,3},{5,4},{6,5},{7,6},{8,7},{9,8},{10,9},{11,1... | collective-permute-start | bytes 1544 | tf_op jit(solution)/shard_map/ppermute | solution.py:22
  951.3 20.8 %collective-permute-start.63 = (f32[2,256]{1,0:T(2,128)}, f32[2,256]{1,0:T(2,128)}, u32[]{:S(2)}, u32[]{:S(2)}) collective-permute-start(f32[2,256]{1,0:T(2,128)} %get-tuple-element.267), channel_id=1, source_target_pairs={{1,0},{2,1},{3,2},{4,3},{5,4},{6,5},{7,6},{8,7},{9,8},{10,9},{11,1... | collective-permute-start | bytes 6152 | tf_op jit(solution)/shard_map/ppermute | solution.py:22
  953.2 18.9 %collective-permute-start.62 = (f32[2,256]{1,0:T(2,128)}, f32[2,256]{1,0:T(2,128)}, u32[]{:S(2)}, u32[]{:S(2)}) collective-permute-start(f32[2,256]{1,0:T(2,128)} %get-tuple-element.266), channel_id=1, source_target_pairs={{0,1},{1,2},{2,3},{3,4},{4,5},{5,6},{6,7},{7,8},{8,9},{9,10},{10,1... | collective-permute-start | bytes 6152 | tf_op jit(solution)/shard_map/ppermute | solution.py:21
  989.9 22.8 %collective-permute-start.65 = (f32[2,512]{1,0:T(2,128)}, f32[2,512]{1,0:T(2,128)}, u32[]{:S(2)}, u32[]{:S(2)}) collective-permute-start(f32[2,512]{1,0:T(2,128)} %get-tuple-element.195), channel_id=1, source_target_pairs={{1,0},{2,1},{3,2},{4,3},{5,4},{6,5},{7,6},{8,7},{9,8},{10,9},{11,1... | collective-permute-start | bytes 12296 | tf_op jit(solution)/shard_map/ppermute | solution.py:22
  992.7 20.1 %collective-permute-start.64 = (f32[2,512]{1,0:T(2,128)}, f32[2,512]{1,0:T(2,128)}, u32[]{:S(2)}, u32[]{:S(2)}) collective-permute-start(f32[2,512]{1,0:T(2,128)} %get-tuple-element.194), channel_id=1, source_target_pairs={{0,1},{1,2},{2,3},{3,4},{4,5},{5,6},{6,7},{7,8},{8,9},{9,10},{10,1... | collective-permute-start | bytes 12296 | tf_op jit(solution)/shard_map/ppermute | solution.py:21
  1031.6 24.3 %collective-permute-start.67 = (f32[2,1024]{1,0:T(2,128)}, f32[2,1024]{1,0:T(2,128)}, u32[]{:S(2)}, u32[]{:S(2)}) collective-permute-start(f32[2,1024]{1,0:T(2,128)} %get-tuple-element.119), channel_id=1, source_target_pairs={{1,0},{2,1},{3,2},{4,3},{5,4},{6,5},{7,6},{8,7},{9,8},{10,9},{11,1... | collective-permute-start | bytes 24584 | tf_op jit(solution)/shard_map/ppermute | solution.py:22
  1034.9 21.0 %collective-permute-start.66 = (f32[2,1024]{1,0:T(2,128)}, f32[2,1024]{1,0:T(2,128)}, u32[]{:S(2)}, u32[]{:S(2)}) collective-permute-start(f32[2,1024]{1,0:T(2,128)} %get-tuple-element.118), channel_id=1, source_target_pairs={{0,1},{1,2},{2,3},{3,4},{4,5},{5,6},{6,7},{7,8},{8,9},{9,10},{10,1... | collective-permute-start | bytes 24584 | tf_op jit(solution)/shard_map/ppermute | solution.py:21
  1064.0 27.6 %collective-permute-start.95 = (f32[2,2,1024]{2,1,0:T(2,128)}, f32[2,2,1024]{2,1,0:T(2,128)}, u32[]{:S(2)}, u32[]{:S(2)}) collective-permute-start(f32[2,2,1024]{2,1,0:T(2,128)} %get-tuple-element.83), channel_id=1, source_target_pairs={{1,0},{2,1},{3,2},{4,3},{5,4},{6,5},{7,6},{8,7},{9,8},{10,9},{11,1... | collective-permute-start | bytes 49160 | tf_op jit(solution)/shard_map/ppermute | solution.py:22
  1067.8 23.8 %collective-permute-start.94 = (f32[2,2,1024]{2,1,0:T(2,128)}, f32[2,2,1024]{2,1,0:T(2,128)}, u32[]{:S(2)}, u32[]{:S(2)}) collective-permute-start(f32[2,2,1024]{2,1,0:T(2,128)} %get-tuple-element.82), channel_id=1, source_target_pairs={{0,1},{1,2},{2,3},{3,4},{4,5},{5,6},{6,7},{7,8},{8,9},{9,10},{10,1... | collective-permute-start | bytes 49160 | tf_op jit(solution)/shard_map/ppermute | solution.py:21
  1079.8 53.8 %collective-permute-start.69 = (f32[2,2048]{1,0:T(2,128)}, f32[2,2048]{1,0:T(2,128)}, u32[]{:S(2)}, u32[]{:S(2)}) collective-permute-start(f32[2,2048]{1,0:T(2,128)} %copy.417), channel_id=1, source_target_pairs={{1,0},{2,1},{3,2},{4,3},{5,4},{6,5},{7,6},{8,7},{9,8},{10,9},{11,1... | collective-permute-start | bytes 49160 | tf_op jit(solution)/shard_map/ppermute | solution.py:22
  1089.6 46.3 %collective-permute-start.68 = (f32[2,2048]{1,0:T(2,128)}, f32[2,2048]{1,0:T(2,128)}, u32[]{:S(2)}, u32[]{:S(2)}) collective-permute-start(f32[2,2048]{1,0:T(2,128)} %copy.416), channel_id=1, source_target_pairs={{0,1},{1,2},{2,3},{3,4},{4,5},{5,6},{6,7},{7,8},{8,9},{9,10},{10,1... | collective-permute-start | bytes 49160 | tf_op jit(solution)/shard_map/ppermute | solution.py:21
  1234.3 13.4 collective-permute-start.113
  1255.5 12.9 collective-permute-start.115
  1276.2 13.1 collective-permute-start.117
  (190 other events, 1842.0 us)
where the time goes:
time: 1380 us; the launch traced here: 1360 us
  local copies, waits for them, and re-layouts  478 us (35%)
  starting transfers between devices  459 us (33%)
  other arithmetic  243 us (18%)
  waiting for transfers between devices  125 us (9%)
  blocking collectives  52.8 us (4%)
    ppermute x59, starting transfers between devices, extended_2(): after = lax.ppermute(initial, axis, down)  328 us
    reshape x14, local copies, waits for them, and re-layouts, quad_sum(): values.reshape(row_count // 2, 2, col_count // 2, 2)  141 us
    ppermute x59, starting transfers between devices, extended_2(): before = lax.ppermute(last, axis, up)  131 us
    ppermute x59, waiting for transfers between devices, extended_2(): before = lax.ppermute(last, axis, up)  121 us
    reduce_sum x15, other arithmetic, quad_sum(): jnp.sum(values.reshape(row_count // 2, 2, col_count // 2, 2), axis=(1, 3))  78.2 us
    reshape x38, local copies, waits for them, and re-layouts, expand(): return jnp.repeat(jnp.repeat(values, 2, axis=0), 2, axis=1)  57.3 us
    all_to_all x1, blocking collectives, sum_at_owner(): lax.all_to_all(blocks, axis, split_axis=0, concat_axis=0, tiled=True)  52.8 us
    exp x3, local copies, waits for them, and re-layouts, local(): coeffs = jnp.exp(log_coef[0])  39.2 us
  transfers between devices with their start and end apart: 118, of which 37 were waited for; matrix products, arithmetic and copies ran while one was open for 28% of the time, Pallas kernels for 0%

commit v1 on v0

v1 whole, which is shorter than its diff:
```python
import functools

import jax
import jax.numpy as jnp
from jax import lax
from jax.experimental import pallas as pl
from jax.experimental.pallas import tpu as pltpu
from jax.sharding import PartitionSpec as P

LANES = 128
PAD = 8
OWN = (64, 32, 16, 8, 4)
HALO = (24, 12, 32, 16, 8)
ROWS = tuple(o + 2 * h for o, h in zip(OWN, HALO))
TILES = (16, 8, 4, 2, 1)
STRIPS = (14, 7, 10, 5, 3)
BUF = tuple(8 * s + 2 * PAD for s in STRIPS)
DAMP = 0.8
F32 = jnp.float32


def loop(count, body, unroll=1):
    lax.fori_loop(0, count, lambda i, c: (body(i), c)[1], 0, unroll=unroll)


def at(i, offset):
    return pl.ds(pl.multiple_of(i * 8, 8) + offset, 8)


def lane_of(x):
    return lax.broadcasted_iota(jnp.int32, x.shape, 2)


def side_values(x):
    lane = lane_of(x)
    right = pltpu.roll(x, 1, 2)
    left = pltpu.roll(x, LANES - 1, 2)
    if x.shape[0] > 1:
        before = jnp.concatenate([right[-1:], right[:-1]], axis=0)
        after = jnp.concatenate([left[1:], left[:1]], axis=0)
        right = jnp.where(lane == 0, before, right)
        left = jnp.where(lane == LANES - 1, after, left)
    return right, left


def harmonic(a, b):
    return 2.0 * a * b / (a + b)


def make_weights(level, c_ref, a_ref, first_row, total_rows):
    def body(i):
        c = c_ref[:, at(i, PAD), :]
        north = c_ref[:, at(i, PAD - 1), :]
        south = c_ref[:, at(i, PAD + 1), :]
        west, east = side_values(c)
        tile = lax.broadcasted_iota(jnp.int32, c.shape, 0)
        lane = lane_of(c)
        row = first_row + i * 8 + lax.broadcasted_iota(jnp.int32, c.shape, 1)
        at_west = jnp.logical_and(tile == 0, lane == 0)
        at_east = jnp.logical_and(tile == c.shape[0] - 1, lane == LANES - 1)
        inside = jnp.logical_and(row >= 0, row < total_rows)
        w_west = harmonic(c, jnp.where(at_west, c, west))
        w_east = harmonic(c, jnp.where(at_east, c, east))
        w_north = harmonic(c, jnp.where(row == 0, c, north))
        w_south = harmonic(c, jnp.where(row == total_rows - 1, c, south))
        diagonal = w_west + w_east + w_north + w_south
        gain = jnp.where(inside, DAMP / diagonal, 0.0)
        rows = at(i, 0)
        a_ref[0, :, rows, :] = jnp.where(at_west, 0.0, gain * w_west)
        a_ref[1, :, rows, :] = jnp.where(at_east, 0.0, gain * w_east)
        a_ref[2, :, rows, :] = gain * w_north
        a_ref[3, :, rows, :] = gain * w_south
        a_ref[4, :, rows, :] = gain
        a_ref[5, :, rows, :] = diagonal * (1.0 / DAMP)

    loop(STRIPS[level], body)


def change(i, v_ref, b_ref, a_ref, start, count):
    tiles = pl.ds(start, count)
    v = v_ref[tiles, at(i, PAD), :]
    north = v_ref[tiles, at(i, PAD - 1), :]
    south = v_ref[tiles, at(i, PAD + 1), :]
    west, east = side_values(v)
    rows = at(i, 0)
    moved = a_ref[0, :, rows, :] * west + a_ref[1, :, rows, :] * east
    moved += a_ref[2, :, rows, :] * north + a_ref[3, :, rows, :] * south
    return v, moved + b_ref[tiles, at(i, PAD), :]


def solves(level, v_ref):
    tiles = TILES[level]
    return [(s, tiles) for s in range(0, v_ref.shape[0], tiles)]


def relax(level, v_ref, out_ref, b_ref, a_ref):
    def body(i):
        for start, count in solves(level, v_ref):
            v, moved = change(i, v_ref, b_ref, a_ref, start, count)
            out_ref[pl.ds(start, count), at(i, PAD), :] = (1.0 - DAMP) * v + moved

    loop(STRIPS[level], body)


def residual(level, v_ref, out_ref, b_ref, a_ref):
    def body(i):
        for start, count in solves(level, v_ref):
            v, moved = change(i, v_ref, b_ref, a_ref, start, count)
            out_ref[pl.ds(start, count), at(i, PAD), :] = a_ref[5, :, at(i, 0), :] * (moved - DAMP * v)

    loop(STRIPS[level], body)


def take(x, index):
    return jnp.take_along_axis(x, index, axis=1, mode="promise_in_bounds")


def quad_strip(ref, j, offset, tiles):
    base = pl.multiple_of(j * 16, 16) + offset
    lane = lax.broadcasted_iota(jnp.int32, (8, LANES), 1)
    even_lane = lax.rem(2 * lane, LANES)
    packed = []
    for t in tiles:
        pair = ref[t, pl.ds(base, 8, stride=2), :] + ref[t, pl.ds(base + 1, 8, stride=2), :]
        pair = pair + pltpu.roll(pair, LANES - 1, 1)
        packed.append(take(pair, even_lane))
    if len(packed) == 1:
        return [jnp.where(lane < LANES // 2, packed[0], 0.0)]
    return [jnp.where(lane < LANES // 2, packed[k], packed[k + 1]) for k in range(0, len(packed), 2)]


def restrict(count, ref, offset, tiles, store):
    def body(j):
        for k, q in enumerate(quad_strip(ref, j, offset, tiles)):
            store(j, k, q)

    loop(count, body)


def spread_strip(e_ref, j, offset, tiles):
    lane = lax.broadcasted_iota(jnp.int32, (8, LANES), 1)
    low = lax.div(lane, 2)
    high = low + LANES // 2
    rows = at(j, offset)
    out = []
    for t in tiles:
        e = e_ref[t, rows, :]
        out += [take(e, low), take(e, high)]
    return out


def prolong(count, e_ref, offset, e_tiles, v_ref, sign=1.0, v_offset=PAD, first=0):
    def body(j):
        base = pl.multiple_of(j * 16, 16) + v_offset
        for k, x in enumerate(spread_strip(e_ref, j, offset, e_tiles)):
            for parity in range(2):
                rows = pl.ds(base + parity, 8, stride=2)
                v_ref[first + k, rows, :] = v_ref[first + k, rows, :] + sign * x

    loop(count, body)


def clear_pads(*refs, value=0.0):
    for ref in refs:
        tiles, rows, _ = ref.shape
        ref[:, 0:PAD, :] = jnp.full((tiles, PAD, LANES), value, F32)
        ref[:, rows - PAD : rows, :] = jnp.full((tiles, PAD, LANES), value, F32)


def fill(ref, value):
    def body(i):
        ref[:, at(i, 0), :] = jnp.full((ref.shape[0], 8, LANES), value, F32)

    loop(ref.shape[1] // 8, body)


def pack_kernel(log_ref, src_ref, up_ref, down_ref):
    halo, own = HALO[0], OWN[0]
    up_ref[0:halo, :] = log_ref[own - halo : own, :]
    up_ref[halo : 2 * halo, :] = src_ref[own - halo : own, :]
    down_ref[0:halo, :] = log_ref[0:halo, :]
    down_ref[halo : 2 * halo, :] = src_ref[0:halo, :]


def first_row(level):
    return lax.axis_index("grid") * OWN[level] - HALO[level]


def scaled_store(bp_ref, a_ref, start=0, coarse_tiles=None):
    def store(j, k, q):
        tile = k if coarse_tiles is None else k % coarse_tiles
        bp_ref[start + k, at(j, PAD), :] = a_ref[4, tile, at(j, 0), :] * q

    return store


def quarter_store(c_ref):
    def store(j, k, q):
        c_ref[k, at(j, PAD), :] = 0.25 * q

    return store


def open_kernel(
    peers, log_ref, src_ref, above_ref, below_ref,
    msg_ref, a0_out, b0_out, v0_out, a1_out, b1_out, v1_out,
    c0, a0, bp0, va0, vb0, c1, a1, bp1, va1, vb1, sems,
):
    copies = []

    def send(src, dst):
        copy = pltpu.make_async_copy(src, dst, sems.at[len(copies)])
        copy.start()
        copies.append(copy)

    halo, own = HALO[0], OWN[0]
    clear_pads(c0, c1, value=1.0)
    clear_pads(bp0, va0, vb0, bp1, va1, vb1)

    def load(count, log_from, log_row, src_from, src_row, row):
        def body(i):
            logs = log_from[at(i, log_row), :]
            sources = src_from[at(i, src_row), :]
            for t in range(TILES[0]):
                c0[t, at(i, PAD + row), :] = jnp.exp(logs[:, t * LANES : (t + 1) * LANES])
                vb0[t, at(i, PAD + row), :] = sources[:, t * LANES : (t + 1) * LANES]

        loop(count // 8, body)

    load(halo, above_ref, 0, above_ref, halo, 0)
    load(own, log_ref, 0, src_ref, 0, halo)
    load(halo, below_ref, 0, below_ref, halo, halo + own)

    make_weights(0, c0, a0, first_row(0), peers * OWN[0])
    send(a0, a0_out)

    def scale(i):
        bp0[:, at(i, PAD), :] = a0[4, :, at(i, 0), :] * vb0[:, at(i, PAD), :]

    loop(STRIPS[0], scale)
    send(bp0, b0_out)
    restrict(STRIPS[1], c0, PAD, range(TILES[0]), quarter_store(c1))
    make_weights(1, c1, a1, first_row(1), peers * OWN[1])
    send(a1, a1_out)
    restrict(STRIPS[1], vb0, PAD, range(TILES[0]), scaled_store(bp1, a1, TILES[1], TILES[1]))
    relax(0, bp0, va0, bp0, a0)
    send(va0, v0_out)
    residual(0, va0, vb0, bp0, a0)
    restrict(STRIPS[1], vb0, PAD, range(TILES[0]), scaled_store(bp1, a1))
    send(bp1, b1_out)
    relax(1, bp1, va1, bp1, a1)
    send(va1, v1_out)
    residual(1, va1, vb1, bp1, a1)

    def store(j, k, q):
        msg_ref[k, at(j, 0), :] = q

    restrict(OWN[2] // 8, vb1, PAD + HALO[1], range(2 * TILES[1]), store)

    def store_coef(j, k, q):
        msg_ref[2 * TILES[2] + k, at(j, 0), :] = 0.25 * q

    restrict(OWN[2] // 8, c1, PAD + HALO[1], range(TILES[1]), store_coef)
    for copy in copies:
        copy.wait()


def deep_solve(a, bp, va, vb):
    relax(2, bp[2], va[2], bp[2], a[2])
    residual(2, va[2], vb[2], bp[2], a[2])
    for s in range(2):
        restrict(STRIPS[3], vb[2], PAD, range(s * 4, s * 4 + 4), scaled_store(bp[3], a[3], s * 2))
    relax(3, bp[3], va[3], bp[3], a[3])
    residual(3, va[3], vb[3], bp[3], a[3])
    for s in range(2):
        restrict(STRIPS[4], vb[3], PAD, range(s * 2, s * 2 + 2), scaled_store(bp[4], a[4], s))
    relax(4, bp[4], va[4], bp[4], a[4])
    relax(4, va[4], vb[4], bp[4], a[4])
    relax(4, vb[4], va[4], bp[4], a[4])
    prolong(STRIPS[4], va[4], PAD, range(2), va[3])
    relax(3, va[3], vb[3], bp[3], a[3])
    relax(3, vb[3], va[3], bp[3], a[3])
    prolong(STRIPS[3], va[3], PAD, range(4), va[2])
    relax(2, va[2], vb[2], bp[2], a[2])
    relax(2, vb[2], va[2], bp[2], a[2])


def up_level_1(va2, va1, vb1, bp1, a1):
    offset = PAD + HALO[2] - HALO[1] // 2
    prolong(4, va2, offset, range(2 * TILES[2]), va1)
    relax(1, va1, vb1, bp1, a1)
    relax(1, vb1, va1, bp1, a1)


def up_level_0(va1, va0, vb0, bp0, a0):
    prolong(STRIPS[1], va1, PAD, range(TILES[1]), va0)
    relax(0, va0, vb0, bp0, a0)
    relax(0, vb0, va0, bp0, a0)


def assemble(messages, a2, bp2):
    for slab, m in enumerate(messages):
        for i in range(2):
            row = slab * OWN[2] + i * 8
            for k in range(2 * TILES[2]):
                bp2[k, PAD + row : PAD + row + 8, :] = (
                    a2[4, k % TILES[2], row : row + 8, :] * m[k, i * 8 : i * 8 + 8, :]
                )


def middle_kernel(
    peers, m0, m1, m2, m3, m4, a0_in, b0_in, v0_in, a1_in, b1_in, v1_in,
    msg_ref, a2_out, a3_out, a4_out, v0_out, b1_out, v1_out,
    a0, bp0, va0, vb0, a1, bp1, va1, vb1,
    c2, a2, bp2, va2, vb2, c3, a3, bp3, va3, vb3, c4, a4, bp4, va4, vb4, sems,
):
    count = 0

    def start(src, dst):
        nonlocal count
        copy = pltpu.make_async_copy(src, dst, sems.at[count])
        copy.start()
        count += 1
        return copy

    loads = [start(s, d) for s, d in ((a1_in, a1), (b1_in, bp1), (v1_in, va1), (a0_in, a0), (b0_in, bp0), (v0_in, va0))]
    messages = (m0, m1, m2, m3, m4)
    fill(c4, 1.0)
    clear_pads(c2, c3, value=1.0)
    for ref in (bp4, va4, vb4):
        fill(ref, 0.0)
    clear_pads(bp2, va2, vb2, bp3, va3, vb3, vb0, vb1)
    top = first_row(2)
    for slab, m in enumerate(messages):
        for i in range(2):
            row = slab * OWN[2] + i * 8
            place = top + row + lax.broadcasted_iota(jnp.int32, (8, LANES), 0)
            inside = jnp.logical_and(place >= 0, place < peers * OWN[2])
            for k in range(TILES[2]):
                c2[k, PAD + row : PAD + row + 8, :] = jnp.where(
                    inside, m[2 * TILES[2] + k, i * 8 : i * 8 + 8, :], 1.0
                )
    make_weights(2, c2, a2, top, peers * OWN[2])
    restrict(STRIPS[3], c2, PAD, range(4), quarter_store(c3))
    make_weights(3, c3, a3, first_row(3), peers * OWN[3])
    restrict(2, c3, PAD, range(2), quarter_store(c4))

    def last_rows(j, k, q):
        keep = lax.broadcasted_iota(jnp.int32, (8, LANES), 0) < ROWS[4] - 16
        c4[k, PAD + 16 : PAD + 24, :] = jnp.where(keep, 0.25 * q, 1.0)

    restrict(1, c3, PAD + 32, range(2), last_rows)
    make_weights(4, c4, a4, first_row(4), peers * OWN[4])
    stores = [start(s, d) for s, d in ((a2, a2_out), (a3, a3_out), (a4, a4_out))]
    assemble(messages, a2, bp2)
    a = {2: a2, 3: a3, 4: a4}
    bp = {2: bp2, 3: bp3, 4: bp4}
    va = {2: va2, 3: va3, 4: va4}
    vb = {2: vb2, 3: vb3, 4: vb4}
    deep_solve(a, bp, va, vb)
    for copy in loads:
        copy.wait()
    up_level_1(va2, va1, vb1, bp1, a1)
    up_level_0(va1, va0, vb0, bp0, a0)

    relax(0, va0, vb0, bp0, a0)
    relax(0, vb0, va0, bp0, a0)
    stores.append(start(va0, v0_out))
    residual(0, va0, vb0, bp0, a0)
    restrict(STRIPS[1], vb0, PAD, range(TILES[0]), scaled_store(bp1, a1))
    stores.append(start(bp1, b1_out))

    def clear(i):
        va1[0 : TILES[1], at(i, 0), :] = jnp.zeros((TILES[1], 8, LANES), F32)

    loop(BUF[1] // 8, clear)
    relax(1, va1, vb1, bp1, a1)
    relax(1, vb1, va1, bp1, a1)
    stores.append(start(va1, v1_out))
    residual(1, va1, vb1, bp1, a1)

    def store(j, k, q):
        msg_ref[k, at(j, 0), :] = q

    restrict(OWN[2] // 8, vb1, PAD + HALO[1], range(2 * TILES[1]), store)
    for copy in stores:
        copy.wait()


def close_kernel(
    m0, m1, m2, m3, m4, a0_in, b0_in, v0_in, a1_in, b1_in, v1_in, a2_in, a3_in, a4_in,
    out_ref, mine_ref, other_ref,
    a0, bp0, va0, vb0, a1, bp1, va1, vb1,
    a2, bp2, va2, vb2, a3, bp3, va3, vb3, a4, bp4, va4, vb4, sems,
):
    count = 0

    def start(src, dst):
        nonlocal count
        copy = pltpu.make_async_copy(src, dst, sems.at[count])
        copy.start()
        count += 1
        return copy

    first = [start(s, d) for s, d in ((a2_in, a2), (a3_in, a3), (a4_in, a4))]
    loads = [start(s, d) for s, d in ((a1_in, a1), (b1_in, bp1), (v1_in, va1), (a0_in, a0), (b0_in, bp0), (v0_in, va0))]
    for ref in (bp4, va4, vb4):
        fill(ref, 0.0)
    clear_pads(bp2, va2, vb2, bp3, va3, vb3, vb0, vb1)
    for copy in first:
        copy.wait()
    assemble((m0, m1, m2, m3, m4), a2, bp2)
    a = {2: a2, 3: a3, 4: a4}
    bp = {2: bp2, 3: bp3, 4: bp4}
    va = {2: va2, 3: va3, 4: va4}
    vb = {2: vb2, 3: vb3, 4: vb4}
    deep_solve(a, bp, va, vb)
    for copy in loads:
        copy.wait()
    up_level_1(va2, va1, vb1, bp1, a1)
    up_level_0(va1, va0, vb0, bp0, a0)
    prolong(OWN[1] // 8, va1, PAD + HALO[1], range(TILES[1], 2 * TILES[1]), va0, -1.0, PAD + HALO[0])
    here = lax.axis_index("samp") * (TILES[0] // 2)
    there = TILES[0] // 2 - here

    def body(i):
        rows = at(i, PAD + HALO[0])
        for t in range(TILES[0]):
            out_ref[at(i, 0), t * LANES : (t + 1) * LANES] = va0[t, rows, :]
        for t in range(TILES[0] // 2):
            mine_ref[at(i, 0), t * LANES : (t + 1) * LANES] = va0[here + t, rows, :]
            other_ref[at(i, 0), t * LANES : (t + 1) * LANES] = va0[there + t, rows, :]

    loop(OWN[0] // 8, body)


VMEM = pl.BlockSpec(memory_space=pltpu.VMEM)
ANY = pl.BlockSpec(memory_space=pl.ANY)


def shape(*dims):
    return jax.ShapeDtypeStruct(dims, F32)


def a_shape(level):
    return (6, TILES[level], 8 * STRIPS[level], LANES)


def v_shape(level):
    return ((1 if level == 0 else 2) * TILES[level], BUF[level], LANES)


def c_shape(level):
    return (TILES[level], BUF[level], LANES)


def scratch(*shapes):
    return [pltpu.VMEM(s, F32) for s in shapes]


def level_scratch(level):
    return [a_shape(level)] + [v_shape(level)] * 3


def shifted(value, distance):
    peers = lax.axis_size("grid")
    pairs = [(i, i + distance) for i in range(peers) if 0 <= i + distance < peers]
    return lax.ppermute(value, "grid", pairs)


def gathered(value):
    return [shifted(value, 2), shifted(value, 1), value, shifted(value, -1), shifted(value, -2)]


def local(log_coef, source):
    peers = lax.axis_size("grid")
    log_field, source_field = log_coef[0], source[0]
    rows, columns = source_field.shape
    edge = shape(2 * HALO[0], columns)
    up, down = pl.pallas_call(
        pack_kernel, out_shape=(edge, edge), in_specs=[VMEM] * 2, out_specs=(VMEM, VMEM), name="pack"
    )(log_field, source_field)
    above, below = shifted(up, 1), shifted(down, -1)

    state = [a_shape(0), v_shape(0), v_shape(0), a_shape(1), v_shape(1), v_shape(1)]
    deep_state = [a_shape(2), a_shape(3), a_shape(4)]
    message, a0, b0, v0, a1, b1, v1 = pl.pallas_call(
        functools.partial(open_kernel, peers),
        out_shape=[shape(3 * TILES[2], OWN[2], LANES)] + [shape(*s) for s in state],
        in_specs=[VMEM] * 4,
        out_specs=[VMEM] + [ANY] * 6,
        scratch_shapes=scratch(c_shape(0), *level_scratch(0), c_shape(1), *level_scratch(1))
        + [pltpu.SemaphoreType.DMA((6,))],
        name="open",
    )(log_field, source_field, above, below)

    deep_scratch = [c_shape(2), *level_scratch(2), c_shape(3), *level_scratch(3), c_shape(4), *level_scratch(4)]
    message, a2, a3, a4, v0, b1, v1 = pl.pallas_call(
        functools.partial(middle_kernel, peers),
        out_shape=[shape(2 * TILES[2], OWN[2], LANES)] + [shape(*s) for s in deep_state + [state[1], state[4], state[5]]],
        in_specs=[VMEM] * 5 + [ANY] * 6,
        out_specs=[VMEM] + [ANY] * 6,
        scratch_shapes=scratch(*level_scratch(0), *level_scratch(1), *deep_scratch) + [pltpu.SemaphoreType.DMA((12,))],
        name="middle",
    )(*gathered(message), a0, b0, v0, a1, b1, v1)

    deep_scratch = [*level_scratch(2), *level_scratch(3), *level_scratch(4)]
    half = shape(rows, columns // 2)
    correction, mine, other = pl.pallas_call(
        close_kernel,
        out_shape=(shape(rows, columns), half, half),
        in_specs=[VMEM] * 5 + [ANY] * 9,
        out_specs=(VMEM,) * 3,
        scratch_shapes=scratch(*level_scratch(0), *level_scratch(1), *deep_scratch) + [pltpu.SemaphoreType.DMA((9,))],
        name="close",
    )(*gathered(message), a0, b0, v0, a1, b1, v1, a2, a3, a4)

    theirs = lax.ppermute(other, "samp", [(0, 1), (1, 0)])
    samples = lax.axis_size("samp")
    level_mean = (mine + theirs) / samples
    squares = mine * mine + theirs * theirs
    level_var = (squares - samples * level_mean * level_mean) / (samples - 1)
    return (correction[None], level_mean, level_var)


def solution(mesh):
    in_specs = (P("samp", "grid", None), P("samp", "grid", None))
    out_specs = (P("samp", "grid", None), P("grid", "samp"), P("grid", "samp"))
    return jax.shard_map(local, mesh=mesh, in_specs=in_specs, out_specs=out_specs, check_vma=False)
```

time: 1380 us -> 133 us (0.10)
  the two profiles are of different devices: /device:TPU:97 before, /device:TPU:67 now
where the time goes in v1:
time: 133 us; the launch traced here: 132 us
  Pallas kernels  62.2 us (47%)
  starting transfers between devices  42.2 us (32%)
  waiting for transfers between devices  23 us (17%)
  local copies, waits for them, and re-layouts  2.04 us (2%)
  other arithmetic  1.81 us (1%)
    ppermute x10, starting transfers between devices, shifted(): return lax.ppermute(value, 'grid', pairs)  36.6 us
    pallas_call x1, Pallas kernels, local(): pl.pallas_call(functools.partial(middle_kernel, peers), out_shape=[shape(...  27.7 us
    ppermute x10, waiting for transfers between devices, shifted(): return lax.ppermute(value, 'grid', pairs)  21.7 us
    pallas_call x1, Pallas kernels, local(): pl.pallas_call(close_kernel, out_shape=(shape(rows, columns), half, half)...  18.4 us
    pallas_call x1, Pallas kernels, local(): pl.pallas_call(functools.partial(open_kernel, peers), out_shape=[shape(3...  14 us
    ppermute x1, starting transfers between devices, local(): theirs = lax.ppermute(other, 'samp', [(0, 1), (1, 0)])  5.59 us
  transfers between devices with their start and end apart: 11, of which 6 were waited for; matrix products, arithmetic and copies ran while one was open for 0% of the time, Pallas kernels for 0%

profile of v1, /device:TPU:67, one launch (start us, length us, event | category | flops | bytes accessed | tf_op | source)
XLA Modules:
  0.0 132.1 jit_solution(9283353448268918467)
XLA Ops:
  0.6 2.1 %pack.1 = (f32[48,2048]{1,0:T(8,128)}, f32[48,2048]{1,0:T(8,128)}) custom-call(f32[64,2048]{1,0:T(8,128)} %bitcast.3, f32[64,2048]{1,0:T(8,128)} %bitcast.5), custom_call_target="tpu_custom_call" | custom-call | tf_op jit(solution)/shard_map/pack/pallas_call | solution.py:480
  2.7 3.1 %collective-permute-start = (f32[48,2048]{1,0:T(8,128)}, f32[48,2048]{1,0:T(8,128)S(1)}, u32[]{:S(2)}, u32[]{:S(2)}) collective-permute-start(f32[48,2048]{1,0:T(8,128)} %get-tuple-element.22), channel_id=1, source_target_pairs={{0,1},{1,2},{2,3},{3,4},{4,5},{5,6},{6,7},{7,8},{8,9},{9,10},{10,1... | collective-permute-start | bytes 1179656 | tf_op jit(solution)/shard_map/ppermute | solution.py:468
  5.8 2.2 %collective-permute-start.1 = (f32[48,2048]{1,0:T(8,128)}, f32[48,2048]{1,0:T(8,128)S(1)}, u32[]{:S(2)}, u32[]{:S(2)}) collective-permute-start(f32[48,2048]{1,0:T(8,128)} %get-tuple-element.23), channel_id=1, source_target_pairs={{1,0},{2,1},{3,2},{4,3},{5,4},{6,5},{7,6},{8,7},{9,8},{10,9},{11,1... | collective-permute-start | bytes 1179656 | tf_op jit(solution)/shard_map/ppermute | solution.py:468
  8.0 6.8 %collective-permute-done.above_ref = f32[48,2048]{1,0:T(8,128)S(1)} collective-permute-done((f32[48,2048]{1,0:T(8,128)}, f32[48,2048]{1,0:T(8,128)S(1)}, u32[]{:S(2)}, u32[]{:S(2)}) %collective-permute-start) | collective-permute-done | bytes 393248 | tf_op jit(solution)/shard_map/ppermute | solution.py:468
  14.8 0.0 copy-start
  14.8 2.8 %collective-permute-done.1.below_ref = f32[48,2048]{1,0:T(8,128)S(1)} collective-permute-done((f32[48,2048]{1,0:T(8,128)}, f32[48,2048]{1,0:T(8,128)S(1)}, u32[]{:S(2)}, u32[]{:S(2)}) %collective-permute-start.1) | collective-permute-done | bytes 393248 | tf_op jit(solution)/shard_map/ppermute | solution.py:468
  17.7 0.0 copy-done
  17.7 0.0 copy-start.1
  17.7 0.8 copy-done.1
  18.4 14.0 %open.1 = (f32[12,16,128]{2,1,0:T(8,128)}, f32[6,16,112,128]{3,2,1,0:T(8,128)}, f32[16,128,128]{2,1,0:T(8,128)}, f32[16,128,128]{2,1,0:T(8,128)}, f32[6,8,56,128...) custom-call(f32[64,2048]{1,0:T(8,128)} %bitcast.4, f32[64,2048]{1,0:T(8,128)} %bitcast.6, ...), custom_call_target="tpu_custom_call" | custom-call | tf_op jit(solution)/shard_map/open/pallas_call | solution.py:487
  32.4 10.0 %collective-permute-start.5 = (f32[12,16,128]{2,1,0:T(8,128)}, f32[12,16,128]{2,1,0:T(8,128)S(1)}, u32[]{:S(2)}, u32[]{:S(2)}) collective-permute-start(f32[12,16,128]{2,1,0:T(8,128)} %get-tuple-element.24.m2), channel_id=1, source_target_pairs={{2,0},{3,1},{4,2},{5,3},{6,4},{7,5},{8,6},{9,7},{10,8},{11,9},{12,... | collective-permute-start | bytes 294920 | tf_op jit(solution)/shard_map/ppermute | solution.py:468
  42.4 1.9 %collective-permute-start.4 = (f32[12,16,128]{2,1,0:T(8,128)}, f32[12,16,128]{2,1,0:T(8,128)S(1)}, u32[]{:S(2)}, u32[]{:S(2)}) collective-permute-start(f32[12,16,128]{2,1,0:T(8,128)} %get-tuple-element.24.m2), channel_id=1, source_target_pairs={{1,0},{2,1},{3,2},{4,3},{5,4},{6,5},{7,6},{8,7},{9,8},{10,9},{11,1... | collective-permute-start | bytes 294920 | tf_op jit(solution)/shard_map/ppermute | solution.py:468
  44.3 3.4 %collective-permute-start.3 = (f32[12,16,128]{2,1,0:T(8,128)}, f32[12,16,128]{2,1,0:T(8,128)S(1)}, u32[]{:S(2)}, u32[]{:S(2)}) collective-permute-start(f32[12,16,128]{2,1,0:T(8,128)} %get-tuple-element.24.m2), channel_id=1, source_target_pairs={{0,1},{1,2},{2,3},{3,4},{4,5},{5,6},{6,7},{7,8},{8,9},{9,10},{10,1... | collective-permute-start | bytes 294920 | tf_op jit(solution)/shard_map/ppermute | solution.py:468
  47.7 1.9 %collective-permute-start.2 = (f32[12,16,128]{2,1,0:T(8,128)}, f32[12,16,128]{2,1,0:T(8,128)S(1)}, u32[]{:S(2)}, u32[]{:S(2)}) collective-permute-start(f32[12,16,128]{2,1,0:T(8,128)} %get-tuple-element.24.m2), channel_id=1, source_target_pairs={{0,2},{1,3},{2,4},{3,5},{4,6},{5,7},{6,8},{7,9},{8,10},{9,11},{10,... | collective-permute-start | bytes 294920 | tf_op jit(solution)/shard_map/ppermute | solution.py:468
  49.6 0.0 collective-permute-done.5.m4
  49.6 0.0 copy-start.2
  49.7 0.0 collective-permute-done.4.m3
  49.7 0.0 copy-start.3
  49.7 0.5 collective-permute-done.3.m1
  50.2 0.0 copy-start.4
  50.2 7.6 %collective-permute-done.2.m0 = f32[12,16,128]{2,1,0:T(8,128)S(1)} collective-permute-done((f32[12,16,128]{2,1,0:T(8,128)}, f32[12,16,128]{2,1,0:T(8,128)S(1)}, u32[]{:S(2)}, u32[]{:S(2)}) %collective-permute-start.2) | collective-permute-done | bytes 98336 | tf_op jit(solution)/shard_map/ppermute | solution.py:468
  57.8 0.0 copy-start.5
  57.8 0.0 copy-done.2
  57.8 0.0 copy-done.3
  57.8 0.0 copy-done.4
  57.8 0.6 copy-done.5
  58.4 27.7 %middle.1 = (f32[8,16,128]{2,1,0:T(8,128)}, f32[6,4,80,128]{3,2,1,0:T(8,128)}, f32[6,2,40,128]{3,2,1,0:T(8,128)}, f32[6,1,24,128]{3,2,1,0:T(8,128)}, f32[16,128,...) custom-call(f32[12,16,128]{2,1,0:T(8,128)} %copy-done.5, f32[12,16,128]{2,1,0:T(8,128)} %copy-done.4, ...), custom_call_target="tpu_custom_call" | custom-call | tf_op jit(solution)/shard_map/middle/pallas_call | solution.py:498
  86.2 3.1 %collective-permute-start.9 = (f32[8,16,128]{2,1,0:T(8,128)}, f32[8,16,128]{2,1,0:T(8,128)S(1)}, u32[]{:S(2)}, u32[]{:S(2)}) collective-permute-start(f32[8,16,128]{2,1,0:T(8,128)} %get-tuple-element.31.m2), channel_id=1, source_target_pairs={{2,0},{3,1},{4,2},{5,3},{6,4},{7,5},{8,6},{9,7},{10,8},{11,9},{12,... | collective-permute-start | bytes 196616 | tf_op jit(solution)/shard_map/ppermute | solution.py:468
  89.3 1.9 %collective-permute-start.8 = (f32[8,16,128]{2,1,0:T(8,128)}, f32[8,16,128]{2,1,0:T(8,128)S(1)}, u32[]{:S(2)}, u32[]{:S(2)}) collective-permute-start(f32[8,16,128]{2,1,0:T(8,128)} %get-tuple-element.31.m2), channel_id=1, source_target_pairs={{1,0},{2,1},{3,2},{4,3},{5,4},{6,5},{7,6},{8,7},{9,8},{10,9},{11,1... | collective-permute-start | bytes 196616 | tf_op jit(solution)/shard_map/ppermute | solution.py:468
  91.2 3.4 %collective-permute-start.7 = (f32[8,16,128]{2,1,0:T(8,128)}, f32[8,16,128]{2,1,0:T(8,128)S(1)}, u32[]{:S(2)}, u32[]{:S(2)}) collective-permute-start(f32[8,16,128]{2,1,0:T(8,128)} %get-tuple-element.31.m2), channel_id=1, source_target_pairs={{0,1},{1,2},{2,3},{3,4},{4,5},{5,6},{6,7},{7,8},{8,9},{9,10},{10,1... | collective-permute-start | bytes 196616 | tf_op jit(solution)/shard_map/ppermute | solution.py:468
  94.6 5.8 %collective-permute-start.6 = (f32[8,16,128]{2,1,0:T(8,128)}, f32[8,16,128]{2,1,0:T(8,128)S(1)}, u32[]{:S(2)}, u32[]{:S(2)}) collective-permute-start(f32[8,16,128]{2,1,0:T(8,128)} %get-tuple-element.31.m2), channel_id=1, source_target_pairs={{0,2},{1,3},{2,4},{3,5},{4,6},{5,7},{6,8},{7,9},{8,10},{9,11},{10,... | collective-permute-start | bytes 196616 | tf_op jit(solution)/shard_map/ppermute | solution.py:468
  100.4 0.0 collective-permute-done.9.m4
  100.4 0.0 copy-start.6
  100.4 0.0 collective-permute-done.8.m3
  100.4 0.0 copy-start.7
  100.4 0.0 collective-permute-done.7.m1
  100.4 0.0 copy-start.8
  100.4 3.9 %collective-permute-done.6.m0 = f32[8,16,128]{2,1,0:T(8,128)S(1)} collective-permute-done((f32[8,16,128]{2,1,0:T(8,128)}, f32[8,16,128]{2,1,0:T(8,128)S(1)}, u32[]{:S(2)}, u32[]{:S(2)}) %collective-permute-start.6) | collective-permute-done | bytes 65568 | tf_op jit(solution)/shard_map/ppermute | solution.py:468
  104.3 0.0 copy-start.9
  104.3 0.0 copy-done.6
  104.3 0.0 copy-done.7
  104.3 0.0 copy-done.8
  104.3 0.6 copy-done.9
  104.9 18.4 %close.1 = (f32[64,2048]{1,0:T(8,128)}, f32[64,1024]{1,0:T(8,128)}, f32[64,1024]{1,0:T(8,128)}) custom-call(f32[8,16,128]{2,1,0:T(8,128)} %copy-done.9, f32[8,16,128]{2,1,0:T(8,128)} %copy-done.8, f32[8,16,128]{2,1,0:T(8,128)} %get-tuple-element.31.m2, f32[8,16,128]{2,1,0:T(8,128)} %copy-done.7, f32[8,16,128]{2,1,0:T(8,128)} %copy-done.6, ...), custom_call_target="tpu_custom_call" | custom-call | tf_op jit(solution)/shard_map/close/pallas_call | solution.py:509
  123.4 5.6 %collective-permute-start.10 = (f32[64,1024]{1,0:T(8,128)}, f32[64,1024]{1,0:T(8,128)S(1)}, u32[]{:S(2)}, u32[]{:S(2)}) collective-permute-start(f32[64,1024]{1,0:T(8,128)} %get-tuple-element.40), channel_id=1, source_target_pairs={{0,64},{64,0},{1,65},{65,1},{2,66},{66,2},{3,67},{67,3},{4,68},{68... | collective-permute-start | bytes 786440 | tf_op jit(solution)/shard_map/ppermute | solution.py:518
  129.0 1.4 %collective-permute-done.10 = f32[64,1024]{1,0:T(8,128)S(1)} collective-permute-done((f32[64,1024]{1,0:T(8,128)}, f32[64,1024]{1,0:T(8,128)S(1)}, u32[]{:S(2)}, u32[]{:S(2)}) %collective-permute-start.10) | collective-permute-done | bytes 262176 | tf_op jit(solution)/shard_map/ppermute | solution.py:518
  130.3 1.8 %multiply_subtract_fusion = (f32[64,1024]{1,0:T(8,128)}, f32[64,1024]{1,0:T(8,128)}) fusion(f32[64,1024]{1,0:T(8,128)S(1)} %collective-permute-done.10, f32[64,1024]{1,0:T(8,128)} %get-tuple-element.39), kind=kLoop, calls=%fused_computation | loop fusion | flops 458752 | bytes 1048576 | tf_op jit(solution)/shard_map/sub | solution.py:522
Async XLA Ops:
  2.7 12.1 %collective-permute-start = (f32[48,2048]{1,0:T(8,128)}, f32[48,2048]{1,0:T(8,128)S(1)}, u32[]{:S(2)}, u32[]{:S(2)}) collective-permute-start(f32[48,2048]{1,0:T(8,128)} %get-tuple-element.22), channel_id=1, source_target_pairs={{0,1},{1,2},{2,3},{3,4},{4,5},{5,6},{6,7},{7,8},{8,9},{9,10},{10,1... | collective-permute-start | bytes 1179656 | tf_op jit(solution)/shard_map/ppermute | solution.py:468
  5.8 11.8 %collective-permute-start.1 = (f32[48,2048]{1,0:T(8,128)}, f32[48,2048]{1,0:T(8,128)S(1)}, u32[]{:S(2)}, u32[]{:S(2)}) collective-permute-start(f32[48,2048]{1,0:T(8,128)} %get-tuple-element.23), channel_id=1, source_target_pairs={{1,0},{2,1},{3,2},{4,3},{5,4},{6,5},{7,6},{8,7},{9,8},{10,9},{11,1... | collective-permute-start | bytes 1179656 | tf_op jit(solution)/shard_map/ppermute | solution.py:468
  14.8 2.8 %copy-start = (f32[48,2048]{1,0:T(8,128)}, f32[48,2048]{1,0:T(8,128)S(1)}, u32[]{:S(2)}) copy-start(f32[48,2048]{1,0:T(8,128)S(1)} %collective-permute-done.above_ref) | copy-start | bytes 1179652
  17.7 0.8 copy-start.1
  32.4 17.2 %collective-permute-start.5 = (f32[12,16,128]{2,1,0:T(8,128)}, f32[12,16,128]{2,1,0:T(8,128)S(1)}, u32[]{:S(2)}, u32[]{:S(2)}) collective-permute-start(f32[12,16,128]{2,1,0:T(8,128)} %get-tuple-element.24.m2), channel_id=1, source_target_pairs={{2,0},{3,1},{4,2},{5,3},{6,4},{7,5},{8,6},{9,7},{10,8},{11,9},{12,... | collective-permute-start | bytes 294920 | tf_op jit(solution)/shard_map/ppermute | solution.py:468
  42.4 7.2 %collective-permute-start.4 = (f32[12,16,128]{2,1,0:T(8,128)}, f32[12,16,128]{2,1,0:T(8,128)S(1)}, u32[]{:S(2)}, u32[]{:S(2)}) collective-permute-start(f32[12,16,128]{2,1,0:T(8,128)} %get-tuple-element.24.m2), channel_id=1, source_target_pairs={{1,0},{2,1},{3,2},{4,3},{5,4},{6,5},{7,6},{8,7},{9,8},{10,9},{11,1... | collective-permute-start | bytes 294920 | tf_op jit(solution)/shard_map/ppermute | solution.py:468
  44.3 5.9 %collective-permute-start.3 = (f32[12,16,128]{2,1,0:T(8,128)}, f32[12,16,128]{2,1,0:T(8,128)S(1)}, u32[]{:S(2)}, u32[]{:S(2)}) collective-permute-start(f32[12,16,128]{2,1,0:T(8,128)} %get-tuple-element.24.m2), channel_id=1, source_target_pairs={{0,1},{1,2},{2,3},{3,4},{4,5},{5,6},{6,7},{7,8},{8,9},{9,10},{10,1... | collective-permute-start | bytes 294920 | tf_op jit(solution)/shard_map/ppermute | solution.py:468
  47.7 10.1 %collective-permute-start.2 = (f32[12,16,128]{2,1,0:T(8,128)}, f32[12,16,128]{2,1,0:T(8,128)S(1)}, u32[]{:S(2)}, u32[]{:S(2)}) collective-permute-start(f32[12,16,128]{2,1,0:T(8,128)} %get-tuple-element.24.m2), channel_id=1, source_target_pairs={{0,2},{1,3},{2,4},{3,5},{4,6},{5,7},{6,8},{7,9},{8,10},{9,11},{10,... | collective-permute-start | bytes 294920 | tf_op jit(solution)/shard_map/ppermute | solution.py:468
  49.6 8.2 %copy-start.2 = (f32[12,16,128]{2,1,0:T(8,128)}, f32[12,16,128]{2,1,0:T(8,128)S(1)}, u32[]{:S(2)}) copy-start(f32[12,16,128]{2,1,0:T(8,128)S(1)} %collective-permute-done.5.m4) | copy-start | bytes 294916
  49.7 8.1 %copy-start.3 = (f32[12,16,128]{2,1,0:T(8,128)}, f32[12,16,128]{2,1,0:T(8,128)S(1)}, u32[]{:S(2)}) copy-start(f32[12,16,128]{2,1,0:T(8,128)S(1)} %collective-permute-done.4.m3) | copy-start | bytes 294916
  50.2 7.6 %copy-start.4 = (f32[12,16,128]{2,1,0:T(8,128)}, f32[12,16,128]{2,1,0:T(8,128)S(1)}, u32[]{:S(2)}) copy-start(f32[12,16,128]{2,1,0:T(8,128)S(1)} %collective-permute-done.3.m1) | copy-start | bytes 294916
  57.8 0.6 copy-start.5
  86.2 14.2 %collective-permute-start.9 = (f32[8,16,128]{2,1,0:T(8,128)}, f32[8,16,128]{2,1,0:T(8,128)S(1)}, u32[]{:S(2)}, u32[]{:S(2)}) collective-permute-start(f32[8,16,128]{2,1,0:T(8,128)} %get-tuple-element.31.m2), channel_id=1, source_target_pairs={{2,0},{3,1},{4,2},{5,3},{6,4},{7,5},{8,6},{9,7},{10,8},{11,9},{12,... | collective-permute-start | bytes 196616 | tf_op jit(solution)/shard_map/ppermute | solution.py:468
  89.3 11.1 %collective-permute-start.8 = (f32[8,16,128]{2,1,0:T(8,128)}, f32[8,16,128]{2,1,0:T(8,128)S(1)}, u32[]{:S(2)}, u32[]{:S(2)}) collective-permute-start(f32[8,16,128]{2,1,0:T(8,128)} %get-tuple-element.31.m2), channel_id=1, source_target_pairs={{1,0},{2,1},{3,2},{4,3},{5,4},{6,5},{7,6},{8,7},{9,8},{10,9},{11,1... | collective-permute-start | bytes 196616 | tf_op jit(solution)/shard_map/ppermute | solution.py:468
  91.2 9.2 %collective-permute-start.7 = (f32[8,16,128]{2,1,0:T(8,128)}, f32[8,16,128]{2,1,0:T(8,128)S(1)}, u32[]{:S(2)}, u32[]{:S(2)}) collective-permute-start(f32[8,16,128]{2,1,0:T(8,128)} %get-tuple-element.31.m2), channel_id=1, source_target_pairs={{0,1},{1,2},{2,3},{3,4},{4,5},{5,6},{6,7},{7,8},{8,9},{9,10},{10,1... | collective-permute-start | bytes 196616 | tf_op jit(solution)/shard_map/ppermute | solution.py:468
  94.6 9.7 %collective-permute-start.6 = (f32[8,16,128]{2,1,0:T(8,128)}, f32[8,16,128]{2,1,0:T(8,128)S(1)}, u32[]{:S(2)}, u32[]{:S(2)}) collective-permute-start(f32[8,16,128]{2,1,0:T(8,128)} %get-tuple-element.31.m2), channel_id=1, source_target_pairs={{0,2},{1,3},{2,4},{3,5},{4,6},{5,7},{6,8},{7,9},{8,10},{9,11},{10,... | collective-permute-start | bytes 196616 | tf_op jit(solution)/shard_map/ppermute | solution.py:468
  100.4 4.0 %copy-start.6 = (f32[8,16,128]{2,1,0:T(8,128)}, f32[8,16,128]{2,1,0:T(8,128)S(1)}, u32[]{:S(2)}) copy-start(f32[8,16,128]{2,1,0:T(8,128)S(1)} %collective-permute-done.9.m4) | copy-start | bytes 196612
  100.4 3.9 %copy-start.7 = (f32[8,16,128]{2,1,0:T(8,128)}, f32[8,16,128]{2,1,0:T(8,128)S(1)}, u32[]{:S(2)}) copy-start(f32[8,16,128]{2,1,0:T(8,128)S(1)} %collective-permute-done.8.m3) | copy-start | bytes 196612
  100.4 3.9 %copy-start.8 = (f32[8,16,128]{2,1,0:T(8,128)}, f32[8,16,128]{2,1,0:T(8,128)S(1)}, u32[]{:S(2)}) copy-start(f32[8,16,128]{2,1,0:T(8,128)S(1)} %collective-permute-done.7.m1) | copy-start | bytes 196612
  104.3 0.6 copy-start.9
  123.4 7.0 %collective-permute-start.10 = (f32[64,1024]{1,0:T(8,128)}, f32[64,1024]{1,0:T(8,128)S(1)}, u32[]{:S(2)}, u32[]{:S(2)}) collective-permute-start(f32[64,1024]{1,0:T(8,128)} %get-tuple-element.40), channel_id=1, source_target_pairs={{0,64},{64,0},{1,65},{65,1},{2,66},{66,2},{3,67},{67,3},{4,68},{68... | collective-permute-start | bytes 786440 | tf_op jit(solution)/shard_map/ppermute | solution.py:518

commit v2 on v1

v2 whole, which is shorter than its diff:
```python
import functools

import jax
import jax.numpy as jnp
from jax import lax
from jax.experimental import pallas as pl
from jax.experimental.pallas import tpu as pltpu
from jax.sharding import PartitionSpec as P

LANES = 128
PAD = 8
OWN = (64, 32, 16, 8, 4)
HALO = (24, 12, 32, 16, 8)
ROWS = tuple(o + 2 * h for o, h in zip(OWN, HALO))
TILES = (16, 8, 4, 2, 1)
STRIPS = (14, 7, 10, 5, 3)
BUF = tuple(8 * s + 2 * PAD for s in STRIPS)
SOLVES = (1, 2, 2, 2, 2)
UNROLL = (2, 7, 5, 5, 3)
DAMP = 0.8
F32 = jnp.float32


def loop(count, body, unroll=1):
    if unroll >= count:
        for i in range(count):
            body(i)
    else:
        lax.fori_loop(0, count, lambda i, c: (body(i), c)[1], 0, unroll=unroll)


def at(i, offset, step=8):
    if isinstance(i, int):
        return pl.ds(i * step + offset, 8)
    return pl.ds(pl.multiple_of(i * step, step) + offset, 8)


def pairs_at(i, offset):
    base = i * 16 if isinstance(i, int) else pl.multiple_of(i * 16, 16)
    return pl.ds(base + offset, 8, stride=2), pl.ds(base + offset + 1, 8, stride=2)


def iota(dim):
    return lax.broadcasted_iota(jnp.int32, (8, LANES), dim)


def side_values(x):
    return [pltpu.roll(x[-1], 1, 1)] + x[:-1], x[1:] + [pltpu.roll(x[0], LANES - 1, 1)]


def harmonic(a, b):
    return 2.0 * a * b / (a + b)


def make_weights(level, c_ref, a_ref, first_row, total_rows, source_ref=None, b_ref=None):
    tiles = TILES[level]

    def body(i):
        c = [c_ref[t, at(i, PAD), :] for t in range(tiles)]
        row = first_row + i * 8 + iota(0)
        lane = iota(1)
        inside = jnp.logical_and(row >= 0, row < total_rows)
        _, east = side_values(c)
        w_east = [harmonic(a, b) for a, b in zip(c, east)]
        w_west, _ = side_values(w_east)
        w_west[0] = jnp.where(lane == 0, harmonic(c[0], c[0]), w_west[0])
        w_east[-1] = jnp.where(lane == LANES - 1, harmonic(c[-1], c[-1]), w_east[-1])
        for t in range(tiles):
            w_north = harmonic(c[t], jnp.where(row == 0, c[t], c_ref[t, at(i, PAD - 1), :]))
            w_south = harmonic(c[t], jnp.where(row == total_rows - 1, c[t], c_ref[t, at(i, PAD + 1), :]))
            diagonal = w_west[t] + w_east[t] + w_north + w_south
            gain = jnp.where(inside, DAMP / diagonal, 0.0)
            a_west, a_east = gain * w_west[t], gain * w_east[t]
            if t == 0:
                a_west = jnp.where(lane == 0, 0.0, a_west)
            if t == tiles - 1:
                a_east = jnp.where(lane == LANES - 1, 0.0, a_east)
            rows = at(i, 0)
            a_ref[0, t, rows, :] = a_west
            a_ref[1, t, rows, :] = a_east
            a_ref[2, t, rows, :] = gain * w_north
            a_ref[3, t, rows, :] = gain * w_south
            a_ref[4, t, rows, :] = gain
            a_ref[5, t, rows, :] = diagonal * (1.0 / DAMP)
            if source_ref is not None:
                b_ref[t, at(i, PAD), :] = gain * source_ref[t, at(i, PAD), :]

    loop(STRIPS[level], body)


def sweep(level, v_ref, out_ref, b_ref, a_ref, finish):
    tiles, solves = TILES[level], SOLVES[level]

    def body(i):
        v = [[v_ref[s * tiles + t, at(i, PAD), :] for t in range(tiles)] for s in range(solves)]
        sides = [side_values(x) for x in v]
        rows = at(i, 0)
        order = list(range(1, tiles - 1)) + ([0, tiles - 1] if tiles > 1 else [0])
        for t in order:
            a_west, a_east, a_north, a_south = (a_ref[k, t, rows, :] for k in range(4))
            for s in range(solves):
                west, east = sides[s]
                k = s * tiles + t
                north, south = v_ref[k, at(i, PAD - 1), :], v_ref[k, at(i, PAD + 1), :]
                moved = (a_north * north + a_south * south) + b_ref[k, at(i, PAD), :]
                moved += a_west * west[t] + a_east * east[t]
                out_ref[k, at(i, PAD), :] = finish(v[s][t], moved, t, rows)

    loop(STRIPS[level], body, UNROLL[level])


def relax(level, v_ref, out_ref, b_ref, a_ref):
    sweep(level, v_ref, out_ref, b_ref, a_ref, lambda v, moved, t, rows: (1.0 - DAMP) * v + moved)


def residual(level, v_ref, out_ref, b_ref, a_ref):
    sweep(level, v_ref, out_ref, b_ref, a_ref, lambda v, moved, t, rows: a_ref[5, t, rows, :] * (moved - DAMP * v))


def restrict(count, ref, offset, tiles, store, unroll=1):
    def body(j):
        even, odd = pairs_at(j, offset)
        for k in range(0, len(tiles), 2):
            a, b = tiles[k], tiles[k + 1]
            store(j, k // 2, (ref[a, even, :] + ref[a, odd, :]) + (ref[b, even, :] + ref[b, odd, :]))

    loop(count, body, unroll)


def prolong(count, e_ref, offset, e_tiles, v_ref, sign=1.0, v_offset=PAD, unroll=1):
    def body(j):
        halves = pairs_at(j, v_offset)
        for k, tile in enumerate(e_tiles):
            e = sign * e_ref[tile, at(j, offset), :]
            for t in (2 * k, 2 * k + 1):
                for rows in halves:
                    v_ref[t, rows, :] = v_ref[t, rows, :] + e

    loop(count, body, unroll)


def clear_pads(*refs, value=0.0):
    for ref in refs:
        tiles, rows, _ = ref.shape
        ref[:, 0:PAD, :] = jnp.full((tiles, PAD, LANES), value, F32)
        ref[:, rows - PAD : rows, :] = jnp.full((tiles, PAD, LANES), value, F32)


def fill(ref, value):
    def body(i):
        ref[:, at(i, 0), :] = jnp.full((ref.shape[0], 8, LANES), value, F32)

    loop(ref.shape[1] // 8, body)


def take(x, index):
    return jnp.take_along_axis(x, index, axis=1, mode="promise_in_bounds")


def exchange_blocks(x):
    lane = iota(1)
    x = list(x)
    for step in (1, 2, 4, 8):
        upper = lax.rem(lane, 16 * step) >= 8 * step
        for i in range(16):
            if i & step == 0:
                j = i + step
                from_j = pltpu.roll(x[j], 8 * step, 1)
                from_i = pltpu.roll(x[i], LANES - 8 * step, 1)
                x[i], x[j] = jnp.where(upper, from_j, x[i]), jnp.where(upper, x[j], from_i)
    return x


def to_tiles(x):
    lane = iota(1)
    index = lax.rem(lane, 8) * 16 + lax.div(lane, 8)
    return exchange_blocks([take(v, index) for v in x])


def from_tiles(x):
    lane = iota(1)
    index = lax.rem(lane, 16) * 8 + lax.div(lane, 16)
    return [take(v, index) for v in exchange_blocks(x)]


def place():
    return lax.axis_index("grid")


def first_row(level):
    return place() * OWN[level] - HALO[level]


def towards_next():
    i = place()
    return lax.rem(i, 2) == 0, lax.rem(i, 4) < 2


def slab_positions():
    near, far = towards_next()
    return (
        jnp.where(near, 3, 1), jnp.where(near, 1, 3), jnp.where(far, 4, 0), jnp.where(far, 0, 4), 2,
    )


def pack_kernel(log_ref, src_ref, own_ref, first_ref, second_ref):
    halo, own = HALO[0], OWN[0]
    tiles = TILES[0]

    def body(i):
        rows = at(i, 0)
        for field, ref in enumerate((log_ref, src_ref)):
            x = [ref[rows, t * LANES : (t + 1) * LANES] for t in range(tiles)]
            if field == 0:
                x = [jnp.exp(v) for v in x]
            for t, v in enumerate(to_tiles(x)):
                own_ref[field * tiles + t, rows, :] = v

    loop(own // 8, body)
    near, _ = towards_next()
    start = jnp.where(near, own - halo, 0)
    for ref, base in ((first_ref, start), (second_ref, own - halo - start)):
        for i in range(halo // 8):
            from_rows = pl.ds(pl.multiple_of(base + 8 * i, 8), 8)
            for t in range(2 * tiles):
                ref[t, 8 * i : 8 * i + 8, :] = own_ref[t, from_rows, :]


def scaled_store(bp_ref, a_ref, start=0):
    def store(j, k, q):
        bp_ref[start + k, at(j, PAD), :] = a_ref[4, k, at(j, 0), :] * q

    return store


def quarter_store(c_ref):
    def store(j, k, q):
        c_ref[k, at(j, PAD), :] = 0.25 * q

    return store


class Copies:
    def __init__(self, sems):
        self.sems, self.count = sems, 0

    def start(self, *pairs):
        started = []
        for src, dst in pairs:
            copy = pltpu.make_async_copy(src, dst, self.sems.at[self.count])
            copy.start()
            self.count += 1
            started.append(copy)
        return started


def wait(copies):
    for copy in copies:
        copy.wait()


def open_kernel(
    peers, own_ref, first_ref, second_ref,
    msg_ref, a0_out, b0_out, v0_out, a1_out, b1_out, v1_out,
    c0, a0, bp0, va0, vb0, c1, a1, bp1, va1, vb1, sems,
):
    halo, own, tiles = HALO[0], OWN[0], TILES[0]
    copies = Copies(sems)
    near, _ = towards_next()
    first_at = pl.multiple_of(jnp.where(near, PAD + halo + own, PAD), 8)
    second_at = pl.multiple_of(jnp.where(near, PAD, PAD + halo + own), 8)
    loads = []
    for field, ref in enumerate((c0, vb0)):
        chunk = pl.ds(field * tiles, tiles)
        loads += copies.start(
            (own_ref.at[chunk], ref.at[:, PAD + halo : PAD + halo + own, :]),
            (first_ref.at[chunk], ref.at[:, pl.ds(first_at, halo), :]),
            (second_ref.at[chunk], ref.at[:, pl.ds(second_at, halo), :]),
        )
    clear_pads(c0, c1, value=1.0)
    clear_pads(bp0, va0, vb0, bp1, va1, vb1)
    wait(loads)
    make_weights(0, c0, a0, first_row(0), peers * OWN[0], vb0, bp0)
    stores = copies.start((a0, a0_out), (bp0, b0_out))
    restrict(STRIPS[1], c0, PAD, range(tiles), quarter_store(c1))
    make_weights(1, c1, a1, first_row(1), peers * OWN[1])
    stores += copies.start((a1, a1_out))
    restrict(STRIPS[1], vb0, PAD, range(tiles), scaled_store(bp1, a1, TILES[1]))
    relax(0, bp0, va0, bp0, a0)
    stores += copies.start((va0, v0_out))
    residual(0, va0, vb0, bp0, a0)
    restrict(STRIPS[1], vb0, PAD, range(tiles), scaled_store(bp1, a1))
    stores += copies.start((bp1, b1_out))
    relax(1, bp1, va1, bp1, a1)
    stores += copies.start((va1, v1_out))
    residual(1, va1, vb1, bp1, a1)

    def store(j, k, q):
        msg_ref[k, at(j, 0), :] = q

    restrict(OWN[2] // 8, vb1, PAD + HALO[1], range(2 * TILES[1]), store, 2)

    def store_coef(j, k, q):
        msg_ref[2 * TILES[2] + k, at(j, 0), :] = 0.25 * q

    restrict(OWN[2] // 8, c1, PAD + HALO[1], range(TILES[1]), store_coef, 2)
    wait(stores)


def deep_solve(a, bp, va, vb):
    relax(2, bp[2], va[2], bp[2], a[2])
    residual(2, va[2], vb[2], bp[2], a[2])
    for s in range(2):
        restrict(STRIPS[3], vb[2], PAD, range(s * 4, s * 4 + 4), scaled_store(bp[3], a[3], s * 2), 5)
    relax(3, bp[3], va[3], bp[3], a[3])
    residual(3, va[3], vb[3], bp[3], a[3])
    for s in range(2):
        restrict(STRIPS[4], vb[3], PAD, range(s * 2, s * 2 + 2), scaled_store(bp[4], a[4], s), 3)
    relax(4, bp[4], va[4], bp[4], a[4])
    relax(4, va[4], vb[4], bp[4], a[4])
    relax(4, vb[4], va[4], bp[4], a[4])
    prolong(STRIPS[4], va[4], PAD, range(2), va[3], unroll=3)
    relax(3, va[3], vb[3], bp[3], a[3])
    relax(3, vb[3], va[3], bp[3], a[3])
    prolong(STRIPS[3], va[3], PAD, range(4), va[2], unroll=5)
    relax(2, va[2], vb[2], bp[2], a[2])
    relax(2, vb[2], va[2], bp[2], a[2])


def up_level_1(va2, va1, vb1, bp1, a1):
    offset = PAD + HALO[2] - HALO[1] // 2
    prolong(4, va2, offset, range(2 * TILES[2]), va1)
    relax(1, va1, vb1, bp1, a1)
    relax(1, vb1, va1, bp1, a1)


def up_level_0(va1, va0, vb0, bp0, a0):
    prolong(STRIPS[1], va1, PAD, range(TILES[1]), va0)
    relax(0, va0, vb0, bp0, a0)
    relax(0, vb0, va0, bp0, a0)


def assemble(messages, a2, bp2):
    for position, m in zip(slab_positions(), messages):
        for i in range(2):
            row = pl.multiple_of(position * OWN[2] + i * 8, 8)
            for k in range(2 * TILES[2]):
                bp2[k, pl.ds(PAD + row, 8), :] = (
                    a2[4, k % TILES[2], pl.ds(row, 8), :] * m[k, i * 8 : i * 8 + 8, :]
                )


def middle_kernel(
    peers, m0, m1, m2, m3, m4, a0_in, b0_in, v0_in, a1_in, b1_in, v1_in,
    msg_ref, a2_out, a3_out, a4_out, v0_out, b1_out, v1_out,
    a0, bp0, va0, vb0, a1, bp1, va1, vb1,
    c2, a2, bp2, va2, vb2, c3, a3, bp3, va3, vb3, c4, a4, bp4, va4, vb4, sems,
):
    copies = Copies(sems)
    loads = copies.start((a1_in, a1), (b1_in, bp1), (v1_in, va1), (a0_in, a0), (b0_in, bp0), (v0_in, va0))
    messages = (m0, m1, m2, m3, m4)
    fill(c4, 1.0)
    clear_pads(c2, c3, value=1.0)
    for ref in (bp4, va4, vb4):
        fill(ref, 0.0)
    clear_pads(bp2, va2, vb2, bp3, va3, vb3, vb0, vb1)
    top = first_row(2)
    for position, m in zip(slab_positions(), messages):
        for i in range(2):
            row = pl.multiple_of(position * OWN[2] + i * 8, 8)
            for k in range(TILES[2]):
                c2[k, pl.ds(PAD + row, 8), :] = m[2 * TILES[2] + k, i * 8 : i * 8 + 8, :]
    make_weights(2, c2, a2, top, peers * OWN[2])
    restrict(STRIPS[3], c2, PAD, range(4), quarter_store(c3), 5)
    make_weights(3, c3, a3, first_row(3), peers * OWN[3])
    restrict(2, c3, PAD, range(2), quarter_store(c4), 2)

    def last_rows(j, k, q):
        c4[k, PAD + 16 : PAD + 24, :] = jnp.where(iota(0) < ROWS[4] - 16, 0.25 * q, 1.0)

    restrict(1, c3, PAD + 32, range(2), last_rows)
    make_weights(4, c4, a4, first_row(4), peers * OWN[4])
    stores = copies.start((a2, a2_out), (a3, a3_out), (a4, a4_out))
    assemble(messages, a2, bp2)
    a = {2: a2, 3: a3, 4: a4}
    bp = {2: bp2, 3: bp3, 4: bp4}
    va = {2: va2, 3: va3, 4: va4}
    vb = {2: vb2, 3: vb3, 4: vb4}
    deep_solve(a, bp, va, vb)
    wait(loads)
    up_level_1(va2, va1, vb1, bp1, a1)
    up_level_0(va1, va0, vb0, bp0, a0)

    relax(0, va0, vb0, bp0, a0)
    relax(0, vb0, va0, bp0, a0)
    stores += copies.start((va0, v0_out))
    residual(0, va0, vb0, bp0, a0)
    restrict(STRIPS[1], vb0, PAD, range(TILES[0]), scaled_store(bp1, a1))
    stores += copies.start((bp1, b1_out))

    def clear(i):
        va1[0 : TILES[1], at(i, 0), :] = jnp.zeros((TILES[1], 8, LANES), F32)

    loop(BUF[1] // 8, clear)
    relax(1, va1, vb1, bp1, a1)
    relax(1, vb1, va1, bp1, a1)
    stores += copies.start((va1, v1_out))
    residual(1, va1, vb1, bp1, a1)

    def store(j, k, q):
        msg_ref[k, at(j, 0), :] = q

    restrict(OWN[2] // 8, vb1, PAD + HALO[1], range(2 * TILES[1]), store, 2)
    wait(stores)


def close_kernel(
    m0, m1, m2, m3, m4, a0_in, b0_in, v0_in, a1_in, b1_in, v1_in, a2_in, a3_in, a4_in,
    out_ref, mine_ref, other_ref,
    a0, bp0, va0, vb0, a1, bp1, va1, vb1,
    a2, bp2, va2, vb2, a3, bp3, va3, vb3, a4, bp4, va4, vb4, sems,
):
    copies = Copies(sems)
    first = copies.start((a2_in, a2), (a3_in, a3), (a4_in, a4))
    loads = copies.start((a1_in, a1), (b1_in, bp1), (v1_in, va1), (a0_in, a0), (b0_in, bp0), (v0_in, va0))
    for ref in (bp4, va4, vb4):
        fill(ref, 0.0)
    clear_pads(bp2, va2, vb2, bp3, va3, vb3, vb0, vb1)
    wait(first)
    assemble((m0, m1, m2, m3, m4), a2, bp2)
    a = {2: a2, 3: a3, 4: a4}
    bp = {2: bp2, 3: bp3, 4: bp4}
    va = {2: va2, 3: va3, 4: va4}
    vb = {2: vb2, 3: vb3, 4: vb4}
    deep_solve(a, bp, va, vb)
    wait(loads)
    up_level_1(va2, va1, vb1, bp1, a1)
    up_level_0(va1, va0, vb0, bp0, a0)
    prolong(OWN[1] // 8, va1, PAD + HALO[1], range(TILES[1], 2 * TILES[1]), va0, -1.0, PAD + HALO[0])
    tiles = TILES[0]
    left = lax.axis_index("samp") == 0

    def body(i):
        x = from_tiles([va0[t, at(i, PAD + HALO[0]), :] for t in range(tiles)])
        for t in range(tiles):
            out_ref[at(i, 0), t * LANES : (t + 1) * LANES] = x[t]
        for t in range(tiles // 2):
            low, high = x[t], x[tiles // 2 + t]
            mine_ref[at(i, 0), t * LANES : (t + 1) * LANES] = jnp.where(left, low, high)
            other_ref[at(i, 0), t * LANES : (t + 1) * LANES] = jnp.where(left, high, low)

    loop(OWN[0] // 8, body)


VMEM = pl.BlockSpec(memory_space=pltpu.VMEM)
ANY = pl.BlockSpec(memory_space=pl.ANY)


def shape(*dims):
    return jax.ShapeDtypeStruct(dims, F32)


def a_shape(level):
    return (6, TILES[level], 8 * STRIPS[level], LANES)


def v_shape(level):
    return (SOLVES[level] * TILES[level], BUF[level], LANES)


def c_shape(level):
    return (TILES[level], BUF[level], LANES)


def scratch(*shapes):
    return [pltpu.VMEM(s, F32) for s in shapes]


def level_scratch(level):
    return [a_shape(level)] + [v_shape(level)] * 3


def swaps(distance):
    peers = lax.axis_size("grid")
    even = [(i, i + distance if i % (2 * distance) < distance else i - distance) for i in range(peers)]
    odd = [((a + distance) % peers, (b + distance) % peers) for a, b in even]
    return even, odd


def gathered(value):
    return [lax.ppermute(value, "grid", pairs) for distance in (1, 2) for pairs in swaps(distance)] + [value]


def local(log_coef, source):
    peers = lax.axis_size("grid")
    log_field, source_field = log_coef[0], source[0]
    rows, columns = source_field.shape
    edge = shape(2 * TILES[0], HALO[0], LANES)
    own, first, second = pl.pallas_call(
        pack_kernel,
        out_shape=(shape(2 * TILES[0], OWN[0], LANES), edge, edge),
        in_specs=[VMEM] * 2,
        out_specs=(VMEM,) * 3,
        name="pack",
    )(log_field, source_field)
    even, odd = swaps(1)
    first, second = lax.ppermute(first, "grid", even), lax.ppermute(second, "grid", odd)

    state = [a_shape(0), v_shape(0), v_shape(0), a_shape(1), v_shape(1), v_shape(1)]
    deep_state = [a_shape(2), a_shape(3), a_shape(4)]
    message, a0, b0, v0, a1, b1, v1 = pl.pallas_call(
        functools.partial(open_kernel, peers),
        out_shape=[shape(3 * TILES[2], OWN[2], LANES)] + [shape(*s) for s in state],
        in_specs=[ANY] * 3,
        out_specs=[VMEM] + [ANY] * 6,
        scratch_shapes=scratch(c_shape(0), *level_scratch(0), c_shape(1), *level_scratch(1))
        + [pltpu.SemaphoreType.DMA((12,))],
        name="open",
    )(own, first, second)

    deep_scratch = [c_shape(2), *level_scratch(2), c_shape(3), *level_scratch(3), c_shape(4), *level_scratch(4)]
    message, a2, a3, a4, v0, b1, v1 = pl.pallas_call(
        functools.partial(middle_kernel, peers),
        out_shape=[shape(2 * TILES[2], OWN[2], LANES)] + [shape(*s) for s in deep_state + [state[1], state[4], state[5]]],
        in_specs=[VMEM] * 5 + [ANY] * 6,
        out_specs=[VMEM] + [ANY] * 6,
        scratch_shapes=scratch(*level_scratch(0), *level_scratch(1), *deep_scratch) + [pltpu.SemaphoreType.DMA((12,))],
        name="middle",
    )(*gathered(message), a0, b0, v0, a1, b1, v1)

    deep_scratch = [*level_scratch(2), *level_scratch(3), *level_scratch(4)]
    half = shape(rows, columns // 2)
    correction, mine, other = pl.pallas_call(
        close_kernel,
        out_shape=(shape(rows, columns), half, half),
        in_specs=[VMEM] * 5 + [ANY] * 9,
        out_specs=(VMEM,) * 3,
        scratch_shapes=scratch(*level_scratch(0), *level_scratch(1), *deep_scratch) + [pltpu.SemaphoreType.DMA((9,))],
        name="close",
    )(*gathered(message), a0, b0, v0, a1, b1, v1, a2, a3, a4)

    theirs = lax.ppermute(other, "samp", [(0, 1), (1, 0)])
    samples = lax.axis_size("samp")
    level_mean = (mine + theirs) / samples
    squares = mine * mine + theirs * theirs
    level_var = (squares - samples * level_mean * level_mean) / (samples - 1)
    return (correction[None], level_mean, level_var)


def solution(mesh):
    in_specs = (P("samp", "grid", None), P("samp", "grid", None))
    out_specs = (P("samp", "grid", None), P("grid", "samp"), P("grid", "samp"))
    return jax.shard_map(local, mesh=mesh, in_specs=in_specs, out_specs=out_specs, check_vma=False)
```

time: 133 us -> 92.5 us (0.70)
  the two profiles are of different devices: /device:TPU:67 before, /device:TPU:1 now
where the time goes in v2:
time: 92.5 us; the launch traced here: 92.3 us
  Pallas kernels  36.2 us (39%)
  starting transfers between devices  29.7 us (32%)
  waiting for transfers between devices  21.7 us (23%)
  local copies, waits for them, and re-layouts  2.06 us (2%)
  other arithmetic  1.81 us (2%)
    ppermute x8, starting transfers between devices, gathered(): lax.ppermute(value, 'grid', pairs)  14.8 us
    ppermute x8, waiting for transfers between devices, gathered(): lax.ppermute(value, 'grid', pairs)  11.6 us
    pallas_call x1, Pallas kernels, local(): pl.pallas_call(close_kernel, out_shape=(shape(rows, columns), half, half)...  11 us
    pallas_call x1, Pallas kernels, local(): pl.pallas_call(functools.partial(middle_kernel, peers), out_shape=[shape(...  10.9 us
    pallas_call x1, Pallas kernels, local(): pl.pallas_call(functools.partial(open_kernel, peers), out_shape=[shape(3...  8.19 us
    ppermute x1, waiting for transfers between devices, local(): lax.ppermute(second, 'grid', odd)  7.88 us
    ppermute x1, starting transfers between devices, local(): lax.ppermute(second, 'grid', odd)  7.74 us
    pallas_call x1, Pallas kernels, local(): pl.pallas_call(pack_kernel, out_shape=(shape(2 * TILES[0], OWN[0], LANES)...  6.11 us
  transfers between devices with their start and end apart: 11, of which 7 were waited for; matrix products, arithmetic and copies ran while one was open for 0% of the time, Pallas kernels for 0%

profile of v2, /device:TPU:1, one launch (start us, length us, event | category | flops | bytes accessed | tf_op | source)
XLA Modules:
  0.0 92.3 jit_solution(7736785516964190174)
XLA Ops:
  0.6 6.1 %pack.1 = (f32[32,64,128]{2,1,0:T(8,128)}, f32[32,24,128]{2,1,0:T(8,128)}, f32[32,24,128]{2,1,0:T(8,128)}) custom-call(f32[64,2048]{1,0:T(8,128)} %bitcast.3, f32[64,2048]{1,0:T(8,128)} %bitcast.4), custom_call_target="tpu_custom_call" | custom-call | tf_op jit(solution)/shard_map/pack/pallas_call | solution.py:499
  6.7 2.0 %collective-permute-start = (f32[32,24,128]{2,1,0:T(8,128)}, f32[32,24,128]{2,1,0:T(8,128)S(1)}, u32[]{:S(2)}, u32[]{:S(2)}) collective-permute-start(f32[32,24,128]{2,1,0:T(8,128)} %get-tuple-element.24), channel_id=1, source_target_pairs={{0,1},{1,0},{2,3},{3,2},{4,5},{5,4},{6,7},{7,6},{8,9},{9,8},{10,11... | collective-permute-start | bytes 1179656 | tf_op jit(solution)/shard_map/ppermute | solution.py:507
  8.8 7.7 %collective-permute-start.1 = (f32[32,24,128]{2,1,0:T(8,128)}, f32[32,24,128]{2,1,0:T(8,128)S(1)}, u32[]{:S(2)}, u32[]{:S(2)}) collective-permute-start(f32[32,24,128]{2,1,0:T(8,128)} %get-tuple-element.25), channel_id=1, source_target_pairs={{1,2},{2,1},{3,4},{4,3},{5,6},{6,5},{7,8},{8,7},{9,10},{10,9},{11,... | collective-permute-start | bytes 1179656 | tf_op jit(solution)/shard_map/ppermute | solution.py:507
  16.5 0.9 collective-permute-done.first_ref
  17.4 0.0 copy-start
  17.4 7.9 %collective-permute-done.1.second_ref = f32[32,24,128]{2,1,0:T(8,128)S(1)} collective-permute-done((f32[32,24,128]{2,1,0:T(8,128)}, f32[32,24,128]{2,1,0:T(8,128)S(1)}, u32[]{:S(2)}, u32[]{:S(2)}) %collective-permute-start.1) | collective-permute-done | bytes 393248 | tf_op jit(solution)/shard_map/ppermute | solution.py:507
  25.3 0.0 copy-start.1
  25.3 0.0 copy-done
  25.3 0.8 copy-done.1
  26.0 8.2 %open.1 = (f32[12,16,128]{2,1,0:T(8,128)}, f32[6,16,112,128]{3,2,1,0:T(8,128)}, f32[16,128,128]{2,1,0:T(8,128)}, f32[16,128,128]{2,1,0:T(8,128)}, f32[6,8,56,128...) custom-call(f32[32,64,128]{2,1,0:T(8,128)} %get-tuple-element.23.own_ref, f32[32,24,128]{2,1,0:T(8,128)} %copy-done, ...), custom_call_target="tpu_custom_call" | custom-call | tf_op jit(solution)/shard_map/open/pallas_call | solution.py:511
  34.2 1.9 %collective-permute-start.5 = (f32[12,16,128]{2,1,0:T(8,128)}, f32[12,16,128]{2,1,0:T(8,128)S(1)}, u32[]{:S(2)}, u32[]{:S(2)}) collective-permute-start(f32[12,16,128]{2,1,0:T(8,128)} %get-tuple-element.26.m4), channel_id=1, source_target_pairs={{2,4},{3,5},{4,2},{5,3},{6,8},{7,9},{8,6},{9,7},{10,12},{11,13},{1... | collective-permute-start | bytes 294920 | tf_op jit(solution)/shard_map/ppermute | solution.py:491
  36.1 0.0 collective-permute-start.4
  36.1 5.0 %collective-permute-start.3 = (f32[12,16,128]{2,1,0:T(8,128)}, f32[12,16,128]{2,1,0:T(8,128)S(1)}, u32[]{:S(2)}, u32[]{:S(2)}) collective-permute-start(f32[12,16,128]{2,1,0:T(8,128)} %get-tuple-element.26.m4), channel_id=1, source_target_pairs={{1,2},{2,1},{3,4},{4,3},{5,6},{6,5},{7,8},{8,7},{9,10},{10,9},{11,... | collective-permute-start | bytes 294920 | tf_op jit(solution)/shard_map/ppermute | solution.py:491
  41.1 0.4 collective-permute-start.2
  41.5 2.2 %collective-permute-done.5.m3 = f32[12,16,128]{2,1,0:T(8,128)S(1)} collective-permute-done((f32[12,16,128]{2,1,0:T(8,128)}, f32[12,16,128]{2,1,0:T(8,128)S(1)}, u32[]{:S(2)}, u32[]{:S(2)}) %collective-permute-start.5) | collective-permute-done | bytes 98336 | tf_op jit(solution)/shard_map/ppermute | solution.py:491
  43.7 0.0 copy-start.2
  43.7 0.0 collective-permute-done.4.m2
  43.7 0.0 copy-start.3
  43.7 4.9 %collective-permute-done.3.m1 = f32[12,16,128]{2,1,0:T(8,128)S(1)} collective-permute-done((f32[12,16,128]{2,1,0:T(8,128)}, f32[12,16,128]{2,1,0:T(8,128)S(1)}, u32[]{:S(2)}, u32[]{:S(2)}) %collective-permute-start.3) | collective-permute-done | bytes 98336 | tf_op jit(solution)/shard_map/ppermute | solution.py:491
  48.6 0.0 copy-start.4
  48.6 0.0 collective-permute-done.2.m0
  48.6 0.0 copy-start.5
  48.6 0.0 copy-done.2
  48.6 0.0 copy-done.3
  48.6 0.6 copy-done.4
  49.2 0.0 copy-done.5
  49.3 10.9 %middle.1 = (f32[8,16,128]{2,1,0:T(8,128)}, f32[6,4,80,128]{3,2,1,0:T(8,128)}, f32[6,2,40,128]{3,2,1,0:T(8,128)}, f32[6,1,24,128]{3,2,1,0:T(8,128)}, f32[16,128,...) custom-call(f32[12,16,128]{2,1,0:T(8,128)} %copy-done.5, f32[12,16,128]{2,1,0:T(8,128)} %copy-done.4, ...), custom_call_target="tpu_custom_call" | custom-call | tf_op jit(solution)/shard_map/middle/pallas_call | solution.py:522
  60.2 0.1 collective-permute-start.9
  60.3 2.8 %collective-permute-start.8 = (f32[8,16,128]{2,1,0:T(8,128)}, f32[8,16,128]{2,1,0:T(8,128)S(1)}, u32[]{:S(2)}, u32[]{:S(2)}) collective-permute-start(f32[8,16,128]{2,1,0:T(8,128)} %get-tuple-element.33.m4), channel_id=1, source_target_pairs={{0,2},{1,3},{2,0},{3,1},{4,6},{5,7},{6,4},{7,5},{8,10},{9,11},{10,... | collective-permute-start | bytes 196616 | tf_op jit(solution)/shard_map/ppermute | solution.py:491
  63.1 4.2 %collective-permute-start.7 = (f32[8,16,128]{2,1,0:T(8,128)}, f32[8,16,128]{2,1,0:T(8,128)S(1)}, u32[]{:S(2)}, u32[]{:S(2)}) collective-permute-start(f32[8,16,128]{2,1,0:T(8,128)} %get-tuple-element.33.m4), channel_id=1, source_target_pairs={{1,2},{2,1},{3,4},{4,3},{5,6},{6,5},{7,8},{8,7},{9,10},{10,9},{11,... | collective-permute-start | bytes 196616 | tf_op jit(solution)/shard_map/ppermute | solution.py:491
  67.3 0.4 collective-permute-start.6
  67.7 1.6 %collective-permute-done.9.m3 = f32[8,16,128]{2,1,0:T(8,128)S(1)} collective-permute-done((f32[8,16,128]{2,1,0:T(8,128)}, f32[8,16,128]{2,1,0:T(8,128)S(1)}, u32[]{:S(2)}, u32[]{:S(2)}) %collective-permute-start.9) | collective-permute-done | bytes 65568 | tf_op jit(solution)/shard_map/ppermute | solution.py:491
  69.3 0.0 copy-start.6
  69.3 0.0 collective-permute-done.8.m2
  69.3 0.0 copy-start.7
  69.3 2.9 %collective-permute-done.7.m1 = f32[8,16,128]{2,1,0:T(8,128)S(1)} collective-permute-done((f32[8,16,128]{2,1,0:T(8,128)}, f32[8,16,128]{2,1,0:T(8,128)S(1)}, u32[]{:S(2)}, u32[]{:S(2)}) %collective-permute-start.7) | collective-permute-done | bytes 65568 | tf_op jit(solution)/shard_map/ppermute | solution.py:491
  72.3 0.0 copy-start.8
  72.3 0.0 collective-permute-done.6.m0
  72.3 0.0 copy-start.9
  72.3 0.0 copy-done.6
  72.3 0.0 copy-done.7
  72.3 0.6 copy-done.8
  72.9 0.0 copy-done.9
  72.9 11.0 %close.1 = (f32[64,2048]{1,0:T(8,128)}, f32[64,1024]{1,0:T(8,128)}, f32[64,1024]{1,0:T(8,128)}) custom-call(f32[8,16,128]{2,1,0:T(8,128)} %copy-done.9, f32[8,16,128]{2,1,0:T(8,128)} %copy-done.8, f32[8,16,128]{2,1,0:T(8,128)} %copy-done.7, f32[8,16,128]{2,1,0:T(8,128)} %copy-done.6, f32[8,16,128]{2,1,0:T(8,128)} %get-tuple-element.33.m4, ...), custom_call_target="tpu_custom_call" | custom-call | tf_op jit(solution)/shard_map/close/pallas_call | solution.py:533
  83.9 5.2 %collective-permute-start.10 = (f32[64,1024]{1,0:T(8,128)}, f32[64,1024]{1,0:T(8,128)S(1)}, u32[]{:S(2)}, u32[]{:S(2)}) collective-permute-start(f32[64,1024]{1,0:T(8,128)} %get-tuple-element.42), channel_id=1, source_target_pairs={{0,64},{64,0},{1,65},{65,1},{2,66},{66,2},{3,67},{67,3},{4,68},{68... | collective-permute-start | bytes 786440 | tf_op jit(solution)/shard_map/ppermute | solution.py:542
  89.1 1.4 %collective-permute-done.10 = f32[64,1024]{1,0:T(8,128)S(1)} collective-permute-done((f32[64,1024]{1,0:T(8,128)}, f32[64,1024]{1,0:T(8,128)S(1)}, u32[]{:S(2)}, u32[]{:S(2)}) %collective-permute-start.10) | collective-permute-done | bytes 262176 | tf_op jit(solution)/shard_map/ppermute | solution.py:542
  90.5 1.8 %multiply_subtract_fusion = (f32[64,1024]{1,0:T(8,128)}, f32[64,1024]{1,0:T(8,128)}) fusion(f32[64,1024]{1,0:T(8,128)S(1)} %collective-permute-done.10, f32[64,1024]{1,0:T(8,128)} %get-tuple-element.41), kind=kLoop, calls=%fused_computation | loop fusion | flops 458752 | bytes 1048576 | tf_op jit(solution)/shard_map/sub | solution.py:546
Async XLA Ops:
  6.7 10.6 %collective-permute-start = (f32[32,24,128]{2,1,0:T(8,128)}, f32[32,24,128]{2,1,0:T(8,128)S(1)}, u32[]{:S(2)}, u32[]{:S(2)}) collective-permute-start(f32[32,24,128]{2,1,0:T(8,128)} %get-tuple-element.24), channel_id=1, source_target_pairs={{0,1},{1,0},{2,3},{3,2},{4,5},{5,4},{6,7},{7,6},{8,9},{9,8},{10,11... | collective-permute-start | bytes 1179656 | tf_op jit(solution)/shard_map/ppermute | solution.py:507
  8.8 16.5 %collective-permute-start.1 = (f32[32,24,128]{2,1,0:T(8,128)}, f32[32,24,128]{2,1,0:T(8,128)S(1)}, u32[]{:S(2)}, u32[]{:S(2)}) collective-permute-start(f32[32,24,128]{2,1,0:T(8,128)} %get-tuple-element.25), channel_id=1, source_target_pairs={{1,2},{2,1},{3,4},{4,3},{5,6},{6,5},{7,8},{8,7},{9,10},{10,9},{11,... | collective-permute-start | bytes 1179656 | tf_op jit(solution)/shard_map/ppermute | solution.py:507
  17.4 7.9 %copy-start = (f32[32,24,128]{2,1,0:T(8,128)}, f32[32,24,128]{2,1,0:T(8,128)S(1)}, u32[]{:S(2)}) copy-start(f32[32,24,128]{2,1,0:T(8,128)S(1)} %collective-permute-done.first_ref) | copy-start | bytes 1179652
  25.3 0.8 copy-start.1
  34.2 9.5 %collective-permute-start.5 = (f32[12,16,128]{2,1,0:T(8,128)}, f32[12,16,128]{2,1,0:T(8,128)S(1)}, u32[]{:S(2)}, u32[]{:S(2)}) collective-permute-start(f32[12,16,128]{2,1,0:T(8,128)} %get-tuple-element.26.m4), channel_id=1, source_target_pairs={{2,4},{3,5},{4,2},{5,3},{6,8},{7,9},{8,6},{9,7},{10,12},{11,13},{1... | collective-permute-start | bytes 294920 | tf_op jit(solution)/shard_map/ppermute | solution.py:491
  36.1 7.6 %collective-permute-start.4 = (f32[12,16,128]{2,1,0:T(8,128)}, f32[12,16,128]{2,1,0:T(8,128)S(1)}, u32[]{:S(2)}, u32[]{:S(2)}) collective-permute-start(f32[12,16,128]{2,1,0:T(8,128)} %get-tuple-element.26.m4), channel_id=1, source_target_pairs={{0,2},{1,3},{2,0},{3,1},{4,6},{5,7},{6,4},{7,5},{8,10},{9,11},{10,... | collective-permute-start | bytes 294920 | tf_op jit(solution)/shard_map/ppermute | solution.py:491
  36.1 12.5 %collective-permute-start.3 = (f32[12,16,128]{2,1,0:T(8,128)}, f32[12,16,128]{2,1,0:T(8,128)S(1)}, u32[]{:S(2)}, u32[]{:S(2)}) collective-permute-start(f32[12,16,128]{2,1,0:T(8,128)} %get-tuple-element.26.m4), channel_id=1, source_target_pairs={{1,2},{2,1},{3,4},{4,3},{5,6},{6,5},{7,8},{8,7},{9,10},{10,9},{11,... | collective-permute-start | bytes 294920 | tf_op jit(solution)/shard_map/ppermute | solution.py:491
  41.1 7.5 %collective-permute-start.2 = (f32[12,16,128]{2,1,0:T(8,128)}, f32[12,16,128]{2,1,0:T(8,128)S(1)}, u32[]{:S(2)}, u32[]{:S(2)}) collective-permute-start(f32[12,16,128]{2,1,0:T(8,128)} %get-tuple-element.26.m4), channel_id=1, source_target_pairs={{0,1},{1,0},{2,3},{3,2},{4,5},{5,4},{6,7},{7,6},{8,9},{9,8},{10,11... | collective-permute-start | bytes 294920 | tf_op jit(solution)/shard_map/ppermute | solution.py:491
  43.7 4.9 %copy-start.2 = (f32[12,16,128]{2,1,0:T(8,128)}, f32[12,16,128]{2,1,0:T(8,128)S(1)}, u32[]{:S(2)}) copy-start(f32[12,16,128]{2,1,0:T(8,128)S(1)} %collective-permute-done.5.m3) | copy-start | bytes 294916
  43.7 4.9 %copy-start.3 = (f32[12,16,128]{2,1,0:T(8,128)}, f32[12,16,128]{2,1,0:T(8,128)S(1)}, u32[]{:S(2)}) copy-start(f32[12,16,128]{2,1,0:T(8,128)S(1)} %collective-permute-done.4.m2) | copy-start | bytes 294916
  48.6 0.6 copy-start.4
  48.6 0.7 copy-start.5
  60.2 9.1 %collective-permute-start.9 = (f32[8,16,128]{2,1,0:T(8,128)}, f32[8,16,128]{2,1,0:T(8,128)S(1)}, u32[]{:S(2)}, u32[]{:S(2)}) collective-permute-start(f32[8,16,128]{2,1,0:T(8,128)} %get-tuple-element.33.m4), channel_id=1, source_target_pairs={{2,4},{3,5},{4,2},{5,3},{6,8},{7,9},{8,6},{9,7},{10,12},{11,13},{1... | collective-permute-start | bytes 196616 | tf_op jit(solution)/shard_map/ppermute | solution.py:491
  60.3 9.0 %collective-permute-start.8 = (f32[8,16,128]{2,1,0:T(8,128)}, f32[8,16,128]{2,1,0:T(8,128)S(1)}, u32[]{:S(2)}, u32[]{:S(2)}) collective-permute-start(f32[8,16,128]{2,1,0:T(8,128)} %get-tuple-element.33.m4), channel_id=1, source_target_pairs={{0,2},{1,3},{2,0},{3,1},{4,6},{5,7},{6,4},{7,5},{8,10},{9,11},{10,... | collective-permute-start | bytes 196616 | tf_op jit(solution)/shard_map/ppermute | solution.py:491
  63.1 9.2 %collective-permute-start.7 = (f32[8,16,128]{2,1,0:T(8,128)}, f32[8,16,128]{2,1,0:T(8,128)S(1)}, u32[]{:S(2)}, u32[]{:S(2)}) collective-permute-start(f32[8,16,128]{2,1,0:T(8,128)} %get-tuple-element.33.m4), channel_id=1, source_target_pairs={{1,2},{2,1},{3,4},{4,3},{5,6},{6,5},{7,8},{8,7},{9,10},{10,9},{11,... | collective-permute-start | bytes 196616 | tf_op jit(solution)/shard_map/ppermute | solution.py:491
  67.3 5.0 %collective-permute-start.6 = (f32[8,16,128]{2,1,0:T(8,128)}, f32[8,16,128]{2,1,0:T(8,128)S(1)}, u32[]{:S(2)}, u32[]{:S(2)}) collective-permute-start(f32[8,16,128]{2,1,0:T(8,128)} %get-tuple-element.33.m4), channel_id=1, source_target_pairs={{0,1},{1,0},{2,3},{3,2},{4,5},{5,4},{6,7},{7,6},{8,9},{9,8},{10,11... | collective-permute-start | bytes 196616 | tf_op jit(solution)/shard_map/ppermute | solution.py:491
  69.3 3.0 %copy-start.6 = (f32[8,16,128]{2,1,0:T(8,128)}, f32[8,16,128]{2,1,0:T(8,128)S(1)}, u32[]{:S(2)}) copy-start(f32[8,16,128]{2,1,0:T(8,128)S(1)} %collective-permute-done.9.m3) | copy-start | bytes 196612
  69.3 3.0 %copy-start.7 = (f32[8,16,128]{2,1,0:T(8,128)}, f32[8,16,128]{2,1,0:T(8,128)S(1)}, u32[]{:S(2)}) copy-start(f32[8,16,128]{2,1,0:T(8,128)S(1)} %collective-permute-done.8.m2) | copy-start | bytes 196612
  72.3 0.6 copy-start.8
  72.3 0.6 copy-start.9
  83.9 6.5 %collective-permute-start.10 = (f32[64,1024]{1,0:T(8,128)}, f32[64,1024]{1,0:T(8,128)S(1)}, u32[]{:S(2)}, u32[]{:S(2)}) collective-permute-start(f32[64,1024]{1,0:T(8,128)} %get-tuple-element.42), channel_id=1, source_target_pairs={{0,64},{64,0},{1,65},{65,1},{2,66},{66,2},{3,67},{67,3},{4,68},{68... | collective-permute-start | bytes 786440 | tf_op jit(solution)/shard_map/ppermute | solution.py:542

commit v3 on v2

v3 whole, which is shorter than its diff:
```python
import functools

import jax
import jax.numpy as jnp
from jax import lax
from jax.experimental import pallas as pl
from jax.experimental.pallas import tpu as pltpu
from jax.sharding import PartitionSpec as P

LANES = 128
PAD = 8
OWN = (64, 32, 16, 8, 4)
HALO = (24, 12, 32, 16, 8)
ROWS = tuple(o + 2 * h for o, h in zip(OWN, HALO))
TILES = (16, 8, 4, 2, 1)
STRIPS = (14, 7, 10, 5, 3)
BUF = tuple(8 * s + 2 * PAD for s in STRIPS)
SOLVES = (1, 2, 2, 2, 2)
UNROLL = (2, 7, 5, 5, 3)
DAMP = 0.8
F32 = jnp.float32


def loop(count, body, unroll=1):
    first, last = count if isinstance(count, tuple) else (0, count)
    if unroll >= last - first:
        for i in range(first, last):
            body(i)
    else:
        lax.fori_loop(first, last, lambda i, c: (body(i), c)[1], 0, unroll=unroll)


def at(i, offset, step=8):
    if isinstance(i, int):
        return pl.ds(i * step + offset, 8)
    return pl.ds(pl.multiple_of(i * step, step) + offset, 8)


def pairs_at(i, offset):
    base = i * 16 if isinstance(i, int) else pl.multiple_of(i * 16, 16)
    return pl.ds(base + offset, 8, stride=2), pl.ds(base + offset + 1, 8, stride=2)


def iota(dim):
    return lax.broadcasted_iota(jnp.int32, (8, LANES), dim)


def from_west(x):
    return jnp.where(iota(1) < 16, pltpu.roll(x, 17, 1), pltpu.roll(x, 16, 1))


def from_east(x):
    return jnp.where(iota(1) >= LANES - 16, pltpu.roll(x, LANES - 17, 1), pltpu.roll(x, LANES - 16, 1))


def side_values(x):
    return [from_west(x[-1])] + x[:-1], x[1:] + [from_east(x[0])]


def harmonic(a, b):
    return 2.0 * a * b / (a + b)


def make_weights(level, c_ref, a_ref, first_row, total_rows, source_ref=None, b_ref=None):
    tiles = TILES[level]

    def body(i):
        c = [c_ref[t, at(i, PAD), :] for t in range(tiles)]
        row = first_row + i * 8 + iota(0)
        lane = iota(1)
        inside = jnp.logical_and(row >= 0, row < total_rows)
        _, east = side_values(c)
        w_east = [harmonic(a, b) for a, b in zip(c, east)]
        w_west, _ = side_values(w_east)
        w_west[0] = jnp.where(lane == 0, harmonic(c[0], c[0]), w_west[0])
        w_east[-1] = jnp.where(lane == LANES - 1, harmonic(c[-1], c[-1]), w_east[-1])
        for t in range(tiles):
            w_north = harmonic(c[t], jnp.where(row == 0, c[t], c_ref[t, at(i, PAD - 1), :]))
            w_south = harmonic(c[t], jnp.where(row == total_rows - 1, c[t], c_ref[t, at(i, PAD + 1), :]))
            diagonal = w_west[t] + w_east[t] + w_north + w_south
            gain = jnp.where(inside, DAMP / diagonal, 0.0)
            a_west, a_east = gain * w_west[t], gain * w_east[t]
            if t == 0:
                a_west = jnp.where(lane == 0, 0.0, a_west)
            if t == tiles - 1:
                a_east = jnp.where(lane == LANES - 1, 0.0, a_east)
            rows = at(i, 0)
            a_ref[0, t, rows, :] = a_west
            a_ref[1, t, rows, :] = a_east
            a_ref[2, t, rows, :] = gain * w_north
            a_ref[3, t, rows, :] = gain * w_south
            a_ref[4, t, rows, :] = gain
            a_ref[5, t, rows, :] = diagonal * (1.0 / DAMP)
            if source_ref is not None:
                b_ref[t, at(i, PAD), :] = gain * source_ref[t, at(i, PAD), :]

    loop(STRIPS[level], body)


def sweep(level, v_ref, out_ref, b_ref, a_ref, finish, strips):
    tiles, solves = TILES[level], SOLVES[level]

    def body(i):
        v = [[v_ref[s * tiles + t, at(i, PAD), :] for t in range(tiles)] for s in range(solves)]
        sides = [side_values(x) for x in v]
        rows = at(i, 0)
        order = list(range(1, tiles - 1)) + ([0, tiles - 1] if tiles > 1 else [0])
        for t in order:
            a_west, a_east, a_north, a_south = (a_ref[k, t, rows, :] for k in range(4))
            for s in range(solves):
                west, east = sides[s]
                k = s * tiles + t
                north, south = v_ref[k, at(i, PAD - 1), :], v_ref[k, at(i, PAD + 1), :]
                moved = (a_north * north + a_south * south) + b_ref[k, at(i, PAD), :]
                moved += a_west * west[t] + a_east * east[t]
                out_ref[k, at(i, PAD), :] = finish(v[s][t], moved, t, rows)

    loop(strips or STRIPS[level], body, UNROLL[level])


def relax(level, v_ref, out_ref, b_ref, a_ref, strips=None):
    sweep(level, v_ref, out_ref, b_ref, a_ref, lambda v, moved, t, rows: (1.0 - DAMP) * v + moved, strips)


def residual(level, v_ref, out_ref, b_ref, a_ref, strips=None):
    def finish(v, moved, t, rows):
        return a_ref[5, t, rows, :] * (moved - DAMP * v)

    sweep(level, v_ref, out_ref, b_ref, a_ref, finish, strips)


def restrict(count, ref, offset, tiles, store, unroll=1):
    def body(j):
        even, odd = pairs_at(j, offset)
        for k in range(0, len(tiles), 2):
            a, b = tiles[k], tiles[k + 1]
            store(j, k // 2, (ref[a, even, :] + ref[a, odd, :]) + (ref[b, even, :] + ref[b, odd, :]))

    loop(count, body, unroll)


def prolong(count, e_ref, offset, e_tiles, v_ref, sign=1.0, v_offset=PAD, unroll=1):
    def body(j):
        halves = pairs_at(j, v_offset)
        for k, tile in enumerate(e_tiles):
            e = sign * e_ref[tile, at(j, offset), :]
            for t in (2 * k, 2 * k + 1):
                for rows in halves:
                    v_ref[t, rows, :] = v_ref[t, rows, :] + e

    loop(count, body, unroll)


def clear_pads(*refs, value=0.0, size=PAD):
    for ref in refs:
        tiles, rows, _ = ref.shape
        ref[:, 0:size, :] = jnp.full((tiles, size, LANES), value, F32)
        ref[:, rows - size : rows, :] = jnp.full((tiles, size, LANES), value, F32)


def fill(ref, value):
    def body(i):
        ref[:, at(i, 0), :] = jnp.full((ref.shape[0], 8, LANES), value, F32)

    loop(ref.shape[1] // 8, body)


def turn(groups):
    lane = iota(1)
    groups = [list(x) for x in groups]
    for step in (1, 2, 4, 8):
        upper = lax.rem(lane, 2 * step) >= step
        for i in range(16):
            if i & step == 0:
                j = i + step
                for x in groups:
                    from_j = pltpu.roll(x[j], step, 1)
                    from_i = pltpu.roll(x[i], LANES - step, 1)
                    x[i], x[j] = jnp.where(upper, from_j, x[i]), jnp.where(upper, x[j], from_i)
    return groups


def place():
    return lax.axis_index("grid")


def first_row(level):
    return place() * OWN[level] - HALO[level]


def towards_next():
    i = place()
    return lax.rem(i, 2) == 0, lax.rem(i, 4) < 2


def slab_positions():
    next_first, far = towards_next()
    return (
        jnp.where(next_first, 3, 1), jnp.where(next_first, 1, 3), jnp.where(far, 4, 0), jnp.where(far, 0, 4), 2,
    )


def pack_kernel(log_ref, src_ref, c0, s0, first_ref, second_ref):
    halo, own = HALO[0], OWN[0]
    tiles = TILES[0]

    def body(i):
        logs, sources = ([ref[at(i, 0), t * LANES : (t + 1) * LANES] for t in range(tiles)] for ref in (log_ref, src_ref))
        for ref, x in zip((c0, s0), turn(([jnp.exp(v) for v in logs], sources))):
            for t, v in enumerate(x):
                ref[t, at(i, PAD + halo), :] = v

    loop(own // 8, body)
    next_first, _ = towards_next()
    start = jnp.where(next_first, own - halo, 0)
    for ref, base in ((first_ref, start), (second_ref, own - halo - start)):
        for i in range(halo // 8):
            rows = pl.ds(pl.multiple_of(PAD + halo + base + 8 * i, 8), 8)
            for t in range(tiles):
                ref[t, 8 * i : 8 * i + 8, :] = c0[t, rows, :]
                ref[tiles + t, 8 * i : 8 * i + 8, :] = s0[t, rows, :]


def scaled_store(bp_ref, a_ref, start=0):
    def store(j, k, q):
        bp_ref[start + k, at(j, PAD), :] = a_ref[4, k, at(j, 0), :] * q

    return store


def quarter_store(c_ref):
    def store(j, k, q):
        c_ref[k, at(j, PAD), :] = 0.25 * q

    return store


def open_kernel(
    peers, c0_in, s0_in, first_ref, second_ref,
    c0, s0, msg_ref, a0, bp0, va0, a1, bp1, va1,
    vb0, c1, vb1,
):
    halo, own, tiles = HALO[0], OWN[0], TILES[0]
    next_first, _ = towards_next()
    above, below = PAD, PAD + halo + own
    for ref, base in ((first_ref, jnp.where(next_first, below, above)), (second_ref, jnp.where(next_first, above, below))):
        for i in range(halo // 8):
            rows = pl.ds(pl.multiple_of(base + 8 * i, 8), 8)
            for t in range(tiles):
                c0[t, rows, :] = ref[t, 8 * i : 8 * i + 8, :]
                s0[t, rows, :] = ref[tiles + t, 8 * i : 8 * i + 8, :]
    clear_pads(c0, c1, value=1.0)
    clear_pads(bp0, va0, vb0, bp1, va1, vb1)
    make_weights(0, c0, a0, first_row(0), peers * OWN[0], s0, bp0)
    restrict(STRIPS[1], c0, PAD, range(tiles), quarter_store(c1))
    make_weights(1, c1, a1, first_row(1), peers * OWN[1])
    restrict(STRIPS[1], s0, PAD, range(tiles), scaled_store(bp1, a1, TILES[1]))
    relax(0, bp0, va0, bp0, a0)
    residual(0, va0, vb0, bp0, a0)
    restrict(STRIPS[1], vb0, PAD, range(tiles), scaled_store(bp1, a1))
    relax(1, bp1, va1, bp1, a1)
    residual(1, va1, vb1, bp1, a1, (1, 6))

    def store(j, k, q):
        msg_ref[k, at(j, 0), :] = q

    restrict(OWN[2] // 8, vb1, PAD + HALO[1], range(2 * TILES[1]), store, 2)

    def store_coef(j, k, q):
        msg_ref[2 * TILES[2] + k, at(j, 0), :] = 0.25 * q

    restrict(OWN[2] // 8, c1, PAD + HALO[1], range(TILES[1]), store_coef, 2)


def deep_solve(a, bp, va, vb):
    relax(2, bp[2], va[2], bp[2], a[2])
    residual(2, va[2], vb[2], bp[2], a[2])
    for s in range(2):
        restrict(STRIPS[3], vb[2], PAD, range(s * 4, s * 4 + 4), scaled_store(bp[3], a[3], s * 2), 5)
    relax(3, bp[3], va[3], bp[3], a[3])
    residual(3, va[3], vb[3], bp[3], a[3])
    for s in range(2):
        restrict(STRIPS[4], vb[3], PAD, range(s * 2, s * 2 + 2), scaled_store(bp[4], a[4], s), 3)
    relax(4, bp[4], va[4], bp[4], a[4])
    relax(4, va[4], vb[4], bp[4], a[4])
    relax(4, vb[4], va[4], bp[4], a[4])
    prolong(2, va[4], PAD, range(2), va[3], unroll=2)
    relax(3, va[3], vb[3], bp[3], a[3], (0, 5))
    relax(3, vb[3], va[3], bp[3], a[3], (1, 4))
    prolong((1, 4), va[3], PAD, range(4), va[2], unroll=3)
    relax(2, va[2], vb[2], bp[2], a[2], (3, 7))
    relax(2, vb[2], va[2], bp[2], a[2], (3, 7))


def up_level_1(va2, va1, vb1, bp1, a1, strips=(0, 7)):
    offset = PAD + HALO[2] - HALO[1] // 2
    prolong(4, va2, offset, range(2 * TILES[2]), va1)
    relax(1, va1, vb1, bp1, a1, strips)
    relax(1, vb1, va1, bp1, a1, strips)


def up_level_0(va1, va0, vb0, bp0, a0, first, second):
    prolong(STRIPS[1], va1, PAD, range(TILES[1]), va0)
    relax(0, va0, vb0, bp0, a0, first)
    relax(0, vb0, va0, bp0, a0, second)


def assemble(messages, a2, bp2):
    for position, m in zip(slab_positions(), messages):
        for i in range(2):
            row = pl.multiple_of(position * OWN[2] + i * 8, 8)
            for k in range(2 * TILES[2]):
                bp2[k, pl.ds(PAD + row, 8), :] = (
                    a2[4, k % TILES[2], pl.ds(row, 8), :] * m[k, i * 8 : i * 8 + 8, :]
                )


def middle_kernel(
    peers, m0, m1, m2, m3, m4, a0, bp0, va0_in, a1, bp1_in, va1_in,
    msg_ref, a2, a3, a4, va0, bp1, va1,
    vb0, vb1, c2, bp2, va2, vb2, c3, bp3, va3, vb3, c4, bp4, va4, vb4,
):
    messages = (m0, m1, m2, m3, m4)
    fill(c4, 1.0)
    clear_pads(c2, c3, value=1.0)
    for ref in (bp4, va4, vb4):
        fill(ref, 0.0)
    clear_pads(bp2, va2, vb2, bp3, va3, vb3)
    clear_pads(vb0, vb1, size=2 * PAD)
    top = first_row(2)
    for position, m in zip(slab_positions(), messages):
        for i in range(2):
            row = pl.multiple_of(position * OWN[2] + i * 8, 8)
            for k in range(TILES[2]):
                c2[k, pl.ds(PAD + row, 8), :] = m[2 * TILES[2] + k, i * 8 : i * 8 + 8, :]
    make_weights(2, c2, a2, top, peers * OWN[2])
    restrict(STRIPS[3], c2, PAD, range(4), quarter_store(c3), 5)
    make_weights(3, c3, a3, first_row(3), peers * OWN[3])
    restrict(2, c3, PAD, range(2), quarter_store(c4), 2)

    def last_rows(j, k, q):
        c4[k, PAD + 16 : PAD + 24, :] = jnp.where(iota(0) < ROWS[4] - 16, 0.25 * q, 1.0)

    restrict(1, c3, PAD + 32, range(2), last_rows)
    make_weights(4, c4, a4, first_row(4), peers * OWN[4])
    assemble(messages, a2, bp2)
    a = {2: a2, 3: a3, 4: a4}
    bp = {2: bp2, 3: bp3, 4: bp4}
    va = {2: va2, 3: va3, 4: va4}
    vb = {2: vb2, 3: vb3, 4: vb4}
    deep_solve(a, bp, va, vb)
    up_level_1(va2, va1, vb1, bp1, a1)
    up_level_0(va1, va0, vb0, bp0, a0, (1, 13), (1, 13))

    relax(0, va0, vb0, bp0, a0, (1, 13))
    relax(0, vb0, va0, bp0, a0, (1, 13))
    residual(0, va0, vb0, bp0, a0, (1, 13))
    restrict((1, 6), vb0, PAD, range(TILES[0]), scaled_store(bp1, a1))

    def clear(i):
        va1[0 : TILES[1], at(i, 0), :] = jnp.zeros((TILES[1], 8, LANES), F32)

    loop(BUF[1] // 8, clear)
    relax(1, va1, vb1, bp1, a1)
    relax(1, vb1, va1, bp1, a1)
    residual(1, va1, vb1, bp1, a1, (1, 6))

    def store(j, k, q):
        msg_ref[k, at(j, 0), :] = q

    restrict(OWN[2] // 8, vb1, PAD + HALO[1], range(2 * TILES[1]), store, 2)


def close_kernel(
    m0, m1, m2, m3, m4, a0, bp0, va0_in, a1, bp1, va1_in, a2, a3, a4,
    va0, va1, out_ref, mine_ref, other_ref,
    vb0, vb1, bp2, va2, vb2, bp3, va3, vb3, bp4, va4, vb4,
):
    for ref in (bp4, va4, vb4):
        fill(ref, 0.0)
    clear_pads(bp2, va2, vb2, bp3, va3, vb3)
    clear_pads(vb0, vb1, size=2 * PAD)
    assemble((m0, m1, m2, m3, m4), a2, bp2)
    a = {2: a2, 3: a3, 4: a4}
    bp = {2: bp2, 3: bp3, 4: bp4}
    va = {2: va2, 3: va3, 4: va4}
    vb = {2: vb2, 3: vb3, 4: vb4}
    deep_solve(a, bp, va, vb)
    up_level_1(va2, va1, vb1, bp1, a1, (1, 6))
    up_level_0(va1, va0, vb0, bp0, a0, (2, 12), (3, 11))
    prolong(OWN[1] // 8, va1, PAD + HALO[1], range(TILES[1], 2 * TILES[1]), va0, -1.0, PAD + HALO[0])
    tiles = TILES[0]
    left = lax.axis_index("samp") == 0

    def body(i):
        strips = (2 * i, 2 * i + 1)
        turned = turn([[va0[t, at(j, PAD + HALO[0]), :] for t in range(tiles)] for j in strips])
        for j, x in zip(strips, turned):
            for t in range(tiles):
                out_ref[at(j, 0), t * LANES : (t + 1) * LANES] = x[t]
            for t in range(tiles // 2):
                low, high = x[t], x[tiles // 2 + t]
                mine_ref[at(j, 0), t * LANES : (t + 1) * LANES] = jnp.where(left, low, high)
                other_ref[at(j, 0), t * LANES : (t + 1) * LANES] = jnp.where(left, high, low)

    loop(OWN[0] // 16, body)


VMEM = pl.BlockSpec(memory_space=pltpu.VMEM)


def near(*dims):
    return pltpu.VMEM(dims, F32)


def held(*values):
    return [pltpu.with_memory_space_constraint(v, pltpu.VMEM) for v in values]


def a_shape(level):
    return (6, TILES[level], 8 * STRIPS[level], LANES)


def v_shape(level):
    return (SOLVES[level] * TILES[level], BUF[level], LANES)


def c_shape(level):
    return (TILES[level], BUF[level], LANES)


def call(kernel, name, arguments, outputs, scratch=(), aliases=None):
    return pl.pallas_call(
        kernel,
        out_shape=outputs,
        in_specs=[VMEM] * len(arguments),
        out_specs=[VMEM] * len(outputs),
        scratch_shapes=[pltpu.VMEM(s, F32) for s in scratch],
        input_output_aliases=aliases or {},
        compiler_params=pltpu.CompilerParams(vmem_limit_bytes=24 * 2**20),
        name=name,
    )(*arguments)


def swaps(distance):
    peers = lax.axis_size("grid")
    even = [(i, i + distance if i % (2 * distance) < distance else i - distance) for i in range(peers)]
    odd = [((a + distance) % peers, (b + distance) % peers) for a, b in even]
    return even, odd


def gathered(value):
    return [lax.ppermute(value, "grid", pairs) for distance in (1, 2) for pairs in swaps(distance)] + [value]


def local(log_coef, source):
    peers = lax.axis_size("grid")
    log_field, source_field = log_coef[0], source[0]
    rows, columns = source_field.shape
    edge = near(2 * TILES[0], HALO[0], LANES)
    c0, s0, first, second = call(
        pack_kernel, "pack", (log_field, source_field), (near(*c_shape(0)), near(*c_shape(0)), edge, edge)
    )
    even, odd = swaps(1)
    first, second = lax.ppermute(first, "grid", even), lax.ppermute(second, "grid", odd)

    state = [near(*f(level)) for level in (0, 1) for f in (a_shape, v_shape, v_shape)]
    c0, s0, message, a0, b0, v0, a1, b1, v1 = call(
        functools.partial(open_kernel, peers),
        "open",
        held(c0, s0, first, second),
        [near(*c_shape(0)), near(*c_shape(0)), near(3 * TILES[2], OWN[2], LANES)] + state,
        [v_shape(0), c_shape(1), v_shape(1)],
        {0: 0, 1: 1},
    )
    deep = [shape for level in (2, 3, 4) for shape in [c_shape(level)] + [v_shape(level)] * 3]
    message, a2, a3, a4, v0, b1, v1 = call(
        functools.partial(middle_kernel, peers),
        "middle",
        held(*gathered(message), a0, b0, v0, a1, b1, v1),
        [near(2 * TILES[2], OWN[2], LANES)] + [near(*a_shape(level)) for level in (2, 3, 4)] + [state[k] for k in (2, 4, 5)],
        [v_shape(0), v_shape(1)] + deep,
        {7: 4, 9: 5, 10: 6},
    )
    deep = [shape for level in (2, 3, 4) for shape in [v_shape(level)] * 3]
    half = near(rows, columns // 2)
    v0, v1, correction, mine, other = call(
        close_kernel,
        "close",
        held(*gathered(message), a0, b0, v0, a1, b1, v1, a2, a3, a4),
        (state[2], state[5], jax.ShapeDtypeStruct((rows, columns), F32), half, half),
        [v_shape(0), v_shape(1)] + deep,
        {7: 0, 10: 1},
    )

    theirs = lax.ppermute(other, "samp", [(0, 1), (1, 0)])
    samples = lax.axis_size("samp")
    level_mean = (mine + theirs) / samples
    squares = mine * mine + theirs * theirs
    level_var = (squares - samples * level_mean * level_mean) / (samples - 1)
    return (correction[None], level_mean, level_var)


def solution(mesh):
    in_specs = (P("samp", "grid", None), P("samp", "grid", None))
    out_specs = (P("samp", "grid", None), P("grid", "samp"), P("grid", "samp"))
    return jax.shard_map(local, mesh=mesh, in_specs=in_specs, out_specs=out_specs, check_vma=False)
```

time: 92.5 us -> 76 us (0.82)
  Pallas kernels: 36.2 us -> 21.5 us
  other arithmetic: 1.81 us -> 0.86 us
    pallas_call x4, Pallas kernels: 36.2 us -> 21.5 us  [call(): pl.pallas_call(kernel, out_shape=outputs, in_specs=[VMEM] * len(arguments...]
    sub x1, other arithmetic: 1.81 us -> 0.86 us  [local(): level_var = (squares - samples * level_mean * level_mean) / (samples - 1)]
    unnamed x20 -> x4, local copies, waits for them, and re-layouts: 2.06 us -> 2.08 us
where the time goes in v3:
time: 76 us; the launch traced here: 75.8 us
  starting transfers between devices  29.7 us (39%)
  Pallas kernels  21.5 us (28%)
  waiting for transfers between devices  20.9 us (28%)
  local copies, waits for them, and re-layouts  2.08 us (3%)
  other arithmetic  0.86 us (1%)
    pallas_call x4, Pallas kernels, call(): pl.pallas_call(kernel, out_shape=outputs, in_specs=[VMEM] * len(arguments...  21.5 us
    ppermute x8, starting transfers between devices, gathered(): lax.ppermute(value, 'grid', pairs)  14.8 us
    ppermute x8, waiting for transfers between devices, gathered(): lax.ppermute(value, 'grid', pairs)  11.2 us
    ppermute x1, waiting for transfers between devices, local(): lax.ppermute(second, 'grid', odd)  7.88 us
    ppermute x1, starting transfers between devices, local(): lax.ppermute(second, 'grid', odd)  7.74 us
    ppermute x1, starting transfers between devices, local(): theirs = lax.ppermute(other, 'samp', [(0, 1), (1, 0)])  5.08 us
    ppermute x1, starting transfers between devices, local(): lax.ppermute(first, 'grid', even)  2.11 us
    unnamed x4, local copies, waits for them, and re-layouts  2.08 us
  transfers between devices with their start and end apart: 11, of which 7 were waited for; matrix products, arithmetic and copies ran while one was open for 0% of the time, Pallas kernels for 0%

profile of v3, /device:TPU:1, one launch (start us, length us, event | category | flops | bytes accessed | tf_op | source)
XLA Modules:
  0.0 75.8 jit_solution(14583056382394913842)
XLA Ops:
  0.6 0.0 copy-start
  0.6 1.0 %copy-done = f32[1,64,2048]{2,1,0:T(8,128)S(1)} copy-done((f32[1,64,2048]{2,1,0:T(8,128)S(1)}, f32[1,64,2048]{2,1,0:T(8,128)}, u32[]{:S(2)}) %copy-start) | copy-done | bytes 524312
  1.7 0.0 copy-start.1
  1.7 1.0 %copy-done.1 = f32[1,64,2048]{2,1,0:T(8,128)S(1)} copy-done((f32[1,64,2048]{2,1,0:T(8,128)S(1)}, f32[1,64,2048]{2,1,0:T(8,128)}, u32[]{:S(2)}) %copy-start.1) | copy-done | bytes 524312
  2.7 3.1 %pack.1 = (f32[16,128,128]{2,1,0:T(8,128)S(1)}, f32[16,128,128]{2,1,0:T(8,128)S(1)}, f32[32,24,128]{2,1,0:T(8,128)S(1)}, f32[32,24,128]{2,1,0:T(8,128)S(1)}) custom-call(f32[64,2048]{1,0:T(8,128)S(1)} %bitcast.3, f32[64,2048]{1,0:T(8,128)S(1)} %bitcast.4), custom_call_target="tpu_custom_call" | custom-call | tf_op jit(solution)/shard_map/pack/pallas_call | solution.py:433
  5.8 2.1 %collective-permute-start = (f32[32,24,128]{2,1,0:T(8,128)S(1)}, f32[32,24,128]{2,1,0:T(8,128)S(1)}, u32[]{:S(2)}, u32[]{:S(2)}) collective-permute-start(f32[32,24,128]{2,1,0:T(8,128)S(1)} %get-tuple-element.26), channel_id=1, source_target_pairs={{0,1},{1,0},{2,3},{3,2},{4,5},{5,4},{6,7},{7,6},{8,9},{9,8},{10,11... | collective-permute-start | bytes 1179656 | tf_op jit(solution)/shard_map/ppermute | solution.py:465
  7.9 7.7 %collective-permute-start.1 = (f32[32,24,128]{2,1,0:T(8,128)S(1)}, f32[32,24,128]{2,1,0:T(8,128)S(1)}, u32[]{:S(2)}, u32[]{:S(2)}) collective-permute-start(f32[32,24,128]{2,1,0:T(8,128)S(1)} %get-tuple-element.27), channel_id=1, source_target_pairs={{1,2},{2,1},{3,4},{4,3},{5,6},{6,5},{7,8},{8,7},{9,10},{10,9},{11,... | collective-permute-start | bytes 1179656 | tf_op jit(solution)/shard_map/ppermute | solution.py:465
  15.6 0.7 collective-permute-done.first_ref
  16.3 7.9 %collective-permute-done.1.second_ref = f32[32,24,128]{2,1,0:T(8,128)S(1)} collective-permute-done((f32[32,24,128]{2,1,0:T(8,128)S(1)}, f32[32,24,128]{2,1,0:T(8,128)S(1)}, u32[]{:S(2)}, u32[]{:S(2)}) %collective-permute-start.1) | collective-permute-done | bytes 393248 | tf_op jit(solution)/shard_map/ppermute | solution.py:465
  24.2 5.5 %open.1 = (f32[16,128,128]{2,1,0:T(8,128)S(1)}, f32[16,128,128]{2,1,0:T(8,128)S(1)}, f32[12,16,128]{2,1,0:T(8,128)S(1)}, f32[6,16,112,128]{3,2,1,0:T(8,128)S(1)}...) custom-call(f32[16,128,128]{2,1,0:T(8,128)S(1)} %get-tuple-element.2, ...), custom_call_target="tpu_custom_call", output_to_operand_aliasing={{0}: (0, {}), {1}: (1, {})} | custom-call | tf_op jit(solution)/shard_map/open/pallas_call | solution.py:433
  29.7 1.9 %collective-permute-start.5 = (f32[12,16,128]{2,1,0:T(8,128)S(1)}, f32[12,16,128]{2,1,0:T(8,128)S(1)}, u32[]{:S(2)}, u32[]{:S(2)}) collective-permute-start(f32[12,16,128]{2,1,0:T(8,128)S(1)} %get-tuple-element.28.m4), channel_id=1, source_target_pairs={{2,4},{3,5},{4,2},{5,3},{6,8},{7,9},{8,6},{9,7},{10,12},{11,13},{1... | collective-permute-start | bytes 294920 | tf_op jit(solution)/shard_map/ppermute | solution.py:453
  31.6 0.0 collective-permute-start.4
  31.6 5.0 %collective-permute-start.3 = (f32[12,16,128]{2,1,0:T(8,128)S(1)}, f32[12,16,128]{2,1,0:T(8,128)S(1)}, u32[]{:S(2)}, u32[]{:S(2)}) collective-permute-start(f32[12,16,128]{2,1,0:T(8,128)S(1)} %get-tuple-element.28.m4), channel_id=1, source_target_pairs={{1,2},{2,1},{3,4},{4,3},{5,6},{6,5},{7,8},{8,7},{9,10},{10,9},{11,... | collective-permute-start | bytes 294920 | tf_op jit(solution)/shard_map/ppermute | solution.py:453
  36.6 0.4 collective-permute-start.2
  37.0 2.0 %collective-permute-done.5.m3 = f32[12,16,128]{2,1,0:T(8,128)S(1)} collective-permute-done((f32[12,16,128]{2,1,0:T(8,128)S(1)}, f32[12,16,128]{2,1,0:T(8,128)S(1)}, u32[]{:S(2)}, u32[]{:S(2)}) %collective-permute-start.5) | collective-permute-done | bytes 98336 | tf_op jit(solution)/shard_map/ppermute | solution.py:453
  39.0 0.0 collective-permute-done.4.m2
  39.0 4.9 %collective-permute-done.3.m1 = f32[12,16,128]{2,1,0:T(8,128)S(1)} collective-permute-done((f32[12,16,128]{2,1,0:T(8,128)S(1)}, f32[12,16,128]{2,1,0:T(8,128)S(1)}, u32[]{:S(2)}, u32[]{:S(2)}) %collective-permute-start.3) | collective-permute-done | bytes 98336 | tf_op jit(solution)/shard_map/ppermute | solution.py:453
  43.9 0.0 collective-permute-done.2.m0
  43.9 8.2 %middle.1 = (f32[8,16,128]{2,1,0:T(8,128)S(1)}, f32[6,4,80,128]{3,2,1,0:T(8,128)S(1)}, f32[6,2,40,128]{3,2,1,0:T(8,128)S(1)}, f32[6,1,24,128]{3,2,1,0:T(8,128)S(...) custom-call(f32[12,16,128]{2,1,0:T(8,128)S(1)} %collective-permute-d, ...), custom_call_target="tpu_custom_call", output_to_operand_aliasing={{4}: (7, {}), {5}: (9, {}), {6}: (10, {})} | custom-call | tf_op jit(solution)/shard_map/middle/pallas_call | solution.py:433
  52.1 0.1 collective-permute-start.9
  52.1 2.8 %collective-permute-start.8 = (f32[8,16,128]{2,1,0:T(8,128)S(1)}, f32[8,16,128]{2,1,0:T(8,128)S(1)}, u32[]{:S(2)}, u32[]{:S(2)}) collective-permute-start(f32[8,16,128]{2,1,0:T(8,128)S(1)} %get-tuple-element.35.m4), channel_id=1, source_target_pairs={{0,2},{1,3},{2,0},{3,1},{4,6},{5,7},{6,4},{7,5},{8,10},{9,11},{10,... | collective-permute-start | bytes 196616 | tf_op jit(solution)/shard_map/ppermute | solution.py:453
  55.0 4.2 %collective-permute-start.7 = (f32[8,16,128]{2,1,0:T(8,128)S(1)}, f32[8,16,128]{2,1,0:T(8,128)S(1)}, u32[]{:S(2)}, u32[]{:S(2)}) collective-permute-start(f32[8,16,128]{2,1,0:T(8,128)S(1)} %get-tuple-element.35.m4), channel_id=1, source_target_pairs={{1,2},{2,1},{3,4},{4,3},{5,6},{6,5},{7,8},{8,7},{9,10},{10,9},{11,... | collective-permute-start | bytes 196616 | tf_op jit(solution)/shard_map/ppermute | solution.py:453
  59.2 0.4 collective-permute-start.6
  59.6 1.4 %collective-permute-done.9.m3 = f32[8,16,128]{2,1,0:T(8,128)S(1)} collective-permute-done((f32[8,16,128]{2,1,0:T(8,128)S(1)}, f32[8,16,128]{2,1,0:T(8,128)S(1)}, u32[]{:S(2)}, u32[]{:S(2)}) %collective-permute-start.9) | collective-permute-done | bytes 65568 | tf_op jit(solution)/shard_map/ppermute | solution.py:453
  61.0 0.0 collective-permute-done.8.m2
  61.0 3.0 %collective-permute-done.7.m1 = f32[8,16,128]{2,1,0:T(8,128)S(1)} collective-permute-done((f32[8,16,128]{2,1,0:T(8,128)S(1)}, f32[8,16,128]{2,1,0:T(8,128)S(1)}, u32[]{:S(2)}, u32[]{:S(2)}) %collective-permute-start.7) | collective-permute-done | bytes 65568 | tf_op jit(solution)/shard_map/ppermute | solution.py:453
  64.0 0.0 collective-permute-done.6.m0
  64.0 4.7 %close.1 = (f32[16,128,128]{2,1,0:T(8,128)S(1)}, f32[16,72,128]{2,1,0:T(8,128)S(1)}, f32[64,2048]{1,0:T(8,128)}, f32[64,1024]{1,0:T(8,128)S(1)}, f32[64,1024]{1,0:T(8,128)S(1)}) custom-call(f32[8,16,128]{2,1,0:T(8,128)S(1)} %collective-permute-done.6.m0, f32[8,16,128]{2,1,0:T(8,128)S(1)} %collective-permute-done.7.m1, ...), custom_call_target="tpu_custom_call", output_to_operand_aliasing={{0}: (7, {}), {1}: (10, {})} | custom-call | tf_op jit(solution)/shard_map/close/pallas_call | solution.py:433
  68.7 5.1 %collective-permute-start.10 = (f32[64,1024]{1,0:T(8,128)S(1)}, f32[64,1024]{1,0:T(8,128)S(1)}, u32[]{:S(2)}, u32[]{:S(2)}) collective-permute-start(f32[64,1024]{1,0:T(8,128)S(1)} %get-tuple-element.44), channel_id=1, source_target_pairs={{0,64},{64,0},{1,65},{65,1},{2,66},{66,2},{3,67},{67,3},{4,68},{68... | collective-permute-start | bytes 786440 | tf_op jit(solution)/shard_map/ppermute | solution.py:496
  73.8 1.2 %collective-permute-done.10 = f32[64,1024]{1,0:T(8,128)S(1)} collective-permute-done((f32[64,1024]{1,0:T(8,128)S(1)}, f32[64,1024]{1,0:T(8,128)S(1)}, u32[]{:S(2)}, u32[]{:S(2)}) %collective-permute-start.10) | collective-permute-done | bytes 262176 | tf_op jit(solution)/shard_map/ppermute | solution.py:496
  74.9 0.9 %multiply_subtract_fusion = (f32[64,1024]{1,0:T(8,128)}, f32[64,1024]{1,0:T(8,128)}) fusion(f32[64,1024]{1,0:T(8,128)S(1)} %collective-permute-done.10, f32[64,1024]{1,0:T(8,128)S(1)} %get-tuple-element.43), kind=kLoop, calls=%fused_computation | loop fusion | flops 458752 | bytes 1048576 | tf_op jit(solution)/shard_map/sub | solution.py:500
Async XLA Ops:
  0.6 1.0 %copy-start = (f32[1,64,2048]{2,1,0:T(8,128)S(1)}, f32[1,64,2048]{2,1,0:T(8,128)}, u32[]{:S(2)}) copy-start(f32[1,64,2048]{2,1,0:T(8,128)} %param.2) | copy-start | bytes 1572868
  1.7 1.0 %copy-start.1 = (f32[1,64,2048]{2,1,0:T(8,128)S(1)}, f32[1,64,2048]{2,1,0:T(8,128)}, u32[]{:S(2)}) copy-start(f32[1,64,2048]{2,1,0:T(8,128)} %param.3) | copy-start | bytes 1572868
  5.8 10.5 %collective-permute-start = (f32[32,24,128]{2,1,0:T(8,128)S(1)}, f32[32,24,128]{2,1,0:T(8,128)S(1)}, u32[]{:S(2)}, u32[]{:S(2)}) collective-permute-start(f32[32,24,128]{2,1,0:T(8,128)S(1)} %get-tuple-element.26), channel_id=1, source_target_pairs={{0,1},{1,0},{2,3},{3,2},{4,5},{5,4},{6,7},{7,6},{8,9},{9,8},{10,11... | collective-permute-start | bytes 1179656 | tf_op jit(solution)/shard_map/ppermute | solution.py:465
  7.9 16.3 %collective-permute-start.1 = (f32[32,24,128]{2,1,0:T(8,128)S(1)}, f32[32,24,128]{2,1,0:T(8,128)S(1)}, u32[]{:S(2)}, u32[]{:S(2)}) collective-permute-start(f32[32,24,128]{2,1,0:T(8,128)S(1)} %get-tuple-element.27), channel_id=1, source_target_pairs={{1,2},{2,1},{3,4},{4,3},{5,6},{6,5},{7,8},{8,7},{9,10},{10,9},{11,... | collective-permute-start | bytes 1179656 | tf_op jit(solution)/shard_map/ppermute | solution.py:465
  29.7 9.3 %collective-permute-start.5 = (f32[12,16,128]{2,1,0:T(8,128)S(1)}, f32[12,16,128]{2,1,0:T(8,128)S(1)}, u32[]{:S(2)}, u32[]{:S(2)}) collective-permute-start(f32[12,16,128]{2,1,0:T(8,128)S(1)} %get-tuple-element.28.m4), channel_id=1, source_target_pairs={{2,4},{3,5},{4,2},{5,3},{6,8},{7,9},{8,6},{9,7},{10,12},{11,13},{1... | collective-permute-start | bytes 294920 | tf_op jit(solution)/shard_map/ppermute | solution.py:453
  31.6 7.4 %collective-permute-start.4 = (f32[12,16,128]{2,1,0:T(8,128)S(1)}, f32[12,16,128]{2,1,0:T(8,128)S(1)}, u32[]{:S(2)}, u32[]{:S(2)}) collective-permute-start(f32[12,16,128]{2,1,0:T(8,128)S(1)} %get-tuple-element.28.m4), channel_id=1, source_target_pairs={{0,2},{1,3},{2,0},{3,1},{4,6},{5,7},{6,4},{7,5},{8,10},{9,11},{10,... | collective-permute-start | bytes 294920 | tf_op jit(solution)/shard_map/ppermute | solution.py:453
  31.6 12.2 %collective-permute-start.3 = (f32[12,16,128]{2,1,0:T(8,128)S(1)}, f32[12,16,128]{2,1,0:T(8,128)S(1)}, u32[]{:S(2)}, u32[]{:S(2)}) collective-permute-start(f32[12,16,128]{2,1,0:T(8,128)S(1)} %get-tuple-element.28.m4), channel_id=1, source_target_pairs={{1,2},{2,1},{3,4},{4,3},{5,6},{6,5},{7,8},{8,7},{9,10},{10,9},{11,... | collective-permute-start | bytes 294920 | tf_op jit(solution)/shard_map/ppermute | solution.py:453
  36.6 7.3 %collective-permute-start.2 = (f32[12,16,128]{2,1,0:T(8,128)S(1)}, f32[12,16,128]{2,1,0:T(8,128)S(1)}, u32[]{:S(2)}, u32[]{:S(2)}) collective-permute-start(f32[12,16,128]{2,1,0:T(8,128)S(1)} %get-tuple-element.28.m4), channel_id=1, source_target_pairs={{0,1},{1,0},{2,3},{3,2},{4,5},{5,4},{6,7},{7,6},{8,9},{9,8},{10,11... | collective-permute-start | bytes 294920 | tf_op jit(solution)/shard_map/ppermute | solution.py:453
  52.1 8.9 %collective-permute-start.9 = (f32[8,16,128]{2,1,0:T(8,128)S(1)}, f32[8,16,128]{2,1,0:T(8,128)S(1)}, u32[]{:S(2)}, u32[]{:S(2)}) collective-permute-start(f32[8,16,128]{2,1,0:T(8,128)S(1)} %get-tuple-element.35.m4), channel_id=1, source_target_pairs={{2,4},{3,5},{4,2},{5,3},{6,8},{7,9},{8,6},{9,7},{10,12},{11,13},{1... | collective-permute-start | bytes 196616 | tf_op jit(solution)/shard_map/ppermute | solution.py:453
  52.1 8.8 %collective-permute-start.8 = (f32[8,16,128]{2,1,0:T(8,128)S(1)}, f32[8,16,128]{2,1,0:T(8,128)S(1)}, u32[]{:S(2)}, u32[]{:S(2)}) collective-permute-start(f32[8,16,128]{2,1,0:T(8,128)S(1)} %get-tuple-element.35.m4), channel_id=1, source_target_pairs={{0,2},{1,3},{2,0},{3,1},{4,6},{5,7},{6,4},{7,5},{8,10},{9,11},{10,... | collective-permute-start | bytes 196616 | tf_op jit(solution)/shard_map/ppermute | solution.py:453
  55.0 9.0 %collective-permute-start.7 = (f32[8,16,128]{2,1,0:T(8,128)S(1)}, f32[8,16,128]{2,1,0:T(8,128)S(1)}, u32[]{:S(2)}, u32[]{:S(2)}) collective-permute-start(f32[8,16,128]{2,1,0:T(8,128)S(1)} %get-tuple-element.35.m4), channel_id=1, source_target_pairs={{1,2},{2,1},{3,4},{4,3},{5,6},{6,5},{7,8},{8,7},{9,10},{10,9},{11,... | collective-permute-start | bytes 196616 | tf_op jit(solution)/shard_map/ppermute | solution.py:453
  59.2 4.8 %collective-permute-start.6 = (f32[8,16,128]{2,1,0:T(8,128)S(1)}, f32[8,16,128]{2,1,0:T(8,128)S(1)}, u32[]{:S(2)}, u32[]{:S(2)}) collective-permute-start(f32[8,16,128]{2,1,0:T(8,128)S(1)} %get-tuple-element.35.m4), channel_id=1, source_target_pairs={{0,1},{1,0},{2,3},{3,2},{4,5},{5,4},{6,7},{7,6},{8,9},{9,8},{10,11... | collective-permute-start | bytes 196616 | tf_op jit(solution)/shard_map/ppermute | solution.py:453
  68.7 6.2 %collective-permute-start.10 = (f32[64,1024]{1,0:T(8,128)S(1)}, f32[64,1024]{1,0:T(8,128)S(1)}, u32[]{:S(2)}, u32[]{:S(2)}) collective-permute-start(f32[64,1024]{1,0:T(8,128)S(1)} %get-tuple-element.44), channel_id=1, source_target_pairs={{0,64},{64,0},{1,65},{65,1},{2,66},{66,2},{3,67},{67,3},{4,68},{68... | collective-permute-start | bytes 786440 | tf_op jit(solution)/shard_map/ppermute | solution.py:496

commit v4 on v3

--- a/solution.py
+++ b/solution.py
@@ -61,19 +61,20 @@
     return 2.0 * a * b / (a + b)
 
 
-def make_weights(level, c_ref, a_ref, first_row, total_rows, source_ref=None, b_ref=None):
+def make_weights(level, c_ref, a_ref, peers, strips=None, source_ref=None, b_ref=None):
     tiles = TILES[level]
+    top, total_rows = first_row(level), peers * OWN[level]
 
     def body(i):
         c = [c_ref[t, at(i, PAD), :] for t in range(tiles)]
-        row = first_row + i * 8 + iota(0)
+        row = top + i * 8 + iota(0)
         lane = iota(1)
         inside = jnp.logical_and(row >= 0, row < total_rows)
-        _, east = side_values(c)
+        west, east = side_values(c)
+        west[0] = jnp.where(lane == 0, c[0], west[0])
+        east[-1] = jnp.where(lane == LANES - 1, c[-1], east[-1])
         w_east = [harmonic(a, b) for a, b in zip(c, east)]
-        w_west, _ = side_values(w_east)
-        w_west[0] = jnp.where(lane == 0, harmonic(c[0], c[0]), w_west[0])
-        w_east[-1] = jnp.where(lane == LANES - 1, harmonic(c[-1], c[-1]), w_east[-1])
+        w_west = [harmonic(c[0], west[0])] + w_east[:-1]
         for t in range(tiles):
             w_north = harmonic(c[t], jnp.where(row == 0, c[t], c_ref[t, at(i, PAD - 1), :]))
             w_south = harmonic(c[t], jnp.where(row == total_rows - 1, c[t], c_ref[t, at(i, PAD + 1), :]))
@@ -94,7 +95,7 @@
             if source_ref is not None:
                 b_ref[t, at(i, PAD), :] = gain * source_ref[t, at(i, PAD), :]
 
-    loop(STRIPS[level], body)
+    loop(strips or STRIPS[level], body, UNROLL[level])
 
 
 def sweep(level, v_ref, out_ref, b_ref, a_ref, finish, strips):
@@ -200,17 +201,34 @@
     )
 
 
-def pack_kernel(log_ref, src_ref, c0, s0, first_ref, second_ref):
-    halo, own = HALO[0], OWN[0]
+def convert(rows_of, log_ref, src_ref, c0, s0):
     tiles = TILES[0]
-
-    def body(i):
-        logs, sources = ([ref[at(i, 0), t * LANES : (t + 1) * LANES] for t in range(tiles)] for ref in (log_ref, src_ref))
+    for row, to in rows_of:
+        logs, sources = ([ref[row : row + 8, t * LANES : (t + 1) * LANES] for t in range(tiles)] for ref in (log_ref, src_ref))
         for ref, x in zip((c0, s0), turn(([jnp.exp(v) for v in logs], sources))):
             for t, v in enumerate(x):
-                ref[t, at(i, PAD + halo), :] = v
-
-    loop(own // 8, body)
+                ref[t, to : to + 8, :] = v
+
+
+def load(sems, *pairs):
+    copies = [pltpu.make_async_copy(src, dst, sems.at[k]) for k, (src, dst) in enumerate(pairs)]
+    for copy in copies:
+        copy.start()
+    return copies
+
+
+def pack_kernel(log_in, src_in, c0, s0, first_ref, second_ref, logs, sources, sems):
+    halo, own, tiles = HALO[0], OWN[0], TILES[0]
+    pairs = []
+    for start in (0, own - halo):
+        to = pl.ds(0 if start == 0 else halo, halo)
+        pairs += [(ref.at[pl.ds(start, halo), :], dst.at[to, :]) for ref, dst in ((log_in, logs), (src_in, sources))]
+    copies = load(sems, *pairs)
+    for side in range(2):
+        for copy in copies[2 * side : 2 * side + 2]:
+            copy.wait()
+        base = PAD + halo + side * (own - halo)
+        convert([(side * halo + k, base + k) for k in range(0, halo, 8)], logs, sources, c0, s0)
     next_first, _ = towards_next()
     start = jnp.where(next_first, own - halo, 0)
     for ref, base in ((first_ref, start), (second_ref, own - halo - start)):
@@ -221,6 +239,20 @@
                 ref[tiles + t, 8 * i : 8 * i + 8, :] = s0[t, rows, :]
 
 
+def inner_kernel(peers, log_in, src_in, c0_in, s0_in, c0, s0, a0, bp0, va0, c1, logs, sources, sems):
+    halo, own, tiles = HALO[0], OWN[0], TILES[0]
+    inner = pl.ds(halo, own - 2 * halo)
+    copies = load(sems, (log_in.at[inner, :], logs), (src_in.at[inner, :], sources))
+    clear_pads(c0, c1, value=1.0)
+    clear_pads(s0, bp0, va0)
+    for copy in copies:
+        copy.wait()
+    convert([(k, PAD + 2 * halo + k) for k in range(0, own - 2 * halo, 8)], logs, sources, c0, s0)
+    make_weights(0, c0, a0, peers, (4, 10), s0, bp0)
+    restrict((2, 5), c0, PAD, range(tiles), quarter_store(c1))
+    relax(0, bp0, va0, bp0, a0, (5, 9))
+
+
 def scaled_store(bp_ref, a_ref, start=0):
     def store(j, k, q):
         bp_ref[start + k, at(j, PAD), :] = a_ref[4, k, at(j, 0), :] * q
@@ -236,9 +268,9 @@
 
 
 def open_kernel(
-    peers, c0_in, s0_in, first_ref, second_ref,
-    c0, s0, msg_ref, a0, bp0, va0, a1, bp1, va1,
-    vb0, c1, vb1,
+    peers, c0_in, s0_in, a0_in, b0_in, v0_in, c1_in, first_ref, second_ref,
+    c0, s0, a0, bp0, va0, c1, msg_ref, a1, bp1, va1,
+    vb0, vb1,
 ):
     halo, own, tiles = HALO[0], OWN[0], TILES[0]
     next_first, _ = towards_next()
@@ -249,13 +281,15 @@
             for t in range(tiles):
                 c0[t, rows, :] = ref[t, 8 * i : 8 * i + 8, :]
                 s0[t, rows, :] = ref[tiles + t, 8 * i : 8 * i + 8, :]
-    clear_pads(c0, c1, value=1.0)
-    clear_pads(bp0, va0, vb0, bp1, va1, vb1)
-    make_weights(0, c0, a0, first_row(0), peers * OWN[0], s0, bp0)
-    restrict(STRIPS[1], c0, PAD, range(tiles), quarter_store(c1))
-    make_weights(1, c1, a1, first_row(1), peers * OWN[1])
+    clear_pads(vb0, bp1, va1, vb1)
+    for strips in ((0, 4), (10, 14)):
+        make_weights(0, c0, a0, peers, strips, s0, bp0)
+    for strips in ((0, 2), (5, 7)):
+        restrict(strips, c0, PAD, range(tiles), quarter_store(c1), 2)
+    make_weights(1, c1, a1, peers)
     restrict(STRIPS[1], s0, PAD, range(tiles), scaled_store(bp1, a1, TILES[1]))
-    relax(0, bp0, va0, bp0, a0)
+    for strips in ((0, 5), (9, 14)):
+        relax(0, bp0, va0, bp0, a0, strips)
     residual(0, va0, vb0, bp0, a0)
     restrict(STRIPS[1], vb0, PAD, range(tiles), scaled_store(bp1, a1))
     relax(1, bp1, va1, bp1, a1)
@@ -327,22 +361,21 @@
         fill(ref, 0.0)
     clear_pads(bp2, va2, vb2, bp3, va3, vb3)
     clear_pads(vb0, vb1, size=2 * PAD)
-    top = first_row(2)
     for position, m in zip(slab_positions(), messages):
         for i in range(2):
             row = pl.multiple_of(position * OWN[2] + i * 8, 8)
             for k in range(TILES[2]):
                 c2[k, pl.ds(PAD + row, 8), :] = m[2 * TILES[2] + k, i * 8 : i * 8 + 8, :]
-    make_weights(2, c2, a2, top, peers * OWN[2])
+    make_weights(2, c2, a2, peers)
     restrict(STRIPS[3], c2, PAD, range(4), quarter_store(c3), 5)
-    make_weights(3, c3, a3, first_row(3), peers * OWN[3])
+    make_weights(3, c3, a3, peers)
     restrict(2, c3, PAD, range(2), quarter_store(c4), 2)
 
     def last_rows(j, k, q):
         c4[k, PAD + 16 : PAD + 24, :] = jnp.where(iota(0) < ROWS[4] - 16, 0.25 * q, 1.0)
 
     restrict(1, c3, PAD + 32, range(2), last_rows)
-    make_weights(4, c4, a4, first_row(4), peers * OWN[4])
+    make_weights(4, c4, a4, peers)
     assemble(messages, a2, bp2)
     a = {2: a2, 3: a3, 4: a4}
     bp = {2: bp2, 3: bp3, 4: bp4}
@@ -373,8 +406,8 @@
 
 def close_kernel(
     m0, m1, m2, m3, m4, a0, bp0, va0_in, a1, bp1, va1_in, a2, a3, a4,
-    va0, va1, out_ref, mine_ref, other_ref,
-    vb0, vb1, bp2, va2, vb2, bp3, va3, vb3, bp4, va4, vb4,
+    va0, va1, out_hbm, mine_ref, other_ref,
+    vb0, vb1, bp2, va2, vb2, bp3, va3, vb3, bp4, va4, vb4, out_ref, sems,
 ):
     for ref in (bp4, va4, vb4):
         fill(ref, 0.0)
@@ -392,8 +425,9 @@
     tiles = TILES[0]
     left = lax.axis_index("samp") == 0
 
-    def body(i):
-        strips = (2 * i, 2 * i + 1)
+    copies = []
+    for piece in range(OWN[0] // 16):
+        strips = (2 * piece, 2 * piece + 1)
         turned = turn([[va0[t, at(j, PAD + HALO[0]), :] for t in range(tiles)] for j in strips])
         for j, x in zip(strips, turned):
             for t in range(tiles):
@@ -402,8 +436,11 @@
                 low, high = x[t], x[tiles // 2 + t]
                 mine_ref[at(j, 0), t * LANES : (t + 1) * LANES] = jnp.where(left, low, high)
                 other_ref[at(j, 0), t * LANES : (t + 1) * LANES] = jnp.where(left, high, low)
-
-    loop(OWN[0] // 16, body)
+        rows = pl.ds(16 * piece, 16)
+        copies.append(pltpu.make_async_copy(out_ref.at[rows, :], out_hbm.at[rows, :], sems.at[piece]))
+        copies[-1].start()
+    for copy in copies:
+        copy.wait()
 
 
 VMEM = pl.BlockSpec(memory_space=pltpu.VMEM)
@@ -429,15 +466,19 @@
     return (TILES[level], BUF[level], LANES)
 
 
-def call(kernel, name, arguments, outputs, scratch=(), aliases=None):
+FAR = pl.BlockSpec(memory_space=pltpu.HBM)
+
+
+def call(kernel, name, arguments, outputs, scratch=(), aliases=None, sems=0, far=0):
     return pl.pallas_call(
         kernel,
         out_shape=outputs,
-        in_specs=[VMEM] * len(arguments),
-        out_specs=[VMEM] * len(outputs),
-        scratch_shapes=[pltpu.VMEM(s, F32) for s in scratch],
+        in_specs=[FAR] * far + [VMEM] * (len(arguments) - far),
+        out_specs=[FAR if isinstance(o, jax.ShapeDtypeStruct) else VMEM for o in outputs],
+        scratch_shapes=[pltpu.VMEM(s, F32) for s in scratch] + ([pltpu.SemaphoreType.DMA((sems,))] if sems else []),
         input_output_aliases=aliases or {},
         compiler_params=pltpu.CompilerParams(vmem_limit_bytes=24 * 2**20),
+        cost_estimate=pl.CostEstimate(flops=10**8, bytes_accessed=10**6, transcendentals=0),
         name=name,
     )(*arguments)
 
@@ -445,7 +486,9 @@
 def swaps(distance):
     peers = lax.axis_size("grid")
     even = [(i, i + distance if i % (2 * distance) < distance else i - distance) for i in range(peers)]
-    odd = [((a + distance) % peers, (b + distance) % peers) for a, b in even]
+    odd = [(a + distance, b + distance) for a, b in even if max(a, b) + distance < peers]
+    last = peers - 1
+    odd += [(0, last), (last, 0)] if distance == 1 else [(0, 1), (1, 0), (last - 1, last), (last, last - 1)]
     return even, odd
 
 
@@ -458,20 +501,28 @@
     log_field, source_field = log_coef[0], source[0]
     rows, columns = source_field.shape
     edge = near(2 * TILES[0], HALO[0], LANES)
+    fields = [pltpu.with_memory_space_constraint(x, pltpu.HBM) for x in (log_field, source_field)]
     c0, s0, first, second = call(
-        pack_kernel, "pack", (log_field, source_field), (near(*c_shape(0)), near(*c_shape(0)), edge, edge)
+        pack_kernel, "pack", fields, (near(*c_shape(0)), near(*c_shape(0)), edge, edge),
+        [(2 * HALO[0], columns)] * 2, sems=4, far=2,
     )
     even, odd = swaps(1)
     first, second = lax.ppermute(first, "grid", even), lax.ppermute(second, "grid", odd)
 
     state = [near(*f(level)) for level in (0, 1) for f in (a_shape, v_shape, v_shape)]
-    c0, s0, message, a0, b0, v0, a1, b1, v1 = call(
+    whole = [near(*c_shape(0)), near(*c_shape(0))] + state[:3] + [near(*c_shape(1))]
+    middle_rows = rows - 2 * HALO[0]
+    started = call(
+        functools.partial(inner_kernel, peers), "inner", [*fields, *held(c0, s0)], whole,
+        [(middle_rows, columns)] * 2, {2: 0, 3: 1}, sems=2, far=2,
+    )
+    c0, s0, a0, b0, v0, c1, message, a1, b1, v1 = call(
         functools.partial(open_kernel, peers),
         "open",
-        held(c0, s0, first, second),
-        [near(*c_shape(0)), near(*c_shape(0)), near(3 * TILES[2], OWN[2], LANES)] + state,
-        [v_shape(0), c_shape(1), v_shape(1)],
-        {0: 0, 1: 1},
+        held(*started, first, second),
+        whole + [near(3 * TILES[2], OWN[2], LANES)] + state[3:],
+        [v_shape(0), v_shape(1)],
+        {k: k for k in range(6)},
     )
     deep = [shape for level in (2, 3, 4) for shape in [c_shape(level)] + [v_shape(level)] * 3]
     message, a2, a3, a4, v0, b1, v1 = call(
@@ -489,8 +540,9 @@
         "close",
         held(*gathered(message), a0, b0, v0, a1, b1, v1, a2, a3, a4),
         (state[2], state[5], jax.ShapeDtypeStruct((rows, columns), F32), half, half),
-        [v_shape(0), v_shape(1)] + deep,
+        [v_shape(0), v_shape(1)] + deep + [(rows, columns)],
         {7: 0, 10: 1},
+        sems=rows // 16,
     )
 
     theirs = lax.ppermute(other, "samp", [(0, 1), (1, 0)])

time: 76 us -> 63.4 us (0.83)
  waiting for transfers between devices: 20.9 us -> 14.4 us
  Pallas kernels: 21.5 us -> 17.4 us
  local copies, waits for them, and re-layouts: 2.08 us -> 0 us
    ppermute x8, waiting for transfers between devices: 11.2 us -> 6.86 us  [gathered(): lax.ppermute(value, 'grid', pairs)]
    pallas_call x4 -> x5, Pallas kernels: 21.5 us -> 17.4 us  [call(): pl.pallas_call(kernel, out_shape=outputs, in_specs=[FAR] * far + [VMEM] *...]
    unnamed x4 -> x0, local copies, waits for them, and re-layouts: 2.08 us -> none
    ppermute x1, waiting for transfers between devices: 7.88 us -> 6.37 us  [local(): lax.ppermute(second, 'grid', odd)]
    ppermute x1, starting transfers between devices: 5.08 us -> 5.87 us  [local(): theirs = lax.ppermute(other, 'samp', [(0, 1), (1, 0)])]
  transfers between devices with their start and end apart: 11 -> 11, of which waited for: 7 -> 6; matrix products, arithmetic and copies ran while one was open for 0% -> 0% of each run, Pallas kernels for 0% -> 3%
where the time goes in v4:
time: 63.4 us; the launch traced here: 63.2 us
  starting transfers between devices  29.9 us (47%)
  Pallas kernels  17.4 us (27%)
  waiting for transfers between devices  14.4 us (23%)
  other arithmetic  0.86 us (1%)
  between operations  0.7 us (1%)
    pallas_call x5, Pallas kernels, call(): pl.pallas_call(kernel, out_shape=outputs, in_specs=[FAR] * far + [VMEM] *...  17.4 us
    ppermute x8, starting transfers between devices, gathered(): lax.ppermute(value, 'grid', pairs)  14.2 us
    ppermute x1, starting transfers between devices, local(): lax.ppermute(second, 'grid', odd)  7.74 us
    ppermute x8, waiting for transfers between devices, gathered(): lax.ppermute(value, 'grid', pairs)  6.86 us
    ppermute x1, waiting for transfers between devices, local(): lax.ppermute(second, 'grid', odd)  6.37 us
    ppermute x1, starting transfers between devices, local(): theirs = lax.ppermute(other, 'samp', [(0, 1), (1, 0)])  5.87 us
    ppermute x1, starting transfers between devices, local(): lax.ppermute(first, 'grid', even)  2.1 us
  transfers between devices with their start and end apart: 11, of which 6 were waited for; matrix products, arithmetic and copies ran while one was open for 0% of the time, Pallas kernels for 3%

profile of v4, /device:TPU:1, one launch (start us, length us, event | category | flops | bytes accessed | tf_op | source)
XLA Modules:
  0.0 63.2 jit_solution(16128478892997520850)
XLA Ops:
  0.6 2.7 %pack.1 = (f32[16,128,128]{2,1,0:T(8,128)S(1)}, f32[16,128,128]{2,1,0:T(8,128)S(1)}, f32[32,24,128]{2,1,0:T(8,128)S(1)}, f32[32,24,128]{2,1,0:T(8,128)S(1)}) custom-call(f32[64,2048]{1,0:T(8,128)} %bitcast.3, f32[64,2048]{1,0:T(8,128)} %bitcast.5), custom_call_target="tpu_custom_call" | custom-call | flops 100000000 | bytes 1000000 | tf_op jit(solution)/shard_map/pack/pallas_call | solution.py:473
  3.3 2.1 %collective-permute-start = (f32[32,24,128]{2,1,0:T(8,128)S(1)}, f32[32,24,128]{2,1,0:T(8,128)S(1)}, u32[]{:S(2)}, u32[]{:S(2)}) collective-permute-start(f32[32,24,128]{2,1,0:T(8,128)S(1)} %get-tuple-element.38), channel_id=1, source_target_pairs={{0,1},{1,0},{2,3},{3,2},{4,5},{5,4},{6,7},{7,6},{8,9},{9,8},{10,11... | collective-permute-start | bytes 1179656 | tf_op jit(solution)/shard_map/ppermute | solution.py:510
  5.4 7.7 %collective-permute-start.1 = (f32[32,24,128]{2,1,0:T(8,128)S(1)}, f32[32,24,128]{2,1,0:T(8,128)S(1)}, u32[]{:S(2)}, u32[]{:S(2)}) collective-permute-start(f32[32,24,128]{2,1,0:T(8,128)S(1)} %get-tuple-element.39), channel_id=1, source_target_pairs={{1,2},{2,1},{3,4},{4,3},{5,6},{6,5},{7,8},{8,7},{9,10},{10,9},{11,... | collective-permute-start | bytes 1179656 | tf_op jit(solution)/shard_map/ppermute | solution.py:510
  13.2 2.1 %inner.1 = (f32[16,128,128]{2,1,0:T(8,128)S(1)}, f32[16,128,128]{2,1,0:T(8,128)S(1)}, f32[6,16,112,128]{3,2,1,0:T(8,128)S(1)}, f32[16,128,128]{2,1,0:T(8,128)S(1...) custom-call(f32[64,2048]{1,0:T(8,128)} %bitcast.4, ...), custom_call_target="tpu_custom_call", output_to_operand_aliasing={{0}: (2, {}), {1}: (3, {})} | custom-call | flops 100000000 | bytes 1000000 | tf_op jit(solution)/shard_map/inner/pallas_call | solution.py:473
  15.3 0.0 collective-permute-done.first_ref
  15.3 6.4 %collective-permute-done.1.second_ref = f32[32,24,128]{2,1,0:T(8,128)S(1)} collective-permute-done((f32[32,24,128]{2,1,0:T(8,128)S(1)}, f32[32,24,128]{2,1,0:T(8,128)S(1)}, u32[]{:S(2)}, u32[]{:S(2)}) %collective-permute-start.1) | collective-permute-done | bytes 393248 | tf_op jit(solution)/shard_map/ppermute | solution.py:510
  21.7 2.6 %open.1 = (f32[16,128,128]{2,1,0:T(8,128)S(1)}, f32[16,128,128]{2,1,0:T(8,128)S(1)}, f32[6,16,112,128]{3,2,1,0:T(8,128)S(1)}, f32[16,128,128]{2,1,0:T(8,128)S(1)...) custom-call(f32[16,128,128]{2,1,0:T(8,128)S(1)} %get-tuple-element.3, ...), custom_call_target="tpu_custom_call", output_to_operand_aliasing={{0}: (0, {}), {1}: (1, {}), {2}: (2, {}), {3}: (3, {}), {4}... | custom-call | flops 100000000 | bytes 1000000 | tf_op jit(solution)/shard_map/open/pallas_call | solution.py:473
  24.3 0.1 collective-permute-start.5
  24.4 0.1 collective-permute-start.4
  24.5 6.7 %collective-permute-start.3 = (f32[12,16,128]{2,1,0:T(8,128)S(1)}, f32[12,16,128]{2,1,0:T(8,128)S(1)}, u32[]{:S(2)}, u32[]{:S(2)}) collective-permute-start(f32[12,16,128]{2,1,0:T(8,128)S(1)} %get-tuple-element.40.m4), channel_id=1, source_target_pairs={{1,2},{2,1},{3,4},{4,3},{5,6},{6,5},{7,8},{8,7},{9,10},{10,9},{11,... | collective-permute-start | bytes 294920 | tf_op jit(solution)/shard_map/ppermute | solution.py:496
  31.2 0.0 collective-permute-start.2
  31.2 0.0 collective-permute-done.5.m3
  31.2 0.0 collective-permute-done.4.m2
  31.2 2.3 %collective-permute-done.3.m1 = f32[12,16,128]{2,1,0:T(8,128)S(1)} collective-permute-done((f32[12,16,128]{2,1,0:T(8,128)S(1)}, f32[12,16,128]{2,1,0:T(8,128)S(1)}, u32[]{:S(2)}, u32[]{:S(2)}) %collective-permute-start.3) | collective-permute-done | bytes 98336 | tf_op jit(solution)/shard_map/ppermute | solution.py:496
  33.5 1.5 %collective-permute-done.2.m0 = f32[12,16,128]{2,1,0:T(8,128)S(1)} collective-permute-done((f32[12,16,128]{2,1,0:T(8,128)S(1)}, f32[12,16,128]{2,1,0:T(8,128)S(1)}, u32[]{:S(2)}, u32[]{:S(2)}) %collective-permute-start.2) | collective-permute-done | bytes 98336 | tf_op jit(solution)/shard_map/ppermute | solution.py:496
  34.9 5.6 %middle.1 = (f32[8,16,128]{2,1,0:T(8,128)S(1)}, f32[6,4,80,128]{3,2,1,0:T(8,128)S(1)}, f32[6,2,40,128]{3,2,1,0:T(8,128)S(1)}, f32[6,1,24,128]{3,2,1,0:T(8,128)S(...) custom-call(f32[12,16,128]{2,1,0:T(8,128)S(1)} %collective-permute-d, ...), custom_call_target="tpu_custom_call", output_to_operand_aliasing={{4}: (7, {}), {5}: (9, {}), {6}: (10, {})} | custom-call | flops 100000000 | bytes 1000000 | tf_op jit(solution)/shard_map/middle/pallas_call | solution.py:473
  40.5 0.1 collective-permute-start.9
  40.6 0.9 %collective-permute-start.8 = (f32[8,16,128]{2,1,0:T(8,128)S(1)}, f32[8,16,128]{2,1,0:T(8,128)S(1)}, u32[]{:S(2)}, u32[]{:S(2)}) collective-permute-start(f32[8,16,128]{2,1,0:T(8,128)S(1)} %get-tuple-element.47.m4), channel_id=1, source_target_pairs={{0,2},{1,3},{2,0},{3,1},{4,6},{5,7},{6,4},{7,5},{8,10},{9,11},{10,... | collective-permute-start | bytes 196616 | tf_op jit(solution)/shard_map/ppermute | solution.py:496
  41.6 6.3 %collective-permute-start.7 = (f32[8,16,128]{2,1,0:T(8,128)S(1)}, f32[8,16,128]{2,1,0:T(8,128)S(1)}, u32[]{:S(2)}, u32[]{:S(2)}) collective-permute-start(f32[8,16,128]{2,1,0:T(8,128)S(1)} %get-tuple-element.47.m4), channel_id=1, source_target_pairs={{1,2},{2,1},{3,4},{4,3},{5,6},{6,5},{7,8},{8,7},{9,10},{10,9},{11,... | collective-permute-start | bytes 196616 | tf_op jit(solution)/shard_map/ppermute | solution.py:496
  47.9 0.0 collective-permute-start.6
  47.9 0.0 collective-permute-done.9.m3
  47.9 0.0 collective-permute-done.8.m2
  47.9 2.2 %collective-permute-done.7.m1 = f32[8,16,128]{2,1,0:T(8,128)S(1)} collective-permute-done((f32[8,16,128]{2,1,0:T(8,128)S(1)}, f32[8,16,128]{2,1,0:T(8,128)S(1)}, u32[]{:S(2)}, u32[]{:S(2)}) %collective-permute-start.7) | collective-permute-done | bytes 65568 | tf_op jit(solution)/shard_map/ppermute | solution.py:496
  50.1 0.9 %collective-permute-done.6.m0 = f32[8,16,128]{2,1,0:T(8,128)S(1)} collective-permute-done((f32[8,16,128]{2,1,0:T(8,128)S(1)}, f32[8,16,128]{2,1,0:T(8,128)S(1)}, u32[]{:S(2)}, u32[]{:S(2)}) %collective-permute-start.6) | collective-permute-done | bytes 65568 | tf_op jit(solution)/shard_map/ppermute | solution.py:496
  51.0 4.4 %close.1 = (f32[16,128,128]{2,1,0:T(8,128)S(1)}, f32[16,72,128]{2,1,0:T(8,128)S(1)}, f32[64,2048]{1,0:T(8,128)}, f32[64,1024]{1,0:T(8,128)S(1)}, f32[64,1024]{1,0:T(8,128)S(1)}) custom-call(f32[8,16,128]{2,1,0:T(8,128)S(1)} %collective-permute-done.6.m0, f32[8,16,128]{2,1,0:T(8,128)S(1)} %collective-permute-done.7.m1, ...), custom_call_target="tpu_custom_call", output_to_operand_aliasing={{0}: (7, {}), {1}: (10, {})} | custom-call | flops 100000000 | bytes 1000000 | tf_op jit(solution)/shard_map/close/pallas_call | solution.py:473
  55.3 5.9 %collective-permute-start.10 = (f32[64,1024]{1,0:T(8,128)S(1)}, f32[64,1024]{1,0:T(8,128)S(1)}, u32[]{:S(2)}, u32[]{:S(2)}) collective-permute-start(f32[64,1024]{1,0:T(8,128)S(1)} %get-tuple-element.56), channel_id=1, source_target_pairs={{0,64},{64,0},{1,65},{65,1},{2,66},{66,2},{3,67},{67,3},{4,68},{68... | collective-permute-start | bytes 786440 | tf_op jit(solution)/shard_map/ppermute | solution.py:548
  61.2 1.2 %collective-permute-done.10 = f32[64,1024]{1,0:T(8,128)S(1)} collective-permute-done((f32[64,1024]{1,0:T(8,128)S(1)}, f32[64,1024]{1,0:T(8,128)S(1)}, u32[]{:S(2)}, u32[]{:S(2)}) %collective-permute-start.10) | collective-permute-done | bytes 262176 | tf_op jit(solution)/shard_map/ppermute | solution.py:548
  62.4 0.9 %multiply_subtract_fusion = (f32[64,1024]{1,0:T(8,128)}, f32[64,1024]{1,0:T(8,128)}) fusion(f32[64,1024]{1,0:T(8,128)S(1)} %collective-permute-done.10, f32[64,1024]{1,0:T(8,128)S(1)} %get-tuple-element.55), kind=kLoop, calls=%fused_computation | loop fusion | flops 458752 | bytes 1048576 | tf_op jit(solution)/shard_map/sub | solution.py:552
Async XLA Ops:
  3.3 12.0 %collective-permute-start = (f32[32,24,128]{2,1,0:T(8,128)S(1)}, f32[32,24,128]{2,1,0:T(8,128)S(1)}, u32[]{:S(2)}, u32[]{:S(2)}) collective-permute-start(f32[32,24,128]{2,1,0:T(8,128)S(1)} %get-tuple-element.38), channel_id=1, source_target_pairs={{0,1},{1,0},{2,3},{3,2},{4,5},{5,4},{6,7},{7,6},{8,9},{9,8},{10,11... | collective-permute-start | bytes 1179656 | tf_op jit(solution)/shard_map/ppermute | solution.py:510
  5.4 16.3 %collective-permute-start.1 = (f32[32,24,128]{2,1,0:T(8,128)S(1)}, f32[32,24,128]{2,1,0:T(8,128)S(1)}, u32[]{:S(2)}, u32[]{:S(2)}) collective-permute-start(f32[32,24,128]{2,1,0:T(8,128)S(1)} %get-tuple-element.39), channel_id=1, source_target_pairs={{1,2},{2,1},{3,4},{4,3},{5,6},{6,5},{7,8},{8,7},{9,10},{10,9},{11,... | collective-permute-start | bytes 1179656 | tf_op jit(solution)/shard_map/ppermute | solution.py:510
  24.3 6.9 %collective-permute-start.5 = (f32[12,16,128]{2,1,0:T(8,128)S(1)}, f32[12,16,128]{2,1,0:T(8,128)S(1)}, u32[]{:S(2)}, u32[]{:S(2)}) collective-permute-start(f32[12,16,128]{2,1,0:T(8,128)S(1)} %get-tuple-element.40.m4), channel_id=1, source_target_pairs={{2,4},{3,5},{4,2},{5,3},{6,8},{7,9},{8,6},{9,7},{10,12},{11,13},{1... | collective-permute-start | bytes 294920 | tf_op jit(solution)/shard_map/ppermute | solution.py:496
  24.4 6.8 %collective-permute-start.4 = (f32[12,16,128]{2,1,0:T(8,128)S(1)}, f32[12,16,128]{2,1,0:T(8,128)S(1)}, u32[]{:S(2)}, u32[]{:S(2)}) collective-permute-start(f32[12,16,128]{2,1,0:T(8,128)S(1)} %get-tuple-element.40.m4), channel_id=1, source_target_pairs={{0,2},{1,3},{2,0},{3,1},{4,6},{5,7},{6,4},{7,5},{8,10},{9,11},{10,... | collective-permute-start | bytes 294920 | tf_op jit(solution)/shard_map/ppermute | solution.py:496
  24.5 9.0 %collective-permute-start.3 = (f32[12,16,128]{2,1,0:T(8,128)S(1)}, f32[12,16,128]{2,1,0:T(8,128)S(1)}, u32[]{:S(2)}, u32[]{:S(2)}) collective-permute-start(f32[12,16,128]{2,1,0:T(8,128)S(1)} %get-tuple-element.40.m4), channel_id=1, source_target_pairs={{1,2},{2,1},{3,4},{4,3},{5,6},{6,5},{7,8},{8,7},{9,10},{10,9},{11,... | collective-permute-start | bytes 294920 | tf_op jit(solution)/shard_map/ppermute | solution.py:496
  31.2 3.8 %collective-permute-start.2 = (f32[12,16,128]{2,1,0:T(8,128)S(1)}, f32[12,16,128]{2,1,0:T(8,128)S(1)}, u32[]{:S(2)}, u32[]{:S(2)}) collective-permute-start(f32[12,16,128]{2,1,0:T(8,128)S(1)} %get-tuple-element.40.m4), channel_id=1, source_target_pairs={{0,1},{1,0},{2,3},{3,2},{4,5},{5,4},{6,7},{7,6},{8,9},{9,8},{10,11... | collective-permute-start | bytes 294920 | tf_op jit(solution)/shard_map/ppermute | solution.py:496
  40.5 7.3 %collective-permute-start.9 = (f32[8,16,128]{2,1,0:T(8,128)S(1)}, f32[8,16,128]{2,1,0:T(8,128)S(1)}, u32[]{:S(2)}, u32[]{:S(2)}) collective-permute-start(f32[8,16,128]{2,1,0:T(8,128)S(1)} %get-tuple-element.47.m4), channel_id=1, source_target_pairs={{2,4},{3,5},{4,2},{5,3},{6,8},{7,9},{8,6},{9,7},{10,12},{11,13},{1... | collective-permute-start | bytes 196616 | tf_op jit(solution)/shard_map/ppermute | solution.py:496
  40.6 7.2 %collective-permute-start.8 = (f32[8,16,128]{2,1,0:T(8,128)S(1)}, f32[8,16,128]{2,1,0:T(8,128)S(1)}, u32[]{:S(2)}, u32[]{:S(2)}) collective-permute-start(f32[8,16,128]{2,1,0:T(8,128)S(1)} %get-tuple-element.47.m4), channel_id=1, source_target_pairs={{0,2},{1,3},{2,0},{3,1},{4,6},{5,7},{6,4},{7,5},{8,10},{9,11},{10,... | collective-permute-start | bytes 196616 | tf_op jit(solution)/shard_map/ppermute | solution.py:496
  41.6 8.5 %collective-permute-start.7 = (f32[8,16,128]{2,1,0:T(8,128)S(1)}, f32[8,16,128]{2,1,0:T(8,128)S(1)}, u32[]{:S(2)}, u32[]{:S(2)}) collective-permute-start(f32[8,16,128]{2,1,0:T(8,128)S(1)} %get-tuple-element.47.m4), channel_id=1, source_target_pairs={{1,2},{2,1},{3,4},{4,3},{5,6},{6,5},{7,8},{8,7},{9,10},{10,9},{11,... | collective-permute-start | bytes 196616 | tf_op jit(solution)/shard_map/ppermute | solution.py:496
  47.9 3.1 %collective-permute-start.6 = (f32[8,16,128]{2,1,0:T(8,128)S(1)}, f32[8,16,128]{2,1,0:T(8,128)S(1)}, u32[]{:S(2)}, u32[]{:S(2)}) collective-permute-start(f32[8,16,128]{2,1,0:T(8,128)S(1)} %get-tuple-element.47.m4), channel_id=1, source_target_pairs={{0,1},{1,0},{2,3},{3,2},{4,5},{5,4},{6,7},{7,6},{8,9},{9,8},{10,11... | collective-permute-start | bytes 196616 | tf_op jit(solution)/shard_map/ppermute | solution.py:496
  55.3 7.0 %collective-permute-start.10 = (f32[64,1024]{1,0:T(8,128)S(1)}, f32[64,1024]{1,0:T(8,128)S(1)}, u32[]{:S(2)}, u32[]{:S(2)}) collective-permute-start(f32[64,1024]{1,0:T(8,128)S(1)} %get-tuple-element.56), channel_id=1, source_target_pairs={{0,64},{64,0},{1,65},{65,1},{2,66},{66,2},{3,67},{67,3},{4,68},{68... | collective-permute-start | bytes 786440 | tf_op jit(solution)/shard_map/ppermute | solution.py:548

commit v5 on v4

--- a/solution.py
+++ b/solution.py
@@ -6,6 +6,7 @@
 from jax.experimental import pallas as pl
 from jax.experimental.pallas import tpu as pltpu
 from jax.sharding import PartitionSpec as P
+
 
 LANES = 128
 PAD = 8
@@ -18,6 +19,7 @@
 SOLVES = (1, 2, 2, 2, 2)
 UNROLL = (2, 7, 5, 5, 3)
 DAMP = 0.8
+NEAR = 8
 F32 = jnp.float32
 
 
@@ -217,23 +219,32 @@
     return copies
 
 
-def pack_kernel(log_in, src_in, c0, s0, first_ref, second_ref, logs, sources, sems):
-    halo, own, tiles = HALO[0], OWN[0], TILES[0]
+def boundary_rows(near):
+    count = NEAR if near else HALO[0] - NEAR
+    start = 0 if near else NEAR
+    return (start, count), (OWN[0] - start - count, count)
+
+
+def pack_kernel(near, log_in, src_in, *refs):
+    c0, s0, first_ref, second_ref, logs, sources, sems = refs if near else refs[2:]
+    tiles = TILES[0]
+    sides = boundary_rows(near)
+    count = sides[0][1]
     pairs = []
-    for start in (0, own - halo):
-        to = pl.ds(0 if start == 0 else halo, halo)
-        pairs += [(ref.at[pl.ds(start, halo), :], dst.at[to, :]) for ref, dst in ((log_in, logs), (src_in, sources))]
+    for side, (start, _) in enumerate(sides):
+        to = pl.ds(side * count, count)
+        pairs += [(ref.at[pl.ds(start, count), :], dst.at[to, :]) for ref, dst in ((log_in, logs), (src_in, sources))]
     copies = load(sems, *pairs)
-    for side in range(2):
+    for side, (start, _) in enumerate(sides):
         for copy in copies[2 * side : 2 * side + 2]:
             copy.wait()
-        base = PAD + halo + side * (own - halo)
-        convert([(side * halo + k, base + k) for k in range(0, halo, 8)], logs, sources, c0, s0)
+        base = PAD + HALO[0] + start
+        convert([(side * count + k, base + k) for k in range(0, count, 8)], logs, sources, c0, s0)
     next_first, _ = towards_next()
-    start = jnp.where(next_first, own - halo, 0)
-    for ref, base in ((first_ref, start), (second_ref, own - halo - start)):
-        for i in range(halo // 8):
-            rows = pl.ds(pl.multiple_of(PAD + halo + base + 8 * i, 8), 8)
+    up, down = (PAD + HALO[0] + start for start, _ in sides)
+    for ref, base in ((first_ref, jnp.where(next_first, down, up)), (second_ref, jnp.where(next_first, up, down))):
+        for i in range(count // 8):
+            rows = pl.ds(pl.multiple_of(base + 8 * i, 8), 8)
             for t in range(tiles):
                 ref[t, 8 * i : 8 * i + 8, :] = c0[t, rows, :]
                 ref[tiles + t, 8 * i : 8 * i + 8, :] = s0[t, rows, :]
@@ -243,8 +254,9 @@
     halo, own, tiles = HALO[0], OWN[0], TILES[0]
     inner = pl.ds(halo, own - 2 * halo)
     copies = load(sems, (log_in.at[inner, :], logs), (src_in.at[inner, :], sources))
-    clear_pads(c0, c1, value=1.0)
-    clear_pads(s0, bp0, va0)
+    clear_pads(c0, value=1.0, size=PAD + halo)
+    clear_pads(s0, bp0, va0, size=PAD + halo)
+    clear_pads(c1, value=1.0)
     for copy in copies:
         copy.wait()
     convert([(k, PAD + 2 * halo + k) for k in range(0, own - 2 * halo, 8)], logs, sources, c0, s0)
@@ -253,46 +265,77 @@
     relax(0, bp0, va0, bp0, a0, (5, 9))
 
 
-def scaled_store(bp_ref, a_ref, start=0):
-    def store(j, k, q):
-        bp_ref[start + k, at(j, PAD), :] = a_ref[4, k, at(j, 0), :] * q
-
-    return store
-
-
-def quarter_store(c_ref):
-    def store(j, k, q):
-        c_ref[k, at(j, PAD), :] = 0.25 * q
-
-    return store
-
-
-def open_kernel(
-    peers, c0_in, s0_in, a0_in, b0_in, v0_in, c1_in, first_ref, second_ref,
-    c0, s0, a0, bp0, va0, c1, msg_ref, a1, bp1, va1,
-    vb0, vb1,
-):
-    halo, own, tiles = HALO[0], OWN[0], TILES[0]
+def insert(first_ref, second_ref, near, c0, s0):
+    tiles = TILES[0]
     next_first, _ = towards_next()
-    above, below = PAD, PAD + halo + own
+    count = first_ref.shape[1]
+    above = PAD + (HALO[0] - NEAR if near else 0)
+    below = PAD + HALO[0] + OWN[0] + (0 if near else NEAR)
     for ref, base in ((first_ref, jnp.where(next_first, below, above)), (second_ref, jnp.where(next_first, above, below))):
-        for i in range(halo // 8):
+        for i in range(count // 8):
             rows = pl.ds(pl.multiple_of(base + 8 * i, 8), 8)
             for t in range(tiles):
                 c0[t, rows, :] = ref[t, 8 * i : 8 * i + 8, :]
                 s0[t, rows, :] = ref[tiles + t, 8 * i : 8 * i + 8, :]
-    clear_pads(vb0, bp1, va1, vb1)
+
+
+def scaled_store(bp_ref, a_ref, start=0):
+    def store(j, k, q):
+        bp_ref[start + k, at(j, PAD), :] = a_ref[4, k, at(j, 0), :] * q
+
+    return store
+
+
+def quarter_store(c_ref):
+    def store(j, k, q):
+        c_ref[k, at(j, PAD), :] = 0.25 * q
+
+    return store
+
+
+def outer_kernel(peers, *refs):
+    first_ref, second_ref = refs[9:11]
+    c0, s0, a0, bp0, va0, c1, a1, bp1, va1, vb0 = refs[11:]
+    tiles = TILES[0]
+    insert(first_ref, second_ref, False, c0, s0)
+    clear_pads(vb0)
+    ends = ((0, 2), (5, 7))
+    for strips in ((0, 3), (11, 14)):
+        make_weights(0, c0, a0, peers, strips, s0, bp0)
+    for strips in ends:
+        restrict(strips, c0, PAD, range(tiles), quarter_store(c1), 2)
+    for strips in ends:
+        make_weights(1, c1, a1, peers, strips)
+        restrict(strips, s0, PAD, range(tiles), scaled_store(bp1, a1, TILES[1]), 2)
     for strips in ((0, 4), (10, 14)):
+        relax(0, bp0, va0, bp0, a0, strips)
+    for strips in ((0, 4), (10, 14)):
+        residual(0, va0, vb0, bp0, a0, strips)
+    for strips in ends:
+        restrict(strips, vb0, PAD, range(tiles), scaled_store(bp1, a1), 2)
+    relax(1, bp1, va1, bp1, a1)
+
+
+def open_kernel(
+    peers, c0_in, s0_in, a0_in, b0_in, v0_in, c1_in, first_ref, second_ref,
+    c0, s0, a0, bp0, va0, c1, a1, bp1, va1, msg_ref,
+    vb0, vb1,
+):
+    tiles = TILES[0]
+    insert(first_ref, second_ref, True, c0, s0)
+    clear_pads(va1, vb1, size=2 * PAD)
+    clear_pads(bp1, size=2 * PAD)
+    for strips in ((2, 4), (10, 12)):
         make_weights(0, c0, a0, peers, strips, s0, bp0)
-    for strips in ((0, 2), (5, 7)):
+    for strips in ((1, 2), (5, 6)):
         restrict(strips, c0, PAD, range(tiles), quarter_store(c1), 2)
-    make_weights(1, c1, a1, peers)
-    restrict(STRIPS[1], s0, PAD, range(tiles), scaled_store(bp1, a1, TILES[1]))
-    for strips in ((0, 5), (9, 14)):
+    make_weights(1, c1, a1, peers, (1, 6))
+    restrict((1, 6), s0, PAD, range(tiles), scaled_store(bp1, a1, TILES[1]))
+    for strips in ((2, 5), (9, 12)):
         relax(0, bp0, va0, bp0, a0, strips)
-    residual(0, va0, vb0, bp0, a0)
-    restrict(STRIPS[1], vb0, PAD, range(tiles), scaled_store(bp1, a1))
-    relax(1, bp1, va1, bp1, a1)
+    residual(0, va0, vb0, bp0, a0, (2, 12))
+    restrict((1, 6), vb0, PAD, range(tiles), scaled_store(bp1, a1))
+    relax(1, bp1, va1, bp1, a1, (1, 6))
     residual(1, va1, vb1, bp1, a1, (1, 6))
 
     def store(j, k, q):
@@ -469,7 +512,7 @@
 FAR = pl.BlockSpec(memory_space=pltpu.HBM)
 
 
-def call(kernel, name, arguments, outputs, scratch=(), aliases=None, sems=0, far=0):
+def call(kernel, arguments, outputs, scratch=(), aliases=None, sems=0, far=0):
     return pl.pallas_call(
         kernel,
         out_shape=outputs,
@@ -479,56 +522,68 @@
         input_output_aliases=aliases or {},
         compiler_params=pltpu.CompilerParams(vmem_limit_bytes=24 * 2**20),
         cost_estimate=pl.CostEstimate(flops=10**8, bytes_accessed=10**6, transcendentals=0),
-        name=name,
     )(*arguments)
 
 
 def swaps(distance):
-    peers = lax.axis_size("grid")
+    peers, samples = lax.axis_size("grid"), lax.axis_size("samp")
     even = [(i, i + distance if i % (2 * distance) < distance else i - distance) for i in range(peers)]
     odd = [(a + distance, b + distance) for a, b in even if max(a, b) + distance < peers]
-    last = peers - 1
-    odd += [(0, last), (last, 0)] if distance == 1 else [(0, 1), (1, 0), (last - 1, last), (last, last - 1)]
-    return even, odd
+    ends = sorted(set(range(peers)) - {a for a, _ in odd})
+    both = [[(s * peers + a, s * peers + b) for s in range(samples) for a, b in pairs] for pairs in (even, odd)]
+    both[1] += [(s * peers + e, (s + 1) % samples * peers + e) for s in range(samples) for e in ends]
+    return both
+
+
+def swapped(value, pairs):
+    return lax.ppermute(value, ("samp", "grid"), pairs)
 
 
 def gathered(value):
-    return [lax.ppermute(value, "grid", pairs) for distance in (1, 2) for pairs in swaps(distance)] + [value]
+    sets = [pairs for distance in (1, 2) for pairs in swaps(distance)]
+    return [swapped(value, pairs) for pairs in sets] + [value]
 
 
 def local(log_coef, source):
     peers = lax.axis_size("grid")
     log_field, source_field = log_coef[0], source[0]
     rows, columns = source_field.shape
-    edge = near(2 * TILES[0], HALO[0], LANES)
     fields = [pltpu.with_memory_space_constraint(x, pltpu.HBM) for x in (log_field, source_field)]
-    c0, s0, first, second = call(
-        pack_kernel, "pack", fields, (near(*c_shape(0)), near(*c_shape(0)), edge, edge),
-        [(2 * HALO[0], columns)] * 2, sems=4, far=2,
-    )
+    tiled = [near(*c_shape(0)), near(*c_shape(0))]
     even, odd = swaps(1)
-    first, second = lax.ppermute(first, "grid", even), lax.ppermute(second, "grid", odd)
-
+
+    def send_rows(first_part, held_fields):
+        count = boundary_rows(first_part)[0][1]
+        edge = near(2 * TILES[0], count, LANES)
+        c0, s0, first, second = call(
+            functools.partial(pack_kernel, first_part), fields + held_fields,
+            tiled + [edge, edge], [(2 * count, columns)] * 2, {} if first_part else {2: 0, 3: 1}, sems=4, far=2,
+        )
+        return [c0, s0], [swapped(first, even), swapped(second, odd)]
+
+    tiles, first_rows = send_rows(True, [])
+    tiles, rest_rows = send_rows(False, held(*tiles))
     state = [near(*f(level)) for level in (0, 1) for f in (a_shape, v_shape, v_shape)]
-    whole = [near(*c_shape(0)), near(*c_shape(0))] + state[:3] + [near(*c_shape(1))]
+    whole = tiled + state[:3] + [near(*c_shape(1))]
     middle_rows = rows - 2 * HALO[0]
     started = call(
-        functools.partial(inner_kernel, peers), "inner", [*fields, *held(c0, s0)], whole,
+        functools.partial(inner_kernel, peers), fields + held(*tiles), whole,
         [(middle_rows, columns)] * 2, {2: 0, 3: 1}, sems=2, far=2,
     )
-    c0, s0, a0, b0, v0, c1, message, a1, b1, v1 = call(
-        functools.partial(open_kernel, peers),
-        "open",
-        held(*started, first, second),
-        whole + [near(3 * TILES[2], OWN[2], LANES)] + state[3:],
-        [v_shape(0), v_shape(1)],
-        {k: k for k in range(6)},
+    *opened, message = call(
+        functools.partial(open_kernel, peers), held(*started, *first_rows),
+        whole + state[3:] + [near(3 * TILES[2], OWN[2], LANES)],
+        [v_shape(0), v_shape(1)], {k: k for k in range(6)},
+    )
+    arrived = gathered(message)
+    _, _, a0, b0, v0, _, a1, b1, v1 = call(
+        functools.partial(outer_kernel, peers), held(*opened, *rest_rows),
+        whole + state[3:], [v_shape(0)], {k: k for k in range(9)},
     )
     deep = [shape for level in (2, 3, 4) for shape in [c_shape(level)] + [v_shape(level)] * 3]
     message, a2, a3, a4, v0, b1, v1 = call(
         functools.partial(middle_kernel, peers),
-        "middle",
-        held(*gathered(message), a0, b0, v0, a1, b1, v1),
+        held(*arrived, a0, b0, v0, a1, b1, v1),
         [near(2 * TILES[2], OWN[2], LANES)] + [near(*a_shape(level)) for level in (2, 3, 4)] + [state[k] for k in (2, 4, 5)],
         [v_shape(0), v_shape(1)] + deep,
         {7: 4, 9: 5, 10: 6},
@@ -537,7 +592,6 @@
     half = near(rows, columns // 2)
     v0, v1, correction, mine, other = call(
         close_kernel,
-        "close",
         held(*gathered(message), a0, b0, v0, a1, b1, v1, a2, a3, a4),
         (state[2], state[5], jax.ShapeDtypeStruct((rows, columns), F32), half, half),
         [v_shape(0), v_shape(1)] + deep + [(rows, columns)],

time: 63.4 us -> 60.7 us (0.957)
  the two profiles are of different devices: /device:TPU:1 before, /device:TPU:97 now
where the time goes in v5:
time: 60.7 us; the launch traced here: 60.5 us
  starting transfers between devices  22.1 us (36%)
  Pallas kernels  18.7 us (31%)
  waiting for transfers between devices  18.1 us (30%)
  other arithmetic  0.86 us (1%)
  between operations  0.69 us (1%)
    pallas_call x7, Pallas kernels, call(): pl.pallas_call(kernel, out_shape=outputs, in_specs=[FAR] * far + [VMEM] *...  18.7 us
    ppermute x12, starting transfers between devices, swapped(): return lax.ppermute(value, ('samp', 'grid'), pairs)  17.8 us
    ppermute x12, waiting for transfers between devices, swapped(): return lax.ppermute(value, ('samp', 'grid'), pairs)  17 us
    ppermute x1, starting transfers between devices, local(): theirs = lax.ppermute(other, 'samp', [(0, 1), (1, 0)])  4.24 us
  transfers between devices with their start and end apart: 13, of which 7 were waited for; matrix products, arithmetic and copies ran while one was open for 0% of the time, Pallas kernels for 9%

profile of v5, /device:TPU:97, one launch (start us, length us, event | category | flops | bytes accessed | tf_op | source)
XLA Modules:
  0.0 60.5 jit_solution(16823061563475914811)
XLA Ops:
  0.6 1.7 %shard_map.49 = (f32[16,128,128]{2,1,0:T(8,128)S(1)}, f32[16,128,128]{2,1,0:T(8,128)S(1)}, f32[32,8,128]{2,1,0:T(8,128)S(1)}, f32[32,8,128]{2,1,0:T(8,128)S(1)}) custom-call(f32[64,2048]{1,0:T(8,128)} %bitcast.3, f32[64,2048]{1,0:T(8,128)} %bitcast.6), custom_call_target="tpu_custom_call" | custom-call | flops 100000000 | bytes 1000000 | tf_op jit(solution)/shard_map/pallas_call | solution.py:516
  2.3 2.1 %shard_map.50 = (f32[16,128,128]{2,1,0:T(8,128)S(1)}, f32[16,128,128]{2,1,0:T(8,128)S(1)}, f32[32,16,128]{2,1,0:T(8,128)S(1)}, f32[32,16,128]{2,1,0:T(8,128)S(1)}) custom-call(f32[64,2048]{1,0:T(8,128)} %bitcast.4, f32[64,2048]{1,0:T(8,128)} %bitcast.7, f32[16,128,128]{2,1,0:T(8,128)S(1)} %get-tuple-element.43.refs_0_, ...), custom_call_target="tpu_custom_call", output_to_operand_aliasing={{0}: (2, {}), {1}: (3, {})} | custom-call | flops 100000000 | bytes 1000000 | tf_op jit(solution)/shard_map/pallas_call | solution.py:516
  4.4 1.3 %collective-permute-start.6 = (f32[32,16,128]{2,1,0:T(8,128)S(1)}, f32[32,16,128]{2,1,0:T(8,128)S(1)}, u32[]{:S(2)}, u32[]{:S(2)}) collective-permute-start(f32[32,16,128]{2,1,0:T(8,128)S(1)} %get-tuple-element.65), channel_id=1, source_target_pairs={{0,1},{1,0},{2,3},{3,2},{4,5},{5,4},{6,7},{7,6},{8,9},{9,8},{10,11... | collective-permute-start | bytes 786440 | tf_op jit(solution)/shard_map/ppermute | solution.py:539
  5.7 4.1 %collective-permute-start.7 = (f32[32,16,128]{2,1,0:T(8,128)S(1)}, f32[32,16,128]{2,1,0:T(8,128)S(1)}, u32[]{:S(2)}, u32[]{:S(2)}) collective-permute-start(f32[32,16,128]{2,1,0:T(8,128)S(1)} %get-tuple-element.66), channel_id=1, source_target_pairs={{1,2},{2,1},{3,4},{4,3},{5,6},{6,5},{7,8},{8,7},{9,10},{10,9},{11,... | collective-permute-start | bytes 786440 | tf_op jit(solution)/shard_map/ppermute | solution.py:539
  9.8 0.0 collective-permute-start
  9.8 1.6 %collective-permute-start.1 = (f32[32,8,128]{2,1,0:T(8,128)S(1)}, f32[32,8,128]{2,1,0:T(8,128)S(1)}, u32[]{:S(2)}, u32[]{:S(2)}) collective-permute-start(f32[32,8,128]{2,1,0:T(8,128)S(1)} %get-tuple-element.54), channel_id=1, source_target_pairs={{1,2},{2,1},{3,4},{4,3},{5,6},{6,5},{7,8},{8,7},{9,10},{10,9},{11,... | collective-permute-start | bytes 393224 | tf_op jit(solution)/shard_map/ppermute | solution.py:539
  11.4 2.1 %shard_map.51 = (f32[16,128,128]{2,1,0:T(8,128)S(1)}, f32[16,128,128]{2,1,0:T(8,128)S(1)}, f32[6,16,112,128]{3,2,1,0:T(8,128)S(1)}, f32[16,128,128]{2,1,0:T(8,12...) custom-call(f32[64,2048]{1,0:T(8,128)} %bitcast.5, ...), custom_call_target="tpu_custom_call", output_to_operand_aliasing={{0}: (2, {}), {1}: (3, {})} | custom-call | flops 100000000 | bytes 1000000 | tf_op jit(solution)/shard_map/pallas_call | solution.py:516
  13.5 0.7 %collective-permute-done.first_ref = f32[32,8,128]{2,1,0:T(8,128)S(1)} collective-permute-done((f32[32,8,128]{2,1,0:T(8,128)S(1)}, f32[32,8,128]{2,1,0:T(8,128)S(1)}, u32[]{:S(2)}, u32[]{:S(2)}) %collective-permute-start) | collective-permute-done | bytes 131104 | tf_op jit(solution)/shard_map/ppermute | solution.py:539
  14.2 5.4 %collective-permute-done.1.second_ref = f32[32,8,128]{2,1,0:T(8,128)S(1)} collective-permute-done((f32[32,8,128]{2,1,0:T(8,128)S(1)}, f32[32,8,128]{2,1,0:T(8,128)S(1)}, u32[]{:S(2)}, u32[]{:S(2)}) %collective-permute-start.1) | collective-permute-done | bytes 131104 | tf_op jit(solution)/shard_map/ppermute | solution.py:539
  19.6 1.6 %shard_map.52 = (f32[16,128,128]{2,1,0:T(8,128)S(1)}, f32[16,128,128]{2,1,0:T(8,128)S(1)}, f32[6,16,112,128]{3,2,1,0:T(8,128)S(1)}, f32[16,128,128]{2,1,0:T(8,12...) custom-call(f32[16,128,128]{2,1,0:T(8,128)S(1)} %get-tuple-element.4, ...), custom_call_target="tpu_custom_call", output_to_operand_aliasing={{0}: (0, {}), {1}: (1, {}), {2}: (2, {}), {3}: (3, {}), {4}... | custom-call | flops 100000000 | bytes 1000000 | tf_op jit(solution)/shard_map/pallas_call | solution.py:516
  21.2 0.6 collective-permute-start.5
  21.8 1.4 %collective-permute-start.4 = (f32[12,16,128]{2,1,0:T(8,128)S(1)}, f32[12,16,128]{2,1,0:T(8,128)S(1)}, u32[]{:S(2)}, u32[]{:S(2)}) collective-permute-start(f32[12,16,128]{2,1,0:T(8,128)S(1)} %get-tuple-element.55.m4), channel_id=1, source_target_pairs={{0,2},{1,3},{2,0},{3,1},{4,6},{5,7},{6,4},{7,5},{8,10},{9,11},{10,... | collective-permute-start | bytes 294920 | tf_op jit(solution)/shard_map/ppermute | solution.py:539
  23.2 3.3 %collective-permute-start.3 = (f32[12,16,128]{2,1,0:T(8,128)S(1)}, f32[12,16,128]{2,1,0:T(8,128)S(1)}, u32[]{:S(2)}, u32[]{:S(2)}) collective-permute-start(f32[12,16,128]{2,1,0:T(8,128)S(1)} %get-tuple-element.55.m4), channel_id=1, source_target_pairs={{1,2},{2,1},{3,4},{4,3},{5,6},{6,5},{7,8},{8,7},{9,10},{10,9},{11,... | collective-permute-start | bytes 294920 | tf_op jit(solution)/shard_map/ppermute | solution.py:539
  26.4 0.0 collective-permute-done.6.refs_9_
  26.4 0.0 collective-permute-start.2
  26.5 0.0 collective-permute-done.7.refs_10_
  26.5 1.5 %shard_map.53 = (f32[16,128,128]{2,1,0:T(8,128)S(1)}, f32[16,128,128]{2,1,0:T(8,128)S(1)}, f32[6,16,112,128]{3,2,1,0:T(8,128)S(1)}, f32[16,128,128]{2,1,0:T(8,12...) custom-call(f32[16,128,128]{2,1,0:T(8,128)S(1)} %get-tuple-element.5, ...), custom_call_target="tpu_custom_call", output_to_operand_aliasing={{0}: (0, {}), {1}: (1, {}), {2}: (2, {}), {3}: (3, {}), {4}... | custom-call | flops 100000000 | bytes 1000000 | tf_op jit(solution)/shard_map/pallas_call | solution.py:516
  28.0 1.3 %collective-permute-done.5.m3 = f32[12,16,128]{2,1,0:T(8,128)S(1)} collective-permute-done((f32[12,16,128]{2,1,0:T(8,128)S(1)}, f32[12,16,128]{2,1,0:T(8,128)S(1)}, u32[]{:S(2)}, u32[]{:S(2)}) %collective-permute-start.5) | collective-permute-done | bytes 98336 | tf_op jit(solution)/shard_map/ppermute | solution.py:539
  29.3 0.0 collective-permute-done.4.m2
  29.3 3.9 %collective-permute-done.3.m1 = f32[12,16,128]{2,1,0:T(8,128)S(1)} collective-permute-done((f32[12,16,128]{2,1,0:T(8,128)S(1)}, f32[12,16,128]{2,1,0:T(8,128)S(1)}, u32[]{:S(2)}, u32[]{:S(2)}) %collective-permute-start.3) | collective-permute-done | bytes 98336 | tf_op jit(solution)/shard_map/ppermute | solution.py:539
  33.2 0.0 collective-permute-done.2.m0
  33.2 5.4 %shard_map.54 = (f32[8,16,128]{2,1,0:T(8,128)S(1)}, f32[6,4,80,128]{3,2,1,0:T(8,128)S(1)}, f32[6,2,40,128]{3,2,1,0:T(8,128)S(1)}, f32[6,1,24,128]{3,2,1,0:T(8,12...) custom-call(f32[12,16,128]{2,1,0:T(8,128)S(1)} %collective-permute-d, ...), custom_call_target="tpu_custom_call", output_to_operand_aliasing={{4}: (7, {}), {5}: (9, {}), {6}: (10, {})} | custom-call | flops 100000000 | bytes 1000000 | tf_op jit(solution)/shard_map/pallas_call | solution.py:516
  38.6 0.1 collective-permute-start.11
  38.7 2.5 %collective-permute-start.10 = (f32[8,16,128]{2,1,0:T(8,128)S(1)}, f32[8,16,128]{2,1,0:T(8,128)S(1)}, u32[]{:S(2)}, u32[]{:S(2)}) collective-permute-start(f32[8,16,128]{2,1,0:T(8,128)S(1)} %get-tuple-element.73.m4), channel_id=1, source_target_pairs={{0,2},{1,3},{2,0},{3,1},{4,6},{5,7},{6,4},{7,5},{8,10},{9,11},{10,... | collective-permute-start | bytes 196616 | tf_op jit(solution)/shard_map/ppermute | solution.py:539
  41.2 2.6 %collective-permute-start.9 = (f32[8,16,128]{2,1,0:T(8,128)S(1)}, f32[8,16,128]{2,1,0:T(8,128)S(1)}, u32[]{:S(2)}, u32[]{:S(2)}) collective-permute-start(f32[8,16,128]{2,1,0:T(8,128)S(1)} %get-tuple-element.73.m4), channel_id=1, source_target_pairs={{1,2},{2,1},{3,4},{4,3},{5,6},{6,5},{7,8},{8,7},{9,10},{10,9},{11,... | collective-permute-start | bytes 196616 | tf_op jit(solution)/shard_map/ppermute | solution.py:539
  43.8 0.4 collective-permute-start.8
  44.2 2.1 %collective-permute-done.11.m3 = f32[8,16,128]{2,1,0:T(8,128)S(1)} collective-permute-done((f32[8,16,128]{2,1,0:T(8,128)S(1)}, f32[8,16,128]{2,1,0:T(8,128)S(1)}, u32[]{:S(2)}, u32[]{:S(2)}) %collective-permute-start.11) | collective-permute-done | bytes 65568 | tf_op jit(solution)/shard_map/ppermute | solution.py:539
  46.3 0.0 collective-permute-done.10.m2
  46.3 3.6 %collective-permute-done.9.m1 = f32[8,16,128]{2,1,0:T(8,128)S(1)} collective-permute-done((f32[8,16,128]{2,1,0:T(8,128)S(1)}, f32[8,16,128]{2,1,0:T(8,128)S(1)}, u32[]{:S(2)}, u32[]{:S(2)}) %collective-permute-start.9) | collective-permute-done | bytes 65568 | tf_op jit(solution)/shard_map/ppermute | solution.py:539
  49.9 0.0 collective-permute-done.8.m0
  49.9 4.3 %shard_map.55 = (f32[16,128,128]{2,1,0:T(8,128)S(1)}, f32[16,72,128]{2,1,0:T(8,128)S(1)}, f32[64,2048]{1,0:T(8,128)}, f32[64,1024]{1,0:T(8,128)S(1)}, f32[64,1024]{1,0:T(8,128)S(1)}) custom-call(f32[8,16,128]{2,1,0:T(8,128)S(1)} %collective-permute-done.8.m0, ...), custom_call_target="tpu_custom_call", output_to_operand_aliasing={{0}: (7, {}), {1}: (10, {})} | custom-call | flops 100000000 | bytes 1000000 | tf_op jit(solution)/shard_map/pallas_call | solution.py:516
  54.2 4.2 %collective-permute-start.12 = (f32[64,1024]{1,0:T(8,128)S(1)}, f32[64,1024]{1,0:T(8,128)S(1)}, u32[]{:S(2)}, u32[]{:S(2)}) collective-permute-start(f32[64,1024]{1,0:T(8,128)S(1)} %get-tuple-element.82), channel_id=1, source_target_pairs={{0,64},{64,0},{1,65},{65,1},{2,66},{66,2},{3,67},{67,3},{4,68},{68... | collective-permute-start | bytes 786440 | tf_op jit(solution)/shard_map/ppermute | solution.py:602
  58.4 1.2 %collective-permute-done.12 = f32[64,1024]{1,0:T(8,128)S(1)} collective-permute-done((f32[64,1024]{1,0:T(8,128)S(1)}, f32[64,1024]{1,0:T(8,128)S(1)}, u32[]{:S(2)}, u32[]{:S(2)}) %collective-permute-start.12) | collective-permute-done | bytes 262176 | tf_op jit(solution)/shard_map/ppermute | solution.py:602
  59.6 0.9 %multiply_subtract_fusion = (f32[64,1024]{1,0:T(8,128)}, f32[64,1024]{1,0:T(8,128)}) fusion(f32[64,1024]{1,0:T(8,128)S(1)} %collective-permute-done.12, f32[64,1024]{1,0:T(8,128)S(1)} %get-tuple-element.81), kind=kLoop, calls=%fused_computation | loop fusion | flops 458752 | bytes 1048576 | tf_op jit(solution)/shard_map/sub | solution.py:606
Async XLA Ops:
  4.4 22.0 %collective-permute-start.6 = (f32[32,16,128]{2,1,0:T(8,128)S(1)}, f32[32,16,128]{2,1,0:T(8,128)S(1)}, u32[]{:S(2)}, u32[]{:S(2)}) collective-permute-start(f32[32,16,128]{2,1,0:T(8,128)S(1)} %get-tuple-element.65), channel_id=1, source_target_pairs={{0,1},{1,0},{2,3},{3,2},{4,5},{5,4},{6,7},{7,6},{8,9},{9,8},{10,11... | collective-permute-start | bytes 786440 | tf_op jit(solution)/shard_map/ppermute | solution.py:539
  5.7 20.8 %collective-permute-start.7 = (f32[32,16,128]{2,1,0:T(8,128)S(1)}, f32[32,16,128]{2,1,0:T(8,128)S(1)}, u32[]{:S(2)}, u32[]{:S(2)}) collective-permute-start(f32[32,16,128]{2,1,0:T(8,128)S(1)} %get-tuple-element.66), channel_id=1, source_target_pairs={{1,2},{2,1},{3,4},{4,3},{5,6},{6,5},{7,8},{8,7},{9,10},{10,9},{11,... | collective-permute-start | bytes 786440 | tf_op jit(solution)/shard_map/ppermute | solution.py:539
  9.8 4.4 %collective-permute-start = (f32[32,8,128]{2,1,0:T(8,128)S(1)}, f32[32,8,128]{2,1,0:T(8,128)S(1)}, u32[]{:S(2)}, u32[]{:S(2)}) collective-permute-start(f32[32,8,128]{2,1,0:T(8,128)S(1)} %get-tuple-element.53), channel_id=1, source_target_pairs={{0,1},{1,0},{2,3},{3,2},{4,5},{5,4},{6,7},{7,6},{8,9},{9,8},{10,11... | collective-permute-start | bytes 393224 | tf_op jit(solution)/shard_map/ppermute | solution.py:539
  9.8 9.8 %collective-permute-start.1 = (f32[32,8,128]{2,1,0:T(8,128)S(1)}, f32[32,8,128]{2,1,0:T(8,128)S(1)}, u32[]{:S(2)}, u32[]{:S(2)}) collective-permute-start(f32[32,8,128]{2,1,0:T(8,128)S(1)} %get-tuple-element.54), channel_id=1, source_target_pairs={{1,2},{2,1},{3,4},{4,3},{5,6},{6,5},{7,8},{8,7},{9,10},{10,9},{11,... | collective-permute-start | bytes 393224 | tf_op jit(solution)/shard_map/ppermute | solution.py:539
  21.2 8.1 %collective-permute-start.5 = (f32[12,16,128]{2,1,0:T(8,128)S(1)}, f32[12,16,128]{2,1,0:T(8,128)S(1)}, u32[]{:S(2)}, u32[]{:S(2)}) collective-permute-start(f32[12,16,128]{2,1,0:T(8,128)S(1)} %get-tuple-element.55.m4), channel_id=1, source_target_pairs={{2,4},{3,5},{4,2},{5,3},{6,8},{7,9},{8,6},{9,7},{10,12},{11,13},{1... | collective-permute-start | bytes 294920 | tf_op jit(solution)/shard_map/ppermute | solution.py:539
  21.8 7.5 %collective-permute-start.4 = (f32[12,16,128]{2,1,0:T(8,128)S(1)}, f32[12,16,128]{2,1,0:T(8,128)S(1)}, u32[]{:S(2)}, u32[]{:S(2)}) collective-permute-start(f32[12,16,128]{2,1,0:T(8,128)S(1)} %get-tuple-element.55.m4), channel_id=1, source_target_pairs={{0,2},{1,3},{2,0},{3,1},{4,6},{5,7},{6,4},{7,5},{8,10},{9,11},{10,... | collective-permute-start | bytes 294920 | tf_op jit(solution)/shard_map/ppermute | solution.py:539
  23.2 10.0 %collective-permute-start.3 = (f32[12,16,128]{2,1,0:T(8,128)S(1)}, f32[12,16,128]{2,1,0:T(8,128)S(1)}, u32[]{:S(2)}, u32[]{:S(2)}) collective-permute-start(f32[12,16,128]{2,1,0:T(8,128)S(1)} %get-tuple-element.55.m4), channel_id=1, source_target_pairs={{1,2},{2,1},{3,4},{4,3},{5,6},{6,5},{7,8},{8,7},{9,10},{10,9},{11,... | collective-permute-start | bytes 294920 | tf_op jit(solution)/shard_map/ppermute | solution.py:539
  26.4 6.7 %collective-permute-start.2 = (f32[12,16,128]{2,1,0:T(8,128)S(1)}, f32[12,16,128]{2,1,0:T(8,128)S(1)}, u32[]{:S(2)}, u32[]{:S(2)}) collective-permute-start(f32[12,16,128]{2,1,0:T(8,128)S(1)} %get-tuple-element.55.m4), channel_id=1, source_target_pairs={{0,1},{1,0},{2,3},{3,2},{4,5},{5,4},{6,7},{7,6},{8,9},{9,8},{10,11... | collective-permute-start | bytes 294920 | tf_op jit(solution)/shard_map/ppermute | solution.py:539
  38.6 7.7 %collective-permute-start.11 = (f32[8,16,128]{2,1,0:T(8,128)S(1)}, f32[8,16,128]{2,1,0:T(8,128)S(1)}, u32[]{:S(2)}, u32[]{:S(2)}) collective-permute-start(f32[8,16,128]{2,1,0:T(8,128)S(1)} %get-tuple-element.73.m4), channel_id=1, source_target_pairs={{2,4},{3,5},{4,2},{5,3},{6,8},{7,9},{8,6},{9,7},{10,12},{11,13},{1... | collective-permute-start | bytes 196616 | tf_op jit(solution)/shard_map/ppermute | solution.py:539
  38.7 7.6 %collective-permute-start.10 = (f32[8,16,128]{2,1,0:T(8,128)S(1)}, f32[8,16,128]{2,1,0:T(8,128)S(1)}, u32[]{:S(2)}, u32[]{:S(2)}) collective-permute-start(f32[8,16,128]{2,1,0:T(8,128)S(1)} %get-tuple-element.73.m4), channel_id=1, source_target_pairs={{0,2},{1,3},{2,0},{3,1},{4,6},{5,7},{6,4},{7,5},{8,10},{9,11},{10,... | collective-permute-start | bytes 196616 | tf_op jit(solution)/shard_map/ppermute | solution.py:539
  41.2 8.7 %collective-permute-start.9 = (f32[8,16,128]{2,1,0:T(8,128)S(1)}, f32[8,16,128]{2,1,0:T(8,128)S(1)}, u32[]{:S(2)}, u32[]{:S(2)}) collective-permute-start(f32[8,16,128]{2,1,0:T(8,128)S(1)} %get-tuple-element.73.m4), channel_id=1, source_target_pairs={{1,2},{2,1},{3,4},{4,3},{5,6},{6,5},{7,8},{8,7},{9,10},{10,9},{11,... | collective-permute-start | bytes 196616 | tf_op jit(solution)/shard_map/ppermute | solution.py:539
  43.8 6.1 %collective-permute-start.8 = (f32[8,16,128]{2,1,0:T(8,128)S(1)}, f32[8,16,128]{2,1,0:T(8,128)S(1)}, u32[]{:S(2)}, u32[]{:S(2)}) collective-permute-start(f32[8,16,128]{2,1,0:T(8,128)S(1)} %get-tuple-element.73.m4), channel_id=1, source_target_pairs={{0,1},{1,0},{2,3},{3,2},{4,5},{5,4},{6,7},{7,6},{8,9},{9,8},{10,11... | collective-permute-start | bytes 196616 | tf_op jit(solution)/shard_map/ppermute | solution.py:539
  54.2 5.4 %collective-permute-start.12 = (f32[64,1024]{1,0:T(8,128)S(1)}, f32[64,1024]{1,0:T(8,128)S(1)}, u32[]{:S(2)}, u32[]{:S(2)}) collective-permute-start(f32[64,1024]{1,0:T(8,128)S(1)} %get-tuple-element.82), channel_id=1, source_target_pairs={{0,64},{64,0},{1,65},{65,1},{2,66},{66,2},{3,67},{67,3},{4,68},{68... | collective-permute-start | bytes 786440 | tf_op jit(solution)/shard_map/ppermute | solution.py:602

commit v6 on v5

--- a/solution.py
+++ b/solution.py
@@ -205,9 +205,13 @@
 
 def convert(rows_of, log_ref, src_ref, c0, s0):
     tiles = TILES[0]
-    for row, to in rows_of:
-        logs, sources = ([ref[row : row + 8, t * LANES : (t + 1) * LANES] for t in range(tiles)] for ref in (log_ref, src_ref))
-        for ref, x in zip((c0, s0), turn(([jnp.exp(v) for v in logs], sources))):
+    for k in range(0, len(rows_of), 2):
+        groups, places = [], []
+        for row, to in rows_of[k : k + 2]:
+            logs, sources = ([ref[row : row + 8, t * LANES : (t + 1) * LANES] for t in range(tiles)] for ref in (log_ref, src_ref))
+            groups += [[jnp.exp(v) for v in logs], sources]
+            places += [(c0, to), (s0, to)]
+        for (ref, to), x in zip(places, turn(groups)):
             for t, v in enumerate(x):
                 ref[t, to : to + 8, :] = v
 
@@ -225,41 +229,43 @@
     return (start, count), (OWN[0] - start - count, count)
 
 
-def pack_kernel(near, log_in, src_in, *refs):
-    c0, s0, first_ref, second_ref, logs, sources, sems = refs if near else refs[2:]
+def write_messages(sides, c0, s0, first_ref, second_ref):
     tiles = TILES[0]
-    sides = boundary_rows(near)
-    count = sides[0][1]
-    pairs = []
-    for side, (start, _) in enumerate(sides):
-        to = pl.ds(side * count, count)
-        pairs += [(ref.at[pl.ds(start, count), :], dst.at[to, :]) for ref, dst in ((log_in, logs), (src_in, sources))]
-    copies = load(sems, *pairs)
-    for side, (start, _) in enumerate(sides):
-        for copy in copies[2 * side : 2 * side + 2]:
-            copy.wait()
-        base = PAD + HALO[0] + start
-        convert([(side * count + k, base + k) for k in range(0, count, 8)], logs, sources, c0, s0)
     next_first, _ = towards_next()
     up, down = (PAD + HALO[0] + start for start, _ in sides)
     for ref, base in ((first_ref, jnp.where(next_first, down, up)), (second_ref, jnp.where(next_first, up, down))):
-        for i in range(count // 8):
+        for i in range(sides[0][1] // 8):
             rows = pl.ds(pl.multiple_of(base + 8 * i, 8), 8)
             for t in range(tiles):
                 ref[t, 8 * i : 8 * i + 8, :] = c0[t, rows, :]
                 ref[tiles + t, 8 * i : 8 * i + 8, :] = s0[t, rows, :]
 
 
-def inner_kernel(peers, log_in, src_in, c0_in, s0_in, c0, s0, a0, bp0, va0, c1, logs, sources, sems):
+def pack_kernel(log_in, src_in, c0, s0, first_ref, second_ref, logs, sources, sems):
+    sides = boundary_rows(True)
+    parts = [pl.ds(start, count) for start, count in sides] + [pl.ds(NEAR, OWN[0] - 2 * NEAR)]
+    copies = load(sems, *((ref.at[p, :], to.at[p, :]) for p in parts for ref, to in ((log_in, logs), (src_in, sources))))
+    for copy in copies[:4]:
+        copy.wait()
+    convert([(start, PAD + HALO[0] + start) for start, _ in sides], logs, sources, c0, s0)
+    write_messages(sides, c0, s0, first_ref, second_ref)
+    for copy in copies[4:]:
+        copy.wait()
+
+
+def pack_rest_kernel(log_ref, src_ref, c0_in, s0_in, c0, s0, first_ref, second_ref):
+    sides = boundary_rows(False)
+    places = [start + k for start, count in sides for k in range(0, count, 8)]
+    convert([(row, PAD + HALO[0] + row) for row in places], log_ref, src_ref, c0, s0)
+    write_messages(sides, c0, s0, first_ref, second_ref)
+
+
+def inner_kernel(peers, log_ref, src_ref, c0_in, s0_in, c0, s0, a0, bp0, va0, c1):
     halo, own, tiles = HALO[0], OWN[0], TILES[0]
-    inner = pl.ds(halo, own - 2 * halo)
-    copies = load(sems, (log_in.at[inner, :], logs), (src_in.at[inner, :], sources))
     clear_pads(c0, value=1.0, size=PAD + halo)
     clear_pads(s0, bp0, va0, size=PAD + halo)
     clear_pads(c1, value=1.0)
-    for copy in copies:
-        copy.wait()
-    convert([(k, PAD + 2 * halo + k) for k in range(0, own - 2 * halo, 8)], logs, sources, c0, s0)
+    convert([(k, PAD + halo + k) for k in range(halo, own - halo, 8)], log_ref, src_ref, c0, s0)
     make_weights(0, c0, a0, peers, (4, 10), s0, bp0)
     restrict((2, 5), c0, PAD, range(tiles), quarter_store(c1))
     relax(0, bp0, va0, bp0, a0, (5, 9))
@@ -548,35 +554,27 @@
     peers = lax.axis_size("grid")
     log_field, source_field = log_coef[0], source[0]
     rows, columns = source_field.shape
-    fields = [pltpu.with_memory_space_constraint(x, pltpu.HBM) for x in (log_field, source_field)]
+    far_fields = [pltpu.with_memory_space_constraint(x, pltpu.HBM) for x in (log_field, source_field)]
     tiled = [near(*c_shape(0)), near(*c_shape(0))]
     even, odd = swaps(1)
-
-    def send_rows(first_part, held_fields):
-        count = boundary_rows(first_part)[0][1]
-        edge = near(2 * TILES[0], count, LANES)
-        c0, s0, first, second = call(
-            functools.partial(pack_kernel, first_part), fields + held_fields,
-            tiled + [edge, edge], [(2 * count, columns)] * 2, {} if first_part else {2: 0, 3: 1}, sems=4, far=2,
-        )
-        return [c0, s0], [swapped(first, even), swapped(second, odd)]
-
-    tiles, first_rows = send_rows(True, [])
-    tiles, rest_rows = send_rows(False, held(*tiles))
+    edge = near(2 * TILES[0], NEAR, LANES)
+    c0, s0, first, second, *fields = call(
+        pack_kernel, far_fields, tiled + [edge, edge] + [near(rows, columns)] * 2, sems=6, far=2
+    )
+    near_rows = [swapped(first, even), swapped(second, odd)]
+    edge = near(2 * TILES[0], HALO[0] - NEAR, LANES)
+    c0, s0, first, second = call(pack_rest_kernel, held(*fields, c0, s0), tiled + [edge, edge], aliases={2: 0, 3: 1})
+    rest_rows = [swapped(first, even), swapped(second, odd)]
     state = [near(*f(level)) for level in (0, 1) for f in (a_shape, v_shape, v_shape)]
     whole = tiled + state[:3] + [near(*c_shape(1))]
-    middle_rows = rows - 2 * HALO[0]
-    started = call(
-        functools.partial(inner_kernel, peers), fields + held(*tiles), whole,
-        [(middle_rows, columns)] * 2, {2: 0, 3: 1}, sems=2, far=2,
-    )
+    started = call(functools.partial(inner_kernel, peers), held(*fields, c0, s0), whole, aliases={2: 0, 3: 1})
     *opened, message = call(
-        functools.partial(open_kernel, peers), held(*started, *first_rows),
+        functools.partial(open_kernel, peers), held(*started, *near_rows),
         whole + state[3:] + [near(3 * TILES[2], OWN[2], LANES)],
         [v_shape(0), v_shape(1)], {k: k for k in range(6)},
     )
     arrived = gathered(message)
-    _, _, a0, b0, v0, _, a1, b1, v1 = call(
+    c0, s0, a0, b0, v0, _, a1, b1, v1 = call(
         functools.partial(outer_kernel, peers), held(*opened, *rest_rows),
         whole + state[3:], [v_shape(0)], {k: k for k in range(9)},
     )

time: 60.7 us -> 59.1 us (0.974)
  Pallas kernels: 18.7 us -> 16.2 us
  waiting for transfers between devices: 18.1 us -> 19.1 us
    pallas_call x7, Pallas kernels: 18.7 us -> 16.2 us  [call(): pl.pallas_call(kernel, out_shape=outputs, in_specs=[FAR] * far + [VMEM] *...]
    ppermute x12, waiting for transfers between devices: 17 us -> 18 us  [swapped(): return lax.ppermute(value, ('samp', 'grid'), pairs)]
  transfers between devices with their start and end apart: 13 -> 13, of which waited for: 7 -> 7; matrix products, arithmetic and copies ran while one was open for 0% -> 0% of each run, Pallas kernels for 9% -> 7%
where the time goes in v6:
time: 59.1 us; the launch traced here: 58.9 us
  starting transfers between devices  22 us (37%)
  waiting for transfers between devices  19.1 us (32%)
  Pallas kernels  16.2 us (27%)
  other arithmetic  0.86 us (1%)
  between operations  0.68 us (1%)
    ppermute x12, waiting for transfers between devices, swapped(): return lax.ppermute(value, ('samp', 'grid'), pairs)  18 us
    ppermute x12, starting transfers between devices, swapped(): return lax.ppermute(value, ('samp', 'grid'), pairs)  17.8 us
    pallas_call x7, Pallas kernels, call(): pl.pallas_call(kernel, out_shape=outputs, in_specs=[FAR] * far + [VMEM] *...  16.2 us
    ppermute x1, starting transfers between devices, local(): theirs = lax.ppermute(other, 'samp', [(0, 1), (1, 0)])  4.23 us
  transfers between devices with their start and end apart: 13, of which 7 were waited for; matrix products, arithmetic and copies ran while one was open for 0% of the time, Pallas kernels for 7%

profile of v6, /device:TPU:97, one launch (start us, length us, event | category | flops | bytes accessed | tf_op | source)
XLA Modules:
  0.0 58.9 jit_solution(442868705404288400)
XLA Ops:
  0.6 1.4 %shard_map.49 = (f32[16,128,128]{2,1,0:T(8,128)S(1)}, f32[16,128,128]{2,1,0:T(8,128)S(1)}, f32[32,8,128]{2,1,0:T(8,128)S(1)}, f32[32,8,128]{2,1,0:T(8,128)S(1)},...) custom-call(f32[64,2048]{1,0:T(8,128)} %bitcast.3, f32[64,2048]{1,0:T(8,128)} %bitcast.4), custom_call_target="tpu_custom_call" | custom-call | flops 100000000 | bytes 1000000 | tf_op jit(solution)/shard_map/pallas_call | solution.py:522
  2.1 0.8 %shard_map.50 = (f32[16,128,128]{2,1,0:T(8,128)S(1)}, f32[16,128,128]{2,1,0:T(8,128)S(1)}, f32[32,16,128]{2,1,0:T(8,128)S(1)}, f32[32,16,128]{2,1,0:T(8,128)S(1)}) custom-call(f32[64,2048]{1,0:T(8,128)S(1)} %get-tuple-element.45.log_ref, f32[64,2048]{1,0:T(8,128)S(1)} %get-tuple-element.46.src_ref, ...), custom_call_target="tpu_custom_call", output_to_operand_aliasing={{0}: (2, {}), {1}: (3, {})} | custom-call | flops 100000000 | bytes 1000000 | tf_op jit(solution)/shard_map/pallas_call | solution.py:522
  2.9 1.3 %collective-permute-start.6 = (f32[32,16,128]{2,1,0:T(8,128)S(1)}, f32[32,16,128]{2,1,0:T(8,128)S(1)}, u32[]{:S(2)}, u32[]{:S(2)}) collective-permute-start(f32[32,16,128]{2,1,0:T(8,128)S(1)} %get-tuple-element.69), channel_id=1, source_target_pairs={{0,1},{1,0},{2,3},{3,2},{4,5},{5,4},{6,7},{7,6},{8,9},{9,8},{10,11... | collective-permute-start | bytes 786440 | tf_op jit(solution)/shard_map/ppermute | solution.py:545
  4.2 4.1 %collective-permute-start.7 = (f32[32,16,128]{2,1,0:T(8,128)S(1)}, f32[32,16,128]{2,1,0:T(8,128)S(1)}, u32[]{:S(2)}, u32[]{:S(2)}) collective-permute-start(f32[32,16,128]{2,1,0:T(8,128)S(1)} %get-tuple-element.70), channel_id=1, source_target_pairs={{1,2},{2,1},{3,4},{4,3},{5,6},{6,5},{7,8},{8,7},{9,10},{10,9},{11,... | collective-permute-start | bytes 786440 | tf_op jit(solution)/shard_map/ppermute | solution.py:545
  8.3 0.0 collective-permute-start
  8.3 1.6 %collective-permute-start.1 = (f32[32,8,128]{2,1,0:T(8,128)S(1)}, f32[32,8,128]{2,1,0:T(8,128)S(1)}, u32[]{:S(2)}, u32[]{:S(2)}) collective-permute-start(f32[32,8,128]{2,1,0:T(8,128)S(1)} %get-tuple-element.58), channel_id=1, source_target_pairs={{1,2},{2,1},{3,4},{4,3},{5,6},{6,5},{7,8},{8,7},{9,10},{10,9},{11,... | collective-permute-start | bytes 393224 | tf_op jit(solution)/shard_map/ppermute | solution.py:545
  9.9 1.1 %shard_map.51 = (f32[16,128,128]{2,1,0:T(8,128)S(1)}, f32[16,128,128]{2,1,0:T(8,128)S(1)}, f32[6,16,112,128]{3,2,1,0:T(8,128)S(1)}, f32[16,128,128]{2,1,0:T(8,12...) custom-call(f32[64,2048]{1,0:T(8,128)S(1)} %get-tuple-element.45.log, ...), custom_call_target="tpu_custom_call", output_to_operand_aliasing={{0}: (2, {}), {1}: (3, {})} | custom-call | flops 100000000 | bytes 1000000 | tf_op jit(solution)/shard_map/pallas_call | solution.py:522
  11.0 1.7 %collective-permute-done.first_ref = f32[32,8,128]{2,1,0:T(8,128)S(1)} collective-permute-done((f32[32,8,128]{2,1,0:T(8,128)S(1)}, f32[32,8,128]{2,1,0:T(8,128)S(1)}, u32[]{:S(2)}, u32[]{:S(2)}) %collective-permute-start) | collective-permute-done | bytes 131104 | tf_op jit(solution)/shard_map/ppermute | solution.py:545
  12.7 5.4 %collective-permute-done.1.second_ref = f32[32,8,128]{2,1,0:T(8,128)S(1)} collective-permute-done((f32[32,8,128]{2,1,0:T(8,128)S(1)}, f32[32,8,128]{2,1,0:T(8,128)S(1)}, u32[]{:S(2)}, u32[]{:S(2)}) %collective-permute-start.1) | collective-permute-done | bytes 131104 | tf_op jit(solution)/shard_map/ppermute | solution.py:545
  18.1 1.6 %shard_map.52 = (f32[16,128,128]{2,1,0:T(8,128)S(1)}, f32[16,128,128]{2,1,0:T(8,128)S(1)}, f32[6,16,112,128]{3,2,1,0:T(8,128)S(1)}, f32[16,128,128]{2,1,0:T(8,12...) custom-call(f32[16,128,128]{2,1,0:T(8,128)S(1)} %get-tuple-element.5, ...), custom_call_target="tpu_custom_call", output_to_operand_aliasing={{0}: (0, {}), {1}: (1, {}), {2}: (2, {}), {3}: (3, {}), {4}... | custom-call | flops 100000000 | bytes 1000000 | tf_op jit(solution)/shard_map/pallas_call | solution.py:522
  19.7 0.6 %collective-permute-start.5 = (f32[12,16,128]{2,1,0:T(8,128)S(1)}, f32[12,16,128]{2,1,0:T(8,128)S(1)}, u32[]{:S(2)}, u32[]{:S(2)}) collective-permute-start(f32[12,16,128]{2,1,0:T(8,128)S(1)} %get-tuple-element.59.m4), channel_id=1, source_target_pairs={{2,4},{3,5},{4,2},{5,3},{6,8},{7,9},{8,6},{9,7},{10,12},{11,13},{1... | collective-permute-start | bytes 294920 | tf_op jit(solution)/shard_map/ppermute | solution.py:545
  20.3 1.4 %collective-permute-start.4 = (f32[12,16,128]{2,1,0:T(8,128)S(1)}, f32[12,16,128]{2,1,0:T(8,128)S(1)}, u32[]{:S(2)}, u32[]{:S(2)}) collective-permute-start(f32[12,16,128]{2,1,0:T(8,128)S(1)} %get-tuple-element.59.m4), channel_id=1, source_target_pairs={{0,2},{1,3},{2,0},{3,1},{4,6},{5,7},{6,4},{7,5},{8,10},{9,11},{10,... | collective-permute-start | bytes 294920 | tf_op jit(solution)/shard_map/ppermute | solution.py:545
  21.6 3.3 %collective-permute-start.3 = (f32[12,16,128]{2,1,0:T(8,128)S(1)}, f32[12,16,128]{2,1,0:T(8,128)S(1)}, u32[]{:S(2)}, u32[]{:S(2)}) collective-permute-start(f32[12,16,128]{2,1,0:T(8,128)S(1)} %get-tuple-element.59.m4), channel_id=1, source_target_pairs={{1,2},{2,1},{3,4},{4,3},{5,6},{6,5},{7,8},{8,7},{9,10},{10,9},{11,... | collective-permute-start | bytes 294920 | tf_op jit(solution)/shard_map/ppermute | solution.py:545
  24.9 0.0 collective-permute-done.6.refs_9_
  24.9 0.0 collective-permute-start.2
  24.9 0.0 collective-permute-done.7.refs_10_
  24.9 1.5 %shard_map.53 = (f32[16,128,128]{2,1,0:T(8,128)S(1)}, f32[16,128,128]{2,1,0:T(8,128)S(1)}, f32[6,16,112,128]{3,2,1,0:T(8,128)S(1)}, f32[16,128,128]{2,1,0:T(8,12...) custom-call(f32[16,128,128]{2,1,0:T(8,128)S(1)} %get-tuple-element.6, ...), custom_call_target="tpu_custom_call", output_to_operand_aliasing={{0}: (0, {}), {1}: (1, {}), {2}: (2, {}), {3}: (3, {}), {4}... | custom-call | flops 100000000 | bytes 1000000 | tf_op jit(solution)/shard_map/pallas_call | solution.py:522
  26.5 1.3 %collective-permute-done.5.m3 = f32[12,16,128]{2,1,0:T(8,128)S(1)} collective-permute-done((f32[12,16,128]{2,1,0:T(8,128)S(1)}, f32[12,16,128]{2,1,0:T(8,128)S(1)}, u32[]{:S(2)}, u32[]{:S(2)}) %collective-permute-start.5) | collective-permute-done | bytes 98336 | tf_op jit(solution)/shard_map/ppermute | solution.py:545
  27.7 0.0 collective-permute-done.4.m2
  27.7 3.9 %collective-permute-done.3.m1 = f32[12,16,128]{2,1,0:T(8,128)S(1)} collective-permute-done((f32[12,16,128]{2,1,0:T(8,128)S(1)}, f32[12,16,128]{2,1,0:T(8,128)S(1)}, u32[]{:S(2)}, u32[]{:S(2)}) %collective-permute-start.3) | collective-permute-done | bytes 98336 | tf_op jit(solution)/shard_map/ppermute | solution.py:545
  31.7 0.0 collective-permute-done.2.m0
  31.7 5.4 %shard_map.54 = (f32[8,16,128]{2,1,0:T(8,128)S(1)}, f32[6,4,80,128]{3,2,1,0:T(8,128)S(1)}, f32[6,2,40,128]{3,2,1,0:T(8,128)S(1)}, f32[6,1,24,128]{3,2,1,0:T(8,12...) custom-call(f32[12,16,128]{2,1,0:T(8,128)S(1)} %collective-permute-d, ...), custom_call_target="tpu_custom_call", output_to_operand_aliasing={{4}: (7, {}), {5}: (9, {}), {6}: (10, {})} | custom-call | flops 100000000 | bytes 1000000 | tf_op jit(solution)/shard_map/pallas_call | solution.py:522
  37.1 0.1 collective-permute-start.11
  37.2 2.5 %collective-permute-start.10 = (f32[8,16,128]{2,1,0:T(8,128)S(1)}, f32[8,16,128]{2,1,0:T(8,128)S(1)}, u32[]{:S(2)}, u32[]{:S(2)}) collective-permute-start(f32[8,16,128]{2,1,0:T(8,128)S(1)} %get-tuple-element.77.m4), channel_id=1, source_target_pairs={{0,2},{1,3},{2,0},{3,1},{4,6},{5,7},{6,4},{7,5},{8,10},{9,11},{10,... | collective-permute-start | bytes 196616 | tf_op jit(solution)/shard_map/ppermute | solution.py:545
  39.7 2.6 %collective-permute-start.9 = (f32[8,16,128]{2,1,0:T(8,128)S(1)}, f32[8,16,128]{2,1,0:T(8,128)S(1)}, u32[]{:S(2)}, u32[]{:S(2)}) collective-permute-start(f32[8,16,128]{2,1,0:T(8,128)S(1)} %get-tuple-element.77.m4), channel_id=1, source_target_pairs={{1,2},{2,1},{3,4},{4,3},{5,6},{6,5},{7,8},{8,7},{9,10},{10,9},{11,... | collective-permute-start | bytes 196616 | tf_op jit(solution)/shard_map/ppermute | solution.py:545
  42.3 0.4 collective-permute-start.8
  42.7 2.1 %collective-permute-done.11.m3 = f32[8,16,128]{2,1,0:T(8,128)S(1)} collective-permute-done((f32[8,16,128]{2,1,0:T(8,128)S(1)}, f32[8,16,128]{2,1,0:T(8,128)S(1)}, u32[]{:S(2)}, u32[]{:S(2)}) %collective-permute-start.11) | collective-permute-done | bytes 65568 | tf_op jit(solution)/shard_map/ppermute | solution.py:545
  44.8 0.0 collective-permute-done.10.m2
  44.8 3.6 %collective-permute-done.9.m1 = f32[8,16,128]{2,1,0:T(8,128)S(1)} collective-permute-done((f32[8,16,128]{2,1,0:T(8,128)S(1)}, f32[8,16,128]{2,1,0:T(8,128)S(1)}, u32[]{:S(2)}, u32[]{:S(2)}) %collective-permute-start.9) | collective-permute-done | bytes 65568 | tf_op jit(solution)/shard_map/ppermute | solution.py:545
  48.4 0.0 collective-permute-done.8.m0
  48.4 4.3 %shard_map.55 = (f32[16,128,128]{2,1,0:T(8,128)S(1)}, f32[16,72,128]{2,1,0:T(8,128)S(1)}, f32[64,2048]{1,0:T(8,128)}, f32[64,1024]{1,0:T(8,128)S(1)}, f32[64,1024]{1,0:T(8,128)S(1)}) custom-call(f32[8,16,128]{2,1,0:T(8,128)S(1)} %collective-permute-done.8.m0, ...), custom_call_target="tpu_custom_call", output_to_operand_aliasing={{0}: (7, {}), {1}: (10, {})} | custom-call | flops 100000000 | bytes 1000000 | tf_op jit(solution)/shard_map/pallas_call | solution.py:522
  52.7 4.2 %collective-permute-start.12 = (f32[64,1024]{1,0:T(8,128)S(1)}, f32[64,1024]{1,0:T(8,128)S(1)}, u32[]{:S(2)}, u32[]{:S(2)}) collective-permute-start(f32[64,1024]{1,0:T(8,128)S(1)} %get-tuple-element.86), channel_id=1, source_target_pairs={{0,64},{64,0},{1,65},{65,1},{2,66},{66,2},{3,67},{67,3},{4,68},{68... | collective-permute-start | bytes 786440 | tf_op jit(solution)/shard_map/ppermute | solution.py:600
  56.9 1.2 %collective-permute-done.12 = f32[64,1024]{1,0:T(8,128)S(1)} collective-permute-done((f32[64,1024]{1,0:T(8,128)S(1)}, f32[64,1024]{1,0:T(8,128)S(1)}, u32[]{:S(2)}, u32[]{:S(2)}) %collective-permute-start.12) | collective-permute-done | bytes 262176 | tf_op jit(solution)/shard_map/ppermute | solution.py:600
  58.1 0.9 %multiply_subtract_fusion = (f32[64,1024]{1,0:T(8,128)}, f32[64,1024]{1,0:T(8,128)}) fusion(f32[64,1024]{1,0:T(8,128)S(1)} %collective-permute-done.12, f32[64,1024]{1,0:T(8,128)S(1)} %get-tuple-element.85), kind=kLoop, calls=%fused_computation | loop fusion | flops 458752 | bytes 1048576 | tf_op jit(solution)/shard_map/sub | solution.py:604
Async XLA Ops:
  2.9 22.0 %collective-permute-start.6 = (f32[32,16,128]{2,1,0:T(8,128)S(1)}, f32[32,16,128]{2,1,0:T(8,128)S(1)}, u32[]{:S(2)}, u32[]{:S(2)}) collective-permute-start(f32[32,16,128]{2,1,0:T(8,128)S(1)} %get-tuple-element.69), channel_id=1, source_target_pairs={{0,1},{1,0},{2,3},{3,2},{4,5},{5,4},{6,7},{7,6},{8,9},{9,8},{10,11... | collective-permute-start | bytes 786440 | tf_op jit(solution)/shard_map/ppermute | solution.py:545
  4.2 20.8 %collective-permute-start.7 = (f32[32,16,128]{2,1,0:T(8,128)S(1)}, f32[32,16,128]{2,1,0:T(8,128)S(1)}, u32[]{:S(2)}, u32[]{:S(2)}) collective-permute-start(f32[32,16,128]{2,1,0:T(8,128)S(1)} %get-tuple-element.70), channel_id=1, source_target_pairs={{1,2},{2,1},{3,4},{4,3},{5,6},{6,5},{7,8},{8,7},{9,10},{10,9},{11,... | collective-permute-start | bytes 786440 | tf_op jit(solution)/shard_map/ppermute | solution.py:545
  8.3 4.4 %collective-permute-start = (f32[32,8,128]{2,1,0:T(8,128)S(1)}, f32[32,8,128]{2,1,0:T(8,128)S(1)}, u32[]{:S(2)}, u32[]{:S(2)}) collective-permute-start(f32[32,8,128]{2,1,0:T(8,128)S(1)} %get-tuple-element.57), channel_id=1, source_target_pairs={{0,1},{1,0},{2,3},{3,2},{4,5},{5,4},{6,7},{7,6},{8,9},{9,8},{10,11... | collective-permute-start | bytes 393224 | tf_op jit(solution)/shard_map/ppermute | solution.py:545
  8.3 9.8 %collective-permute-start.1 = (f32[32,8,128]{2,1,0:T(8,128)S(1)}, f32[32,8,128]{2,1,0:T(8,128)S(1)}, u32[]{:S(2)}, u32[]{:S(2)}) collective-permute-start(f32[32,8,128]{2,1,0:T(8,128)S(1)} %get-tuple-element.58), channel_id=1, source_target_pairs={{1,2},{2,1},{3,4},{4,3},{5,6},{6,5},{7,8},{8,7},{9,10},{10,9},{11,... | collective-permute-start | bytes 393224 | tf_op jit(solution)/shard_map/ppermute | solution.py:545
  19.7 8.1 %collective-permute-start.5 = (f32[12,16,128]{2,1,0:T(8,128)S(1)}, f32[12,16,128]{2,1,0:T(8,128)S(1)}, u32[]{:S(2)}, u32[]{:S(2)}) collective-permute-start(f32[12,16,128]{2,1,0:T(8,128)S(1)} %get-tuple-element.59.m4), channel_id=1, source_target_pairs={{2,4},{3,5},{4,2},{5,3},{6,8},{7,9},{8,6},{9,7},{10,12},{11,13},{1... | collective-permute-start | bytes 294920 | tf_op jit(solution)/shard_map/ppermute | solution.py:545
  20.3 7.5 %collective-permute-start.4 = (f32[12,16,128]{2,1,0:T(8,128)S(1)}, f32[12,16,128]{2,1,0:T(8,128)S(1)}, u32[]{:S(2)}, u32[]{:S(2)}) collective-permute-start(f32[12,16,128]{2,1,0:T(8,128)S(1)} %get-tuple-element.59.m4), channel_id=1, source_target_pairs={{0,2},{1,3},{2,0},{3,1},{4,6},{5,7},{6,4},{7,5},{8,10},{9,11},{10,... | collective-permute-start | bytes 294920 | tf_op jit(solution)/shard_map/ppermute | solution.py:545
  21.6 10.0 %collective-permute-start.3 = (f32[12,16,128]{2,1,0:T(8,128)S(1)}, f32[12,16,128]{2,1,0:T(8,128)S(1)}, u32[]{:S(2)}, u32[]{:S(2)}) collective-permute-start(f32[12,16,128]{2,1,0:T(8,128)S(1)} %get-tuple-element.59.m4), channel_id=1, source_target_pairs={{1,2},{2,1},{3,4},{4,3},{5,6},{6,5},{7,8},{8,7},{9,10},{10,9},{11,... | collective-permute-start | bytes 294920 | tf_op jit(solution)/shard_map/ppermute | solution.py:545
  24.9 6.7 %collective-permute-start.2 = (f32[12,16,128]{2,1,0:T(8,128)S(1)}, f32[12,16,128]{2,1,0:T(8,128)S(1)}, u32[]{:S(2)}, u32[]{:S(2)}) collective-permute-start(f32[12,16,128]{2,1,0:T(8,128)S(1)} %get-tuple-element.59.m4), channel_id=1, source_target_pairs={{0,1},{1,0},{2,3},{3,2},{4,5},{5,4},{6,7},{7,6},{8,9},{9,8},{10,11... | collective-permute-start | bytes 294920 | tf_op jit(solution)/shard_map/ppermute | solution.py:545
  37.1 7.7 %collective-permute-start.11 = (f32[8,16,128]{2,1,0:T(8,128)S(1)}, f32[8,16,128]{2,1,0:T(8,128)S(1)}, u32[]{:S(2)}, u32[]{:S(2)}) collective-permute-start(f32[8,16,128]{2,1,0:T(8,128)S(1)} %get-tuple-element.77.m4), channel_id=1, source_target_pairs={{2,4},{3,5},{4,2},{5,3},{6,8},{7,9},{8,6},{9,7},{10,12},{11,13},{1... | collective-permute-start | bytes 196616 | tf_op jit(solution)/shard_map/ppermute | solution.py:545
  37.2 7.6 %collective-permute-start.10 = (f32[8,16,128]{2,1,0:T(8,128)S(1)}, f32[8,16,128]{2,1,0:T(8,128)S(1)}, u32[]{:S(2)}, u32[]{:S(2)}) collective-permute-start(f32[8,16,128]{2,1,0:T(8,128)S(1)} %get-tuple-element.77.m4), channel_id=1, source_target_pairs={{0,2},{1,3},{2,0},{3,1},{4,6},{5,7},{6,4},{7,5},{8,10},{9,11},{10,... | collective-permute-start | bytes 196616 | tf_op jit(solution)/shard_map/ppermute | solution.py:545
  39.7 8.7 %collective-permute-start.9 = (f32[8,16,128]{2,1,0:T(8,128)S(1)}, f32[8,16,128]{2,1,0:T(8,128)S(1)}, u32[]{:S(2)}, u32[]{:S(2)}) collective-permute-start(f32[8,16,128]{2,1,0:T(8,128)S(1)} %get-tuple-element.77.m4), channel_id=1, source_target_pairs={{1,2},{2,1},{3,4},{4,3},{5,6},{6,5},{7,8},{8,7},{9,10},{10,9},{11,... | collective-permute-start | bytes 196616 | tf_op jit(solution)/shard_map/ppermute | solution.py:545
  42.3 6.1 %collective-permute-start.8 = (f32[8,16,128]{2,1,0:T(8,128)S(1)}, f32[8,16,128]{2,1,0:T(8,128)S(1)}, u32[]{:S(2)}, u32[]{:S(2)}) collective-permute-start(f32[8,16,128]{2,1,0:T(8,128)S(1)} %get-tuple-element.77.m4), channel_id=1, source_target_pairs={{0,1},{1,0},{2,3},{3,2},{4,5},{5,4},{6,7},{7,6},{8,9},{9,8},{10,11... | collective-permute-start | bytes 196616 | tf_op jit(solution)/shard_map/ppermute | solution.py:545
  52.7 5.4 %collective-permute-start.12 = (f32[64,1024]{1,0:T(8,128)S(1)}, f32[64,1024]{1,0:T(8,128)S(1)}, u32[]{:S(2)}, u32[]{:S(2)}) collective-permute-start(f32[64,1024]{1,0:T(8,128)S(1)} %get-tuple-element.86), channel_id=1, source_target_pairs={{0,64},{64,0},{1,65},{65,1},{2,66},{66,2},{3,67},{67,3},{4,68},{68... | collective-permute-start | bytes 786440 | tf_op jit(solution)/shard_map/ppermute | solution.py:600

commit v7 on v6

--- a/solution.py
+++ b/solution.py
@@ -382,8 +382,8 @@
     relax(1, vb1, va1, bp1, a1, strips)
 
 
-def up_level_0(va1, va0, vb0, bp0, a0, first, second):
-    prolong(STRIPS[1], va1, PAD, range(TILES[1]), va0)
+def up_level_0(va1, va0, vb0, bp0, a0, first, second, coarse=STRIPS[1]):
+    prolong(coarse, va1, PAD, range(TILES[1]), va0)
     relax(0, va0, vb0, bp0, a0, first)
     relax(0, vb0, va0, bp0, a0, second)
 
@@ -436,7 +436,7 @@
 
     relax(0, va0, vb0, bp0, a0, (1, 13))
     relax(0, vb0, va0, bp0, a0, (1, 13))
-    residual(0, va0, vb0, bp0, a0, (1, 13))
+    residual(0, va0, vb0, bp0, a0, (2, 12))
     restrict((1, 6), vb0, PAD, range(TILES[0]), scaled_store(bp1, a1))
 
     def clear(i):
@@ -455,8 +455,8 @@
 
 def close_kernel(
     m0, m1, m2, m3, m4, a0, bp0, va0_in, a1, bp1, va1_in, a2, a3, a4,
-    va0, va1, out_hbm, mine_ref, other_ref,
-    vb0, vb1, bp2, va2, vb2, bp3, va3, vb3, bp4, va4, vb4, out_ref, sems,
+    va0, va1, out_ref, mine_ref, other_ref,
+    vb0, vb1, bp2, va2, vb2, bp3, va3, vb3, bp4, va4, vb4,
 ):
     for ref in (bp4, va4, vb4):
         fill(ref, 0.0)
@@ -469,14 +469,13 @@
     vb = {2: vb2, 3: vb3, 4: vb4}
     deep_solve(a, bp, va, vb)
     up_level_1(va2, va1, vb1, bp1, a1, (1, 6))
-    up_level_0(va1, va0, vb0, bp0, a0, (2, 12), (3, 11))
+    up_level_0(va1, va0, vb0, bp0, a0, (2, 12), (3, 11), (1, 6))
     prolong(OWN[1] // 8, va1, PAD + HALO[1], range(TILES[1], 2 * TILES[1]), va0, -1.0, PAD + HALO[0])
     tiles = TILES[0]
     left = lax.axis_index("samp") == 0
 
-    copies = []
-    for piece in range(OWN[0] // 16):
-        strips = (2 * piece, 2 * piece + 1)
+    for piece in range(0, OWN[0] // 8, 4):
+        strips = range(piece, piece + 4)
         turned = turn([[va0[t, at(j, PAD + HALO[0]), :] for t in range(tiles)] for j in strips])
         for j, x in zip(strips, turned):
             for t in range(tiles):
@@ -485,11 +484,6 @@
                 low, high = x[t], x[tiles // 2 + t]
                 mine_ref[at(j, 0), t * LANES : (t + 1) * LANES] = jnp.where(left, low, high)
                 other_ref[at(j, 0), t * LANES : (t + 1) * LANES] = jnp.where(left, high, low)
-        rows = pl.ds(16 * piece, 16)
-        copies.append(pltpu.make_async_copy(out_ref.at[rows, :], out_hbm.at[rows, :], sems.at[piece]))
-        copies[-1].start()
-    for copy in copies:
-        copy.wait()
 
 
 VMEM = pl.BlockSpec(memory_space=pltpu.VMEM)
@@ -591,10 +585,9 @@
     v0, v1, correction, mine, other = call(
         close_kernel,
         held(*gathered(message), a0, b0, v0, a1, b1, v1, a2, a3, a4),
-        (state[2], state[5], jax.ShapeDtypeStruct((rows, columns), F32), half, half),
-        [v_shape(0), v_shape(1)] + deep + [(rows, columns)],
+        (state[2], state[5], near(rows, columns), half, half),
+        [v_shape(0), v_shape(1)] + deep,
         {7: 0, 10: 1},
-        sems=rows // 16,
     )
 
     theirs = lax.ppermute(other, "samp", [(0, 1), (1, 0)])

time: 59.1 us -> 58 us (0.981)
  Pallas kernels: 16.2 us -> 15.1 us
  local copies, waits for them, and re-layouts: 0 us -> 0.79 us
  waiting for transfers between devices: 19.1 us -> 18.4 us
    pallas_call x7, Pallas kernels: 16.2 us -> 15.1 us  [call(): pl.pallas_call(kernel, out_shape=outputs, in_specs=[FAR] * far + [VMEM] *...]
    ppermute x1, waiting for transfers between devices: 1.16 us -> 0.37 us  [local(): theirs = lax.ppermute(other, 'samp', [(0, 1), (1, 0)])]
    unnamed x0 -> x1, local copies, waits for them, and re-layouts: none -> 0.79 us
  transfers between devices with their start and end apart: 13 -> 13, of which waited for: 7 -> 7; matrix products, arithmetic and copies ran while one was open for 0% -> 1% of each run, Pallas kernels for 7% -> 7%
where the time goes in v7:
time: 58 us; the launch traced here: 57.8 us
  starting transfers between devices  22 us (38%)
  waiting for transfers between devices  18.4 us (32%)
  Pallas kernels  15.1 us (26%)
  other arithmetic  0.86 us (1%)
  local copies, waits for them, and re-layouts  0.79 us (1%)
  between operations  0.69 us (1%)
    ppermute x12, waiting for transfers between devices, swapped(): return lax.ppermute(value, ('samp', 'grid'), pairs)  18 us
    ppermute x12, starting transfers between devices, swapped(): return lax.ppermute(value, ('samp', 'grid'), pairs)  17.8 us
    pallas_call x7, Pallas kernels, call(): pl.pallas_call(kernel, out_shape=outputs, in_specs=[FAR] * far + [VMEM] *...  15.1 us
    ppermute x1, starting transfers between devices, local(): theirs = lax.ppermute(other, 'samp', [(0, 1), (1, 0)])  4.23 us
  transfers between devices with their start and end apart: 13, of which 7 were waited for; matrix products, arithmetic and copies ran while one was open for 1% of the time, Pallas kernels for 7%

profile of v7, /device:TPU:97, one launch (start us, length us, event | category | flops | bytes accessed | tf_op | source)
XLA Modules:
  0.0 57.8 jit_solution(3121907350466014152)
XLA Ops:
  0.6 1.4 %shard_map.49 = (f32[16,128,128]{2,1,0:T(8,128)S(1)}, f32[16,128,128]{2,1,0:T(8,128)S(1)}, f32[32,8,128]{2,1,0:T(8,128)S(1)}, f32[32,8,128]{2,1,0:T(8,128)S(1)},...) custom-call(f32[64,2048]{1,0:T(8,128)} %bitcast.4, f32[64,2048]{1,0:T(8,128)} %bitcast.5), custom_call_target="tpu_custom_call" | custom-call | flops 100000000 | bytes 1000000 | tf_op jit(solution)/shard_map/pallas_call | solution.py:516
  2.1 0.8 %shard_map.50 = (f32[16,128,128]{2,1,0:T(8,128)S(1)}, f32[16,128,128]{2,1,0:T(8,128)S(1)}, f32[32,16,128]{2,1,0:T(8,128)S(1)}, f32[32,16,128]{2,1,0:T(8,128)S(1)}) custom-call(f32[64,2048]{1,0:T(8,128)S(1)} %get-tuple-element.45.log_ref, f32[64,2048]{1,0:T(8,128)S(1)} %get-tuple-element.46.src_ref, ...), custom_call_target="tpu_custom_call", output_to_operand_aliasing={{0}: (2, {}), {1}: (3, {})} | custom-call | flops 100000000 | bytes 1000000 | tf_op jit(solution)/shard_map/pallas_call | solution.py:516
  2.9 1.3 %collective-permute-start.6 = (f32[32,16,128]{2,1,0:T(8,128)S(1)}, f32[32,16,128]{2,1,0:T(8,128)S(1)}, u32[]{:S(2)}, u32[]{:S(2)}) collective-permute-start(f32[32,16,128]{2,1,0:T(8,128)S(1)} %get-tuple-element.69), channel_id=1, source_target_pairs={{0,1},{1,0},{2,3},{3,2},{4,5},{5,4},{6,7},{7,6},{8,9},{9,8},{10,11... | collective-permute-start | bytes 786440 | tf_op jit(solution)/shard_map/ppermute | solution.py:539
  4.2 4.1 %collective-permute-start.7 = (f32[32,16,128]{2,1,0:T(8,128)S(1)}, f32[32,16,128]{2,1,0:T(8,128)S(1)}, u32[]{:S(2)}, u32[]{:S(2)}) collective-permute-start(f32[32,16,128]{2,1,0:T(8,128)S(1)} %get-tuple-element.70), channel_id=1, source_target_pairs={{1,2},{2,1},{3,4},{4,3},{5,6},{6,5},{7,8},{8,7},{9,10},{10,9},{11,... | collective-permute-start | bytes 786440 | tf_op jit(solution)/shard_map/ppermute | solution.py:539
  8.3 0.0 collective-permute-start
  8.3 1.6 %collective-permute-start.1 = (f32[32,8,128]{2,1,0:T(8,128)S(1)}, f32[32,8,128]{2,1,0:T(8,128)S(1)}, u32[]{:S(2)}, u32[]{:S(2)}) collective-permute-start(f32[32,8,128]{2,1,0:T(8,128)S(1)} %get-tuple-element.58), channel_id=1, source_target_pairs={{1,2},{2,1},{3,4},{4,3},{5,6},{6,5},{7,8},{8,7},{9,10},{10,9},{11,... | collective-permute-start | bytes 393224 | tf_op jit(solution)/shard_map/ppermute | solution.py:539
  9.9 1.1 %shard_map.51 = (f32[16,128,128]{2,1,0:T(8,128)S(1)}, f32[16,128,128]{2,1,0:T(8,128)S(1)}, f32[6,16,112,128]{3,2,1,0:T(8,128)S(1)}, f32[16,128,128]{2,1,0:T(8,12...) custom-call(f32[64,2048]{1,0:T(8,128)S(1)} %get-tuple-element.45.log, ...), custom_call_target="tpu_custom_call", output_to_operand_aliasing={{0}: (2, {}), {1}: (3, {})} | custom-call | flops 100000000 | bytes 1000000 | tf_op jit(solution)/shard_map/pallas_call | solution.py:516
  11.0 1.7 %collective-permute-done.first_ref = f32[32,8,128]{2,1,0:T(8,128)S(1)} collective-permute-done((f32[32,8,128]{2,1,0:T(8,128)S(1)}, f32[32,8,128]{2,1,0:T(8,128)S(1)}, u32[]{:S(2)}, u32[]{:S(2)}) %collective-permute-start) | collective-permute-done | bytes 131104 | tf_op jit(solution)/shard_map/ppermute | solution.py:539
  12.7 5.4 %collective-permute-done.1.second_ref = f32[32,8,128]{2,1,0:T(8,128)S(1)} collective-permute-done((f32[32,8,128]{2,1,0:T(8,128)S(1)}, f32[32,8,128]{2,1,0:T(8,128)S(1)}, u32[]{:S(2)}, u32[]{:S(2)}) %collective-permute-start.1) | collective-permute-done | bytes 131104 | tf_op jit(solution)/shard_map/ppermute | solution.py:539
  18.1 1.6 %shard_map.52 = (f32[16,128,128]{2,1,0:T(8,128)S(1)}, f32[16,128,128]{2,1,0:T(8,128)S(1)}, f32[6,16,112,128]{3,2,1,0:T(8,128)S(1)}, f32[16,128,128]{2,1,0:T(8,12...) custom-call(f32[16,128,128]{2,1,0:T(8,128)S(1)} %get-tuple-element.5, ...), custom_call_target="tpu_custom_call", output_to_operand_aliasing={{0}: (0, {}), {1}: (1, {}), {2}: (2, {}), {3}: (3, {}), {4}... | custom-call | flops 100000000 | bytes 1000000 | tf_op jit(solution)/shard_map/pallas_call | solution.py:516
  19.7 0.6 %collective-permute-start.5 = (f32[12,16,128]{2,1,0:T(8,128)S(1)}, f32[12,16,128]{2,1,0:T(8,128)S(1)}, u32[]{:S(2)}, u32[]{:S(2)}) collective-permute-start(f32[12,16,128]{2,1,0:T(8,128)S(1)} %get-tuple-element.59.m4), channel_id=1, source_target_pairs={{2,4},{3,5},{4,2},{5,3},{6,8},{7,9},{8,6},{9,7},{10,12},{11,13},{1... | collective-permute-start | bytes 294920 | tf_op jit(solution)/shard_map/ppermute | solution.py:539
  20.3 1.4 %collective-permute-start.4 = (f32[12,16,128]{2,1,0:T(8,128)S(1)}, f32[12,16,128]{2,1,0:T(8,128)S(1)}, u32[]{:S(2)}, u32[]{:S(2)}) collective-permute-start(f32[12,16,128]{2,1,0:T(8,128)S(1)} %get-tuple-element.59.m4), channel_id=1, source_target_pairs={{0,2},{1,3},{2,0},{3,1},{4,6},{5,7},{6,4},{7,5},{8,10},{9,11},{10,... | collective-permute-start | bytes 294920 | tf_op jit(solution)/shard_map/ppermute | solution.py:539
  21.6 3.3 %collective-permute-start.3 = (f32[12,16,128]{2,1,0:T(8,128)S(1)}, f32[12,16,128]{2,1,0:T(8,128)S(1)}, u32[]{:S(2)}, u32[]{:S(2)}) collective-permute-start(f32[12,16,128]{2,1,0:T(8,128)S(1)} %get-tuple-element.59.m4), channel_id=1, source_target_pairs={{1,2},{2,1},{3,4},{4,3},{5,6},{6,5},{7,8},{8,7},{9,10},{10,9},{11,... | collective-permute-start | bytes 294920 | tf_op jit(solution)/shard_map/ppermute | solution.py:539
  24.9 0.0 collective-permute-done.6.refs_9_
  24.9 0.0 collective-permute-start.2
  24.9 0.0 collective-permute-done.7.refs_10_
  24.9 1.5 %shard_map.53 = (f32[16,128,128]{2,1,0:T(8,128)S(1)}, f32[16,128,128]{2,1,0:T(8,128)S(1)}, f32[6,16,112,128]{3,2,1,0:T(8,128)S(1)}, f32[16,128,128]{2,1,0:T(8,12...) custom-call(f32[16,128,128]{2,1,0:T(8,128)S(1)} %get-tuple-element.6, ...), custom_call_target="tpu_custom_call", output_to_operand_aliasing={{0}: (0, {}), {1}: (1, {}), {2}: (2, {}), {3}: (3, {}), {4}... | custom-call | flops 100000000 | bytes 1000000 | tf_op jit(solution)/shard_map/pallas_call | solution.py:516
  26.5 1.3 %collective-permute-done.5.m3 = f32[12,16,128]{2,1,0:T(8,128)S(1)} collective-permute-done((f32[12,16,128]{2,1,0:T(8,128)S(1)}, f32[12,16,128]{2,1,0:T(8,128)S(1)}, u32[]{:S(2)}, u32[]{:S(2)}) %collective-permute-start.5) | collective-permute-done | bytes 98336 | tf_op jit(solution)/shard_map/ppermute | solution.py:539
  27.7 0.0 collective-permute-done.4.m2
  27.7 3.9 %collective-permute-done.3.m1 = f32[12,16,128]{2,1,0:T(8,128)S(1)} collective-permute-done((f32[12,16,128]{2,1,0:T(8,128)S(1)}, f32[12,16,128]{2,1,0:T(8,128)S(1)}, u32[]{:S(2)}, u32[]{:S(2)}) %collective-permute-start.3) | collective-permute-done | bytes 98336 | tf_op jit(solution)/shard_map/ppermute | solution.py:539
  31.7 0.0 collective-permute-done.2.m0
  31.7 5.3 %shard_map.54 = (f32[8,16,128]{2,1,0:T(8,128)S(1)}, f32[6,4,80,128]{3,2,1,0:T(8,128)S(1)}, f32[6,2,40,128]{3,2,1,0:T(8,128)S(1)}, f32[6,1,24,128]{3,2,1,0:T(8,12...) custom-call(f32[12,16,128]{2,1,0:T(8,128)S(1)} %collective-permute-d, ...), custom_call_target="tpu_custom_call", output_to_operand_aliasing={{4}: (7, {}), {5}: (9, {}), {6}: (10, {})} | custom-call | flops 100000000 | bytes 1000000 | tf_op jit(solution)/shard_map/pallas_call | solution.py:516
  37.0 0.1 collective-permute-start.11
  37.1 2.5 %collective-permute-start.10 = (f32[8,16,128]{2,1,0:T(8,128)S(1)}, f32[8,16,128]{2,1,0:T(8,128)S(1)}, u32[]{:S(2)}, u32[]{:S(2)}) collective-permute-start(f32[8,16,128]{2,1,0:T(8,128)S(1)} %get-tuple-element.77.m4), channel_id=1, source_target_pairs={{0,2},{1,3},{2,0},{3,1},{4,6},{5,7},{6,4},{7,5},{8,10},{9,11},{10,... | collective-permute-start | bytes 196616 | tf_op jit(solution)/shard_map/ppermute | solution.py:539
  39.6 2.6 %collective-permute-start.9 = (f32[8,16,128]{2,1,0:T(8,128)S(1)}, f32[8,16,128]{2,1,0:T(8,128)S(1)}, u32[]{:S(2)}, u32[]{:S(2)}) collective-permute-start(f32[8,16,128]{2,1,0:T(8,128)S(1)} %get-tuple-element.77.m4), channel_id=1, source_target_pairs={{1,2},{2,1},{3,4},{4,3},{5,6},{6,5},{7,8},{8,7},{9,10},{10,9},{11,... | collective-permute-start | bytes 196616 | tf_op jit(solution)/shard_map/ppermute | solution.py:539
  42.2 0.4 collective-permute-start.8
  42.6 2.1 %collective-permute-done.11.m3 = f32[8,16,128]{2,1,0:T(8,128)S(1)} collective-permute-done((f32[8,16,128]{2,1,0:T(8,128)S(1)}, f32[8,16,128]{2,1,0:T(8,128)S(1)}, u32[]{:S(2)}, u32[]{:S(2)}) %collective-permute-start.11) | collective-permute-done | bytes 65568 | tf_op jit(solution)/shard_map/ppermute | solution.py:539
  44.7 0.0 collective-permute-done.10.m2
  44.7 3.6 %collective-permute-done.9.m1 = f32[8,16,128]{2,1,0:T(8,128)S(1)} collective-permute-done((f32[8,16,128]{2,1,0:T(8,128)S(1)}, f32[8,16,128]{2,1,0:T(8,128)S(1)}, u32[]{:S(2)}, u32[]{:S(2)}) %collective-permute-start.9) | collective-permute-done | bytes 65568 | tf_op jit(solution)/shard_map/ppermute | solution.py:539
  48.3 0.0 collective-permute-done.8.m0
  48.3 3.3 %shard_map.55 = (f32[16,128,128]{2,1,0:T(8,128)S(1)}, f32[16,72,128]{2,1,0:T(8,128)S(1)}, f32[64,2048]{1,0:T(8,128)S(1)}, f32[64,1024]{1,0:T(8,128)S(1)}, f32[64,1024]{1,0:T(8,128)S(1)}) custom-call(f32[8,16,128]{2,1,0:T(8,128)S(1)} %collective-permute-done.8.m0, ...), custom_call_target="tpu_custom_call", output_to_operand_aliasing={{0}: (7, {}), {1}: (10, {})} | custom-call | flops 100000000 | bytes 1000000 | tf_op jit(solution)/shard_map/pallas_call | solution.py:516
  51.6 4.2 %collective-permute-start.12 = (f32[64,1024]{1,0:T(8,128)S(1)}, f32[64,1024]{1,0:T(8,128)S(1)}, u32[]{:S(2)}, u32[]{:S(2)}) collective-permute-start(f32[64,1024]{1,0:T(8,128)S(1)} %get-tuple-element.86), channel_id=1, source_target_pairs={{0,64},{64,0},{1,65},{65,1},{2,66},{66,2},{3,67},{67,3},{4,68},{68... | collective-permute-start | bytes 786440 | tf_op jit(solution)/shard_map/ppermute | solution.py:593
  55.8 0.8 %copy.53 = f32[1,64,2048]{2,1,0:T(8,128)} copy(f32[1,64,2048]{2,1,0:T(8,128)S(1)} %bitcast.3) | data formatting | bytes 1048576
  56.6 0.4 collective-permute-done.12
  57.0 0.9 %multiply_subtract_fusion = (f32[64,1024]{1,0:T(8,128)}, f32[64,1024]{1,0:T(8,128)}) fusion(f32[64,1024]{1,0:T(8,128)S(1)} %collective-permute-done.12, f32[64,1024]{1,0:T(8,128)S(1)} %get-tuple-element.85), kind=kLoop, calls=%fused_computation | loop fusion | flops 458752 | bytes 1048576 | tf_op jit(solution)/shard_map/sub | solution.py:597
Async XLA Ops:
  2.9 22.0 %collective-permute-start.6 = (f32[32,16,128]{2,1,0:T(8,128)S(1)}, f32[32,16,128]{2,1,0:T(8,128)S(1)}, u32[]{:S(2)}, u32[]{:S(2)}) collective-permute-start(f32[32,16,128]{2,1,0:T(8,128)S(1)} %get-tuple-element.69), channel_id=1, source_target_pairs={{0,1},{1,0},{2,3},{3,2},{4,5},{5,4},{6,7},{7,6},{8,9},{9,8},{10,11... | collective-permute-start | bytes 786440 | tf_op jit(solution)/shard_map/ppermute | solution.py:539
  4.2 20.8 %collective-permute-start.7 = (f32[32,16,128]{2,1,0:T(8,128)S(1)}, f32[32,16,128]{2,1,0:T(8,128)S(1)}, u32[]{:S(2)}, u32[]{:S(2)}) collective-permute-start(f32[32,16,128]{2,1,0:T(8,128)S(1)} %get-tuple-element.70), channel_id=1, source_target_pairs={{1,2},{2,1},{3,4},{4,3},{5,6},{6,5},{7,8},{8,7},{9,10},{10,9},{11,... | collective-permute-start | bytes 786440 | tf_op jit(solution)/shard_map/ppermute | solution.py:539
  8.3 4.4 %collective-permute-start = (f32[32,8,128]{2,1,0:T(8,128)S(1)}, f32[32,8,128]{2,1,0:T(8,128)S(1)}, u32[]{:S(2)}, u32[]{:S(2)}) collective-permute-start(f32[32,8,128]{2,1,0:T(8,128)S(1)} %get-tuple-element.57), channel_id=1, source_target_pairs={{0,1},{1,0},{2,3},{3,2},{4,5},{5,4},{6,7},{7,6},{8,9},{9,8},{10,11... | collective-permute-start | bytes 393224 | tf_op jit(solution)/shard_map/ppermute | solution.py:539
  8.3 9.8 %collective-permute-start.1 = (f32[32,8,128]{2,1,0:T(8,128)S(1)}, f32[32,8,128]{2,1,0:T(8,128)S(1)}, u32[]{:S(2)}, u32[]{:S(2)}) collective-permute-start(f32[32,8,128]{2,1,0:T(8,128)S(1)} %get-tuple-element.58), channel_id=1, source_target_pairs={{1,2},{2,1},{3,4},{4,3},{5,6},{6,5},{7,8},{8,7},{9,10},{10,9},{11,... | collective-permute-start | bytes 393224 | tf_op jit(solution)/shard_map/ppermute | solution.py:539
  19.7 8.1 %collective-permute-start.5 = (f32[12,16,128]{2,1,0:T(8,128)S(1)}, f32[12,16,128]{2,1,0:T(8,128)S(1)}, u32[]{:S(2)}, u32[]{:S(2)}) collective-permute-start(f32[12,16,128]{2,1,0:T(8,128)S(1)} %get-tuple-element.59.m4), channel_id=1, source_target_pairs={{2,4},{3,5},{4,2},{5,3},{6,8},{7,9},{8,6},{9,7},{10,12},{11,13},{1... | collective-permute-start | bytes 294920 | tf_op jit(solution)/shard_map/ppermute | solution.py:539
  20.3 7.5 %collective-permute-start.4 = (f32[12,16,128]{2,1,0:T(8,128)S(1)}, f32[12,16,128]{2,1,0:T(8,128)S(1)}, u32[]{:S(2)}, u32[]{:S(2)}) collective-permute-start(f32[12,16,128]{2,1,0:T(8,128)S(1)} %get-tuple-element.59.m4), channel_id=1, source_target_pairs={{0,2},{1,3},{2,0},{3,1},{4,6},{5,7},{6,4},{7,5},{8,10},{9,11},{10,... | collective-permute-start | bytes 294920 | tf_op jit(solution)/shard_map/ppermute | solution.py:539
  21.6 10.0 %collective-permute-start.3 = (f32[12,16,128]{2,1,0:T(8,128)S(1)}, f32[12,16,128]{2,1,0:T(8,128)S(1)}, u32[]{:S(2)}, u32[]{:S(2)}) collective-permute-start(f32[12,16,128]{2,1,0:T(8,128)S(1)} %get-tuple-element.59.m4), channel_id=1, source_target_pairs={{1,2},{2,1},{3,4},{4,3},{5,6},{6,5},{7,8},{8,7},{9,10},{10,9},{11,... | collective-permute-start | bytes 294920 | tf_op jit(solution)/shard_map/ppermute | solution.py:539
  24.9 6.7 %collective-permute-start.2 = (f32[12,16,128]{2,1,0:T(8,128)S(1)}, f32[12,16,128]{2,1,0:T(8,128)S(1)}, u32[]{:S(2)}, u32[]{:S(2)}) collective-permute-start(f32[12,16,128]{2,1,0:T(8,128)S(1)} %get-tuple-element.59.m4), channel_id=1, source_target_pairs={{0,1},{1,0},{2,3},{3,2},{4,5},{5,4},{6,7},{7,6},{8,9},{9,8},{10,11... | collective-permute-start | bytes 294920 | tf_op jit(solution)/shard_map/ppermute | solution.py:539
  37.0 7.7 %collective-permute-start.11 = (f32[8,16,128]{2,1,0:T(8,128)S(1)}, f32[8,16,128]{2,1,0:T(8,128)S(1)}, u32[]{:S(2)}, u32[]{:S(2)}) collective-permute-start(f32[8,16,128]{2,1,0:T(8,128)S(1)} %get-tuple-element.77.m4), channel_id=1, source_target_pairs={{2,4},{3,5},{4,2},{5,3},{6,8},{7,9},{8,6},{9,7},{10,12},{11,13},{1... | collective-permute-start | bytes 196616 | tf_op jit(solution)/shard_map/ppermute | solution.py:539
  37.1 7.6 %collective-permute-start.10 = (f32[8,16,128]{2,1,0:T(8,128)S(1)}, f32[8,16,128]{2,1,0:T(8,128)S(1)}, u32[]{:S(2)}, u32[]{:S(2)}) collective-permute-start(f32[8,16,128]{2,1,0:T(8,128)S(1)} %get-tuple-element.77.m4), channel_id=1, source_target_pairs={{0,2},{1,3},{2,0},{3,1},{4,6},{5,7},{6,4},{7,5},{8,10},{9,11},{10,... | collective-permute-start | bytes 196616 | tf_op jit(solution)/shard_map/ppermute | solution.py:539
  39.6 8.7 %collective-permute-start.9 = (f32[8,16,128]{2,1,0:T(8,128)S(1)}, f32[8,16,128]{2,1,0:T(8,128)S(1)}, u32[]{:S(2)}, u32[]{:S(2)}) collective-permute-start(f32[8,16,128]{2,1,0:T(8,128)S(1)} %get-tuple-element.77.m4), channel_id=1, source_target_pairs={{1,2},{2,1},{3,4},{4,3},{5,6},{6,5},{7,8},{8,7},{9,10},{10,9},{11,... | collective-permute-start | bytes 196616 | tf_op jit(solution)/shard_map/ppermute | solution.py:539
  42.2 6.1 %collective-permute-start.8 = (f32[8,16,128]{2,1,0:T(8,128)S(1)}, f32[8,16,128]{2,1,0:T(8,128)S(1)}, u32[]{:S(2)}, u32[]{:S(2)}) collective-permute-start(f32[8,16,128]{2,1,0:T(8,128)S(1)} %get-tuple-element.77.m4), channel_id=1, source_target_pairs={{0,1},{1,0},{2,3},{3,2},{4,5},{5,4},{6,7},{7,6},{8,9},{9,8},{10,11... | collective-permute-start | bytes 196616 | tf_op jit(solution)/shard_map/ppermute | solution.py:539
  51.6 5.4 %collective-permute-start.12 = (f32[64,1024]{1,0:T(8,128)S(1)}, f32[64,1024]{1,0:T(8,128)S(1)}, u32[]{:S(2)}, u32[]{:S(2)}) collective-permute-start(f32[64,1024]{1,0:T(8,128)S(1)} %get-tuple-element.86), channel_id=1, source_target_pairs={{0,64},{64,0},{1,65},{65,1},{2,66},{66,2},{3,67},{67,3},{4,68},{68... | collective-permute-start | bytes 786440 | tf_op jit(solution)/shard_map/ppermute | solution.py:593
